TPU v7x, 256 devices: a whole 4x4x8 slice. The times are simulated.
256 devices in a mesh: dp: 32 (over x, y, core), mp: 8 (over z).
Axes of the slice: x: 4, y: 4, z: 8, core: 2. Of those that a mesh axis runs over, the one named last changes fastest.
Arguments:
- vit_features: bfloat16 [128, 256, 1024], P('dp', 'mp'), may hold values from -6 to 6
- patch_counts: int32 [128], P('dp'), may hold values from 64 to 192
- text_counts: int32 [128], P('dp'), may hold values from 1 to 63
- tile_dest: int32 [128], P('dp'), may hold values from 0 to 31, as said below
- text_embeds: bfloat16 [128, 256, 4096], P('dp', 'mp'), may hold values from -6 to 6
- w_proj: bfloat16 [1024, 4096], replicated, may hold values from -0.1875 to 0.1875
- b_proj: float32 [4096], replicated, may hold values from -3 to 3
- norm_gain: float32 [1, 4096], replicated, may hold values from 0.1 to 1.9
- w_qkv: bfloat16 [1, 4096, 8, 512], P(None, 'dp', 'mp'), may hold values from -0.375 to 0.375
- w_out: bfloat16 [1, 8, 256, 4096], P(None, 'mp', None, 'dp'), may hold values from -0.125 to 0.125
Outputs:
- hidden_out: bfloat16 [128, 256, 4096], P('dp', 'mp')
Inputs may be any that keep to these rules, and one draw needn't show every extreme that they name: `tile_dest`: each language-model rank receives exactly 4 tiles; one source rank sends at most 2 tiles to one language-model rank, and every source rank sends 2 to some rank.
All inputs are finite; a program needn't handle non-finite values.
Results may differ from a plain program's by a relative error of at most 0.01.
Values may be sent and summed in bfloat16 or wider, within the bound.
No kernel may reach another device: no remote copies, remote signals or barrier semaphores. Data moves between devices by JAX's collectives and lax.ppermute only.
A program may use at most 128 MiB of HBM per device.

v0:
```python
import functools
import math

import jax
import jax.numpy as jnp
from jax import lax
from jax.experimental import pallas as pl
from jax.experimental.pallas import tpu as pltpu
from jax.sharding import PartitionSpec as P


HS = 128
GROUP = 2
WINDOW = 64
EXTRA = 128

rope_base = 500000.0
epsilon = 1e-05


def shifted(value, axis, step):
    size = lax.axis_size(axis)
    return lax.ppermute(value, axis, [(i, (i + step) % size) for i in range(size)])


def ring_chunks(own, axis):
    size = lax.axis_size(axis)
    chunks = [own] + [None] * (size - 1)
    for s in range(1, size // 2 + 1):
        chunks[s] = shifted(chunks[s - 1], axis, 1)
        if s < size - s:
            chunks[size - s] = shifted(chunks[(size - s + 1) % size], axis, -1)
    return chunks


def rotation_tables(rows):
    half_size = HS // 2
    inverse = jnp.exp(
        -(2.0 * jnp.arange(half_size, dtype=jnp.float32) / HS) * math.log(rope_base)
    )
    angles = rows.astype(jnp.float32)[..., None] * inverse
    cosine, sine = jnp.cos(angles), jnp.sin(angles)
    return (
        jnp.concatenate([cosine, cosine], axis=-1),
        jnp.concatenate([-sine, sine], axis=-1),
    )


def rotate_store(joined, cosine, sine, store):
    heads = joined.shape[1] // HS
    for p in range(heads):
        part = joined[:, p * HS : (p + 1) * HS]
        if p < heads - 1:
            part = part * cosine + pltpu.roll(part, HS // 2, 1) * sine
        store(p, part.astype(jnp.bfloat16))


def order_kernel(got_ref, out_ref, *, image_count):
    total, wide = got_ref.shape
    width = wide - EXTRA
    dest = got_ref[:, width:].astype(jnp.float32)
    row = lax.broadcasted_iota(jnp.int32, (total, total), 0)
    col = lax.broadcasted_iota(jnp.int32, (total, total), 1)
    earlier = (dest == dest.T) & (col < row)
    slots = jnp.sum(jnp.where(earlier, 1.0, 0.0), axis=1, keepdims=True)
    targets = (dest * image_count + slots).T
    placing = jnp.where(targets == row.astype(jnp.float32), 1.0, 0.0).astype(jnp.bfloat16)
    out_ref[...] = jnp.dot(
        placing, got_ref[:, :width], preferred_element_type=jnp.float32
    ).astype(jnp.bfloat16)


def exchange_tiles(vit_features, tile_dest):
    image_count, _, width = vit_features.shape
    ranks = lax.axis_size("dp")
    by_row = jnp.moveaxis(vit_features, 1, 0)
    tags = jnp.broadcast_to(
        tile_dest.astype(jnp.bfloat16)[None, :, None], (ranks, image_count, EXTRA)
    )
    sent = jnp.concatenate([by_row, tags], axis=2)
    got = lax.all_to_all(sent, "dp", split_axis=0, concat_axis=0, tiled=True)
    total = ranks * image_count
    ordered = pl.pallas_call(
        functools.partial(order_kernel, image_count=image_count),
        out_shape=jax.ShapeDtypeStruct((total, width), jnp.bfloat16),
        cost_estimate=pl.CostEstimate(
            flops=2 * total * total * width, bytes_accessed=4 * total * width, transcendentals=0
        ),
    )(got.reshape(total, width + EXTRA))
    arrived = lax.all_to_all(
        ordered.reshape(ranks, image_count, width),
        "dp",
        split_axis=0,
        concat_axis=0,
        tiled=True,
    )
    return jnp.moveaxis(arrived, 0, 1)


def pack_kernel(place_ref, text_ref, heads_ref, *out_refs):
    parts = len(out_refs)
    rows, wide = out_refs[0].shape
    folds = heads_ref.shape[0] // rows
    cols = heads_ref.shape[1]
    width = wide - folds * cols
    mine = place_ref[0]
    for s, out_ref in enumerate(out_refs):
        at = pl.multiple_of(lax.rem(mine + s, parts) * width, width)
        out_ref[:, :width] = text_ref[:, :, pl.ds(at, width)].reshape(rows, width)
        for f in range(folds):
            out_ref[:, width + f * cols : width + (f + 1) * cols] = heads_ref[
                f * rows : (f + 1) * rows, :
            ]


def pack(text_embeds, head_rows, mine, parts):
    tiles, local_rows, model_width = text_embeds.shape
    rows = tiles * local_rows
    width = model_width // parts
    wide = width + head_rows.shape[0] * head_rows.shape[1] // rows
    whole = pl.BlockSpec(memory_space=pltpu.VMEM)
    return pl.pallas_call(
        pack_kernel,
        in_specs=[pl.BlockSpec(memory_space=pltpu.SMEM), whole, whole],
        out_specs=[whole] * parts,
        out_shape=[jax.ShapeDtypeStruct((rows, wide), jnp.bfloat16)] * parts,
        cost_estimate=pl.CostEstimate(
            flops=1 << 20, bytes_accessed=4 * parts * rows * wide, transcendentals=0
        ),
    )(mine.reshape(1), text_embeds, head_rows)


def unpack_kernel(counts_ref, *refs, tiles, width):
    parts = len(refs) - 3
    got_refs = refs[:parts]
    window_ref, heads_ref, rows_ref = refs[parts:]
    mine = counts_ref[2, 0]
    each, wide = got_refs[0].shape
    local_rows = each // tiles
    cols = heads_ref.shape[1]
    folds = (wide - width) // cols
    for s, got_ref in enumerate(got_refs):
        at = lax.rem(mine + (parts - s), parts)
        for f in range(folds):
            begin = pl.multiple_of((at * folds + f) * each, each)
            heads_ref[pl.ds(begin, each), :] = got_ref[:, width + f * cols : width + (f + 1) * cols]
        for t in range(tiles):
            rows_ref[t, at] = got_ref[t * local_rows : (t + 1) * local_rows, :width]
    rows = parts * local_rows
    place = lax.broadcasted_iota(jnp.int32, (WINDOW, rows), 0)
    row = lax.broadcasted_iota(jnp.int32, (WINDOW, rows), 1)
    for t in range(tiles):
        picks = (row == counts_ref[0, t] + place) & (place < counts_ref[1, t])
        window_ref[t * WINDOW : (t + 1) * WINDOW, :] = jnp.dot(
            jnp.where(picks, 1.0, 0.0).astype(jnp.bfloat16),
            rows_ref[t].reshape(rows, width),
            preferred_element_type=jnp.float32,
        ).astype(jnp.bfloat16)


def unpack(got, counts, tiles, width, cols):
    parts = len(got)
    each, wide = got[0].shape
    local_rows = each // tiles
    whole = pl.BlockSpec(memory_space=pltpu.VMEM)
    return pl.pallas_call(
        functools.partial(unpack_kernel, tiles=tiles, width=width),
        in_specs=[pl.BlockSpec(memory_space=pltpu.SMEM)] + [whole] * parts,
        out_specs=[whole, whole],
        out_shape=[
            jax.ShapeDtypeStruct((tiles * WINDOW, width), jnp.bfloat16),
            jax.ShapeDtypeStruct((parts * each * ((wide - width) // cols), cols), jnp.bfloat16),
        ],
        scratch_shapes=[pltpu.VMEM((tiles, parts, local_rows, width), jnp.bfloat16)],
        cost_estimate=pl.CostEstimate(
            flops=2 * tiles * WINDOW * parts * local_rows * width,
            bytes_accessed=2 * parts * each * wide,
            transcendentals=0,
        ),
    )(counts, *got)


def text_kernel(place_ref, *refs):
    parts = len(refs) - 5
    chunk_refs = refs[:parts]
    cos_ref, sin_ref, gain_ref, weight_ref, out_ref = refs[parts:]
    width = chunk_refs[0].shape[1]
    mine = place_ref[0]
    squares = None
    total = None
    for s, chunk_ref in enumerate(chunk_refs):
        at = lax.rem(mine + (parts - s), parts)
        rows = chunk_ref[...].astype(jnp.float32)
        part = jnp.sum(rows * rows, axis=1, keepdims=True)
        squares = part if squares is None else squares + part
        scaled = (rows * gain_ref[pl.ds(at, 1), :]).astype(jnp.bfloat16)
        block = weight_ref[pl.ds(pl.multiple_of(at * width, width), width), :]
        term = jnp.dot(scaled, block, preferred_element_type=jnp.float32)
        total = term if total is None else total + term
    scale = lax.rsqrt(squares * (1.0 / (parts * width)) + epsilon)

    def store(p, value):
        out_ref[:, p * HS : (p + 1) * HS] = value

    rotate_store(total * scale, cos_ref[...], sin_ref[...], store)


def text_qkv_of(chunks, mine, cosine, sine, gain, all_qkv):
    rows, width = chunks[0].shape
    parts = len(chunks)
    outs = all_qkv.shape[1]
    whole = pl.BlockSpec(memory_space=pltpu.VMEM)
    return pl.pallas_call(
        text_kernel,
        in_specs=[pl.BlockSpec(memory_space=pltpu.SMEM)] + [whole] * (parts + 4),
        out_specs=whole,
        out_shape=jax.ShapeDtypeStruct((rows, outs), jnp.bfloat16),
        cost_estimate=pl.CostEstimate(
            flops=2 * rows * parts * width * outs,
            bytes_accessed=2 * parts * width * (rows + outs),
            transcendentals=0,
        ),
    )(mine.reshape(1), *chunks, cosine, sine, gain.reshape(parts, width), all_qkv)


def image_kernel(*refs, groups, with_hidden):
    chunk_refs = refs[:groups]
    cos_ref, sin_ref, proj_ref, bias_ref, gain_ref, qkv_ref = refs[groups : groups + 6]
    out_ref = refs[groups + 6]
    hidden_ref = refs[groups + 7] if with_hidden else None
    rows_ref, sum_ref, squares_ref = refs[-3:]
    tiles, local_rows, depth = chunk_refs[0].shape
    each = tiles * local_rows
    step = pl.program_id(0)

    @pl.when(step == 0)
    def _():
        for g, chunk_ref in enumerate(chunk_refs):
            rows_ref[g * each : (g + 1) * each, :] = chunk_ref[...].reshape(each, depth)
        sum_ref[...] = jnp.zeros_like(sum_ref)
        squares_ref[...] = jnp.zeros_like(squares_ref)

    projected = (
        jnp.dot(rows_ref[...], proj_ref[...], preferred_element_type=jnp.float32) + bias_ref[...]
    ).astype(jnp.bfloat16)
    if with_hidden:
        hidden_ref[...] = projected[:each]
    wide = projected.astype(jnp.float32)
    squares_ref[...] += jnp.sum(wide * wide, axis=1, keepdims=True)
    scaled = (wide * gain_ref[...]).astype(jnp.bfloat16)
    sum_ref[...] += jnp.dot(scaled, qkv_ref[...], preferred_element_type=jnp.float32)

    @pl.when(step == pl.num_programs(0) - 1)
    def _():
        model_width = proj_ref.shape[1] * pl.num_programs(0)
        scale = lax.rsqrt(squares_ref[...] * (1.0 / model_width) + epsilon)
        shape = (groups, tiles, local_rows, HS)
        cosine = jnp.broadcast_to(cos_ref[...][:, None], shape).reshape(groups * each, HS)
        sine = jnp.broadcast_to(sin_ref[...][:, None], shape).reshape(groups * each, HS)

        def store(p, value):
            out_ref[:, :, :, p * HS : (p + 1) * HS] = value.reshape(shape)

        rotate_store(sum_ref[...] * scale, cosine, sine, store)


def image_qkv_of(chunks, cosine, sine, w_proj, bias, gain, all_qkv, with_hidden):
    groups = len(chunks)
    tiles, local_rows, depth = chunks[0].shape
    model_width, outs = all_qkv.shape
    each = tiles * local_rows
    block = 512
    fixed = lambda *shape: pl.BlockSpec(shape, lambda i: (0,) * len(shape))
    out_specs = [fixed(groups, tiles, local_rows, outs)]
    out_shape = [jax.ShapeDtypeStruct((groups, tiles, local_rows, outs), jnp.bfloat16)]
    if with_hidden:
        out_specs.append(pl.BlockSpec((each, block), lambda i: (0, i)))
        out_shape.append(jax.ShapeDtypeStruct((each, model_width), jnp.bfloat16))
    return pl.pallas_call(
        functools.partial(image_kernel, groups=groups, with_hidden=with_hidden),
        grid=(model_width // block,),
        in_specs=[fixed(tiles, local_rows, depth)] * groups
        + [
            fixed(groups, local_rows, HS),
            fixed(groups, local_rows, HS),
            pl.BlockSpec((depth, block), lambda i: (0, i)),
            pl.BlockSpec((1, block), lambda i: (0, i)),
            pl.BlockSpec((1, block), lambda i: (0, i)),
            pl.BlockSpec((block, outs), lambda i: (i, 0)),
        ],
        out_specs=out_specs,
        out_shape=out_shape,
        scratch_shapes=[
            pltpu.VMEM((groups * each, depth), jnp.bfloat16),
            pltpu.VMEM((groups * each, outs), jnp.float32),
            pltpu.VMEM((groups * each, 1), jnp.float32),
        ],
        compiler_params=pltpu.CompilerParams(dimension_semantics=("arbitrary",)),
        cost_estimate=pl.CostEstimate(
            flops=2 * groups * each * model_width * (depth + outs),
            bytes_accessed=2 * model_width * (depth + outs),
            transcendentals=0,
        ),
    )(*chunks, cosine, sine, w_proj, bias, gain, all_qkv)


def attend_kernel(counts_ref, early_ref, late_ref, text_ref, out_ref, rows_ref, *, orders):
    tile = pl.program_id(0)
    patch = counts_ref[0, tile]
    texts = counts_ref[1, tile]
    mine = counts_ref[2, 0]
    length = patch + texts
    parts, local_rows, outs = rows_ref.shape
    for ref, order in zip((early_ref, late_ref), orders):
        for at, s in enumerate(order):
            rows_ref[lax.rem(mine + (parts - s), parts)] = ref[at, 0]
    rows = parts * local_rows
    row = lax.broadcasted_iota(jnp.int32, (rows, WINDOW), 0)
    place = lax.broadcasted_iota(jnp.int32, (rows, WINDOW), 1)
    placing = jnp.where((row == patch + place) & (place < texts), 1.0, 0.0).astype(jnp.bfloat16)
    placed = jnp.dot(placing, text_ref[...], preferred_element_type=jnp.float32)
    image_row = lax.broadcasted_iota(jnp.int32, (rows, outs), 0) < patch
    qkv = jnp.where(
        image_row, rows_ref[...].reshape(rows, outs).astype(jnp.float32), placed
    ).astype(jnp.bfloat16)
    keys = qkv[:, GROUP * HS : (GROUP + 1) * HS]
    values = qkv[:, (GROUP + 1) * HS :]
    at_row = lax.broadcasted_iota(jnp.int32, (rows, rows), 0)
    at_col = lax.broadcasted_iota(jnp.int32, (rows, rows), 1)
    allowed = (at_col <= at_row) & (at_col < length)
    for g in range(GROUP):
        scores = lax.dot_general(
            qkv[:, g * HS : (g + 1) * HS],
            keys,
            (((1,), (1,)), ((), ())),
            preferred_element_type=jnp.float32,
        ) * (1.0 / math.sqrt(HS))
        scores = jnp.where(allowed, scores, -1e30)
        row_max = jnp.max(scores, axis=1, keepdims=True)
        weights = jnp.where(allowed, jnp.exp(scores - row_max), 0.0)
        probabilities = (weights / jnp.sum(weights, axis=1, keepdims=True)).astype(jnp.bfloat16)
        attended = jnp.dot(probabilities, values, preferred_element_type=jnp.float32)
        out_ref[:, :, :, g * HS : (g + 1) * HS] = attended.astype(jnp.bfloat16).reshape(
            parts, 1, local_rows, HS
        )


def attend(early, late, orders, text_qkv, counts):
    tiles, local_rows, outs = early.shape[1:]
    parts = early.shape[0] + late.shape[0]
    rows = parts * local_rows
    return pl.pallas_call(
        functools.partial(attend_kernel, orders=orders),
        grid_spec=pltpu.PrefetchScalarGridSpec(
            num_scalar_prefetch=1,
            grid=(tiles,),
            in_specs=[
                pl.BlockSpec((early.shape[0], 1, local_rows, outs), lambda t, c: (0, t, 0, 0)),
                pl.BlockSpec((late.shape[0], 1, local_rows, outs), lambda t, c: (0, t, 0, 0)),
                pl.BlockSpec((WINDOW, outs), lambda t, c: (t, 0)),
            ],
            out_specs=pl.BlockSpec((parts, 1, local_rows, GROUP * HS), lambda t, c: (0, t, 0, 0)),
            scratch_shapes=[pltpu.VMEM((parts, local_rows, outs), jnp.bfloat16)],
        ),
        out_shape=jax.ShapeDtypeStruct((parts, tiles, local_rows, GROUP * HS), jnp.bfloat16),
        compiler_params=pltpu.CompilerParams(dimension_semantics=("arbitrary",)),
        cost_estimate=pl.CostEstimate(
            flops=tiles * rows * (2 * WINDOW * outs + 4 * GROUP * rows * HS),
            bytes_accessed=4 * tiles * rows * outs,
            transcendentals=tiles * GROUP * rows * rows,
        ),
    )(counts, early, late, text_qkv)


def out_kernel(att_ref, weight_ref, hidden_ref, out_ref, rows_ref):
    heads, _, head_width = att_ref.shape

    @pl.when(pl.program_id(0) == 0)
    def _():
        for h in range(heads):
            rows_ref[:, h * head_width : (h + 1) * head_width] = att_ref[h]

    weights = jnp.concatenate([weight_ref[j] for j in range(weight_ref.shape[0])], axis=1)
    total = jnp.dot(rows_ref[...], weights, preferred_element_type=jnp.float32)
    out_ref[...] = (hidden_ref[...].astype(jnp.float32) + total).astype(jnp.bfloat16)


def project_out(attended, weight_blocks, hidden):
    heads, rows, head_width = attended.shape
    blocks, depth, width = weight_blocks.shape
    step = 4
    return pl.pallas_call(
        out_kernel,
        grid=(blocks // step,),
        in_specs=[
            pl.BlockSpec((heads, rows, head_width), lambda i: (0, 0, 0)),
            pl.BlockSpec((step, depth, width), lambda i: (i, 0, 0)),
            pl.BlockSpec((rows, step * width), lambda i: (0, i)),
        ],
        out_specs=pl.BlockSpec((rows, step * width), lambda i: (0, i)),
        out_shape=jax.ShapeDtypeStruct((rows, blocks * width), jnp.bfloat16),
        scratch_shapes=[pltpu.VMEM((rows, depth), jnp.bfloat16)],
        compiler_params=pltpu.CompilerParams(dimension_semantics=("arbitrary",)),
        cost_estimate=pl.CostEstimate(
            flops=2 * rows * depth * blocks * width,
            bytes_accessed=2 * depth * blocks * width,
            transcendentals=0,
        ),
    )(attended, weight_blocks, hidden)


def body(
    vit_features,
    patch_counts,
    text_counts,
    tile_dest,
    text_embeds,
    w_proj,
    b_proj,
    norm_gain,
    w_qkv,
    w_out,
):
    parts = lax.axis_size("mp")
    mine = lax.axis_index("mp")
    image_count, local_rows, _ = vit_features.shape
    model_width = text_embeds.shape[-1]
    slice_width = model_width // parts
    each = image_count * local_rows
    lengths = patch_counts + text_counts
    counts = jnp.stack([patch_counts, text_counts, jnp.full((image_count,), mine, jnp.int32)])

    all_qkv = lax.all_gather(w_qkv[0, :, 0], "dp", axis=0, tiled=True)

    payload = pack(text_embeds, w_out[0, 0], mine, parts)
    got = [payload[0]] + [shifted(payload[s], "mp", s) for s in range(1, parts)]
    window, all_heads = unpack(got, counts, image_count, slice_width, w_out.shape[3])
    all_out = lax.all_gather(all_heads[None], "dp", axis=0, tiled=True)

    arrived = exchange_tiles(vit_features, tile_dest)
    chunks = ring_chunks(arrived, "mp")
    text_chunks = ring_chunks(window, "mp")

    text_places = patch_counts[:, None] + jnp.arange(WINDOW, dtype=jnp.int32)[None, :]
    text_cos, text_sin = rotation_tables(text_places.reshape(-1))
    half = parts // 2
    near = [0] + [s for k in range(1, half - 1) for s in (k, parts - k)]
    far = [half - 1, half + 1, half]
    orders = (tuple(near), tuple(far))
    local = jnp.arange(local_rows, dtype=jnp.int32)
    begins = jnp.stack([lax.rem(mine + (parts - s), parts) * local_rows for s in near + far])
    chunk_cos, chunk_sin = rotation_tables(begins[:, None] + local[None, :])

    bias = b_proj.reshape(1, model_width)
    early, own_projected = image_qkv_of(
        [chunks[s] for s in near],
        chunk_cos[: len(near)],
        chunk_sin[: len(near)],
        w_proj,
        bias,
        norm_gain,
        all_qkv,
        True,
    )
    (late,) = image_qkv_of(
        [chunks[s] for s in far],
        chunk_cos[len(near) :],
        chunk_sin[len(near) :],
        w_proj,
        bias,
        norm_gain,
        all_qkv,
        False,
    )
    text_qkv = text_qkv_of(text_chunks, mine, text_cos, text_sin, norm_gain, all_qkv)

    own_rows = (mine * local_rows + local)[None, :, None]
    hidden = jnp.where(
        own_rows < patch_counts[:, None, None],
        own_projected.reshape(image_count, local_rows, model_width),
        jnp.where(
            own_rows < lengths[:, None, None], text_embeds, jnp.zeros_like(text_embeds)
        ),
    ).reshape(each, model_width)

    attended = attend(early, late, orders, text_qkv, counts)
    returned = lax.all_to_all(
        attended.reshape(parts, each, -1), "mp", split_axis=0, concat_axis=0, tiled=True
    )
    out = project_out(returned, all_out, hidden)
    return out.reshape(image_count, local_rows, model_width)


def solution(mesh):
    in_specs = (
        P("dp", "mp", None),
        P("dp"),
        P("dp"),
        P("dp"),
        P("dp", "mp", None),
        P(),
        P(),
        P(),
        P(None, "dp", "mp", None),
        P(None, "mp", None, "dp"),
    )
    out_specs = P("dp", "mp", None)

    return jax.shard_map(body, mesh=mesh, in_specs=in_specs, out_specs=out_specs, check_vma=False)
```

profile of v0, /device:TPU:1, one launch (start us, length us, event | category | flops | bytes accessed | tf_op | source)
XLA Modules:
  0.0 213.7 jit_solution(10563479736871875056)
XLA Ops:
  6.5 0.7 all-gather.5.cloned.1.call-update
  7.3 2.5 %shard_map.103 = (bf16[128,768]{1,0:T(8,128)(2,1)}, bf16[128,768]{1,0:T(8,128)(2,1)}, bf16[128,768]{1,0:T(8,128)(2,1)}, bf16[128,768]{1,0:T(8,128)(2,1)}, bf16[1...) custom-call(s32[1]{0:T(128)} %bitcast.21.place_ref, ...), custom_call_target="tpu_custom_call" | custom-call | flops 1048576 | bytes 3145728 | tf_op jit(solution)/shard_map/pallas_call | solution.py:122
  9.8 7.7 %collective-permute-start.10 = (bf16[128,768]{1,0:T(8,128)(2,1)}, bf16[128,768]{1,0:T(8,128)(2,1)S(1)}, u32[]{:S(2)}, u32[]{:S(2)}) collective-permute-start(bf16[128,768]{1,0:T(8,128)(2,1)} %get-tuple-element.22), channel_id=1, source_target_pairs={{0,4},{1,5},{2,6},{3,7},{4,0},{5,1},{6,2},{7,3},{8,12},{9,13},{10,... | collective-permute-start | bytes 589832 | tf_op jit(solution)/shard_map/ppermute | solution.py:23
  17.5 4.0 %collective-permute-start.12 = (bf16[128,768]{1,0:T(8,128)(2,1)}, bf16[128,768]{1,0:T(8,128)(2,1)S(1)}, u32[]{:S(2)}, u32[]{:S(2)}) collective-permute-start(bf16[128,768]{1,0:T(8,128)(2,1)} %get-tuple-element.24), channel_id=1, source_target_pairs={{0,6},{1,7},{2,0},{3,1},{4,2},{5,3},{6,4},{7,5},{8,14},{9,15},{10,... | collective-permute-start | bytes 589832 | tf_op jit(solution)/shard_map/ppermute | solution.py:23
  21.5 0.7 collective-permute-start.13
  22.3 0.7 collective-permute-start.7
  23.0 0.1 pad.12.clone
  23.1 5.0 %collective-permute-start.8 = (bf16[128,768]{1,0:T(8,128)(2,1)}, bf16[128,768]{1,0:T(8,128)(2,1)S(1)}, u32[]{:S(2)}, u32[]{:S(2)}) collective-permute-start(bf16[128,768]{1,0:T(8,128)(2,1)} %get-tuple-element.20), channel_id=1, source_target_pairs={{0,2},{1,3},{2,4},{3,5},{4,6},{5,7},{6,0},{7,1},{8,10},{9,11},{10,... | collective-permute-start | bytes 589832 | tf_op jit(solution)/shard_map/ppermute | solution.py:23
  28.1 12.2 %collective-permute-done.11.refs_5_ = bf16[128,768]{1,0:T(8,128)(2,1)S(1)} collective-permute-done((bf16[128,768]{1,0:T(8,128)(2,1)}, bf16[128,768]{1,0:T(8,128)(2,1)S(1)}, u32[]{:S(2)}, u32[]{:S(2)}) %collective-permute-start.11) | collective-permute-done | bytes 196640 | tf_op jit(solution)/shard_map/ppermute | solution.py:23
  40.4 5.3 %collective-permute-start.9 = (bf16[128,768]{1,0:T(8,128)(2,1)}, bf16[128,768]{1,0:T(8,128)(2,1)S(1)}, u32[]{:S(2)}, u32[]{:S(2)}) collective-permute-start(bf16[128,768]{1,0:T(8,128)(2,1)} %get-tuple-element.21), channel_id=1, source_target_pairs={{0,3},{1,4},{2,5},{3,6},{4,7},{5,0},{6,1},{7,2},{8,11},{9,12},{10,... | collective-permute-start | bytes 589832 | tf_op jit(solution)/shard_map/ppermute | solution.py:23
  45.6 1.3 add_add_fusion.counts_ref
  46.9 1.8 collective-permute-done.12.refs_6_
  48.7 3.8 %collective-permute-done.13.refs_7_ = bf16[128,768]{1,0:T(8,128)(2,1)S(1)} collective-permute-done((bf16[128,768]{1,0:T(8,128)(2,1)}, bf16[128,768]{1,0:T(8,128)(2,1)S(1)}, u32[]{:S(2)}, u32[]{:S(2)}) %collective-permute-start.13) | collective-permute-done | bytes 196640 | tf_op jit(solution)/shard_map/ppermute | solution.py:23
  52.5 2.8 %collective-permute-done.9.refs_3_ = bf16[128,768]{1,0:T(8,128)(2,1)S(1)} collective-permute-done((bf16[128,768]{1,0:T(8,128)(2,1)}, bf16[128,768]{1,0:T(8,128)(2,1)S(1)}, u32[]{:S(2)}, u32[]{:S(2)}) %collective-permute-start.9) | collective-permute-done | bytes 196640 | tf_op jit(solution)/shard_map/ppermute | solution.py:23
  55.3 0.6 copy-done.16
  55.9 2.6 %shard_map.104 = (bf16[256,512]{1,0:T(8,128)(2,1)}, bf16[2048,128]{1,0:T(8,128)(2,1)}) custom-call(s32[3,4]{1,0:T(4,128)} %add_add_fusion.counts_ref, bf16[128,768]{1,0:T(8,128)(2,1)} %get-tuple-element.18.refs_0_, bf16[128,768]{1,0:T(8,128)(2,1)} %copy-done.14, bf16[128,768]{1,0:T(8,128)(2,1)} %copy-done.15, bf16[128,768]{1,0:T(8,128)(2,1)} %copy-done.16, ...), custom_call_target="tpu_custom_call" | custom-call | flops 67108864 | bytes 1572864 | tf_op jit(solution)/shard_map/pallas_call | solution.py:166
  58.6 1.2 copy.19
  59.8 0.7 convert_element_type.20
  60.4 0.1 broadcast_in_dim.16
  60.5 0.8 pad_maximum_fusion
  61.3 8.1 %all-to-all-start = ((bf16[32,4,1152]{2,1,0:T(4,128)(2,1)}), bf16[32,4,1152]{2,1,0:T(4,128)(2,1)S(1)}, u32[]{:S(2)}, u32[]{:S(2)}) async-start(bf16[32,4,1152]{2,1,0:T(4,128)(2,1)} %pad_maximum_fusion), calls=%async_computation | async-start | bytes 589824 | tf_op jit(solution)/shard_map/all_to_all | solution.py:81
  69.5 0.1 stack.47
  69.6 9.2 %all-to-all-done = bf16[32,4,1152]{2,1,0:T(4,128)(2,1)S(1)} async-done(((bf16[32,4,1152]{2,1,0:T(4,128)(2,1)}), bf16[32,4,1152]{2,1,0:T(4,128)(2,1)S(1)}, u32[]{:S(2)}, u32[]{:S(2)}) %all-to-all-start) | async-done | bytes 294944 | tf_op jit(solution)/shard_map/all_to_all | solution.py:81
  78.8 0.8 reshape.149.got_ref
  79.5 2.1 shard_map.100
  81.6 1.8 reshape.150
  83.4 3.7 %all-to-all-start.1 = ((bf16[32,4,1024]{2,1,0:T(4,128)(2,1)}), bf16[32,4,1024]{2,1,0:T(4,128)(2,1)S(1)}, u32[]{:S(2)}, u32[]{:S(2)}) async-start(bf16[32,4,1024]{2,1,0:T(4,128)(2,1)} %reshape.150), calls=%async_computation.1 | async-start | bytes 524288 | tf_op jit(solution)/shard_map/all_to_all | solution.py:90
  87.2 2.3 %collective-permute-start.14 = (bf16[256,512]{1,0:T(8,128)(2,1)}, bf16[256,512]{1,0:T(8,128)(2,1)S(1)}, u32[]{:S(2)}, u32[]{:S(2)}) collective-permute-start(bf16[256,512]{1,0:T(8,128)(2,1)} %get-tuple-element.26.refs_0_), channel_id=1, source_target_pairs={{0,1},{1,2},{2,3},{3,4},{4,5},{5,6},{6,7},{7,0},{8,9},{9,10},{10,1... | collective-permute-start | bytes 786440 | tf_op jit(solution)/shard_map/ppermute | solution.py:23
  89.5 7.9 %all-to-all-done.1 = bf16[32,4,1024]{2,1,0:T(4,128)(2,1)S(1)} async-done(((bf16[32,4,1024]{2,1,0:T(4,128)(2,1)}), bf16[32,4,1024]{2,1,0:T(4,128)(2,1)S(1)}, u32[]{:S(2)}, u32[]{:S(2)}) %all-to-all-start.1) | async-done | bytes 262176 | tf_op jit(solution)/shard_map/all_to_all | solution.py:90
  97.4 0.1 copy.18
  97.5 1.9 collective-permute-start
  99.3 0.5 multiply_sine_fusion.1
  99.9 1.6 collective-permute-start.18
  101.6 0.1 convert_element_type.23
  101.7 2.8 %collective-permute-start.1 = (bf16[4,32,1024]{2,1,0:T(8,128)(2,1)S(1)}, bf16[4,32,1024]{2,1,0:T(8,128)(2,1)S(1)}, u32[]{:S(2)}, u32[]{:S(2)}) collective-permute-start(bf16[4,32,1024]{2,1,0:T(8,128)(2,1)S(1)} %bitcast.35), channel_id=1, source_target_pairs={{0,7},{1,0},{2,1},{3,2},{4,3},{5,4},{6,5},{7,6},{8,15},{9,8},{10,9... | collective-permute-start | bytes 786440 | tf_op jit(solution)/shard_map/ppermute | solution.py:23
  104.5 2.5 %collective-permute-done.refs_1_ = bf16[4,32,1024]{2,1,0:T(8,128)(2,1)S(1)} collective-permute-done((bf16[4,32,1024]{2,1,0:T(8,128)(2,1)S(1)}, bf16[4,32,1024]{2,1,0:T(8,128)(2,1)S(1)}, u32[]{:S(2)}, u32[]{:S(2)}) %collective-permute-start) | collective-permute-done | bytes 262176 | tf_op jit(solution)/shard_map/ppermute | solution.py:23
  107.0 0.5 fusion.2
  107.6 2.7 %collective-permute-start.19 = (bf16[256,512]{1,0:T(8,128)(2,1)S(1)}, bf16[256,512]{1,0:T(8,128)(2,1)S(1)}, u32[]{:S(2)}, u32[]{:S(2)}) collective-permute-start(bf16[256,512]{1,0:T(8,128)(2,1)S(1)} %collective-permute-done.18.refs_7_), channel_id=1, source_target_pairs={{0,7},{1,0},{2,1},{3,2},{4,3},{5,4},{6,5},{7,6},{8,15},{9,8},{10,9... | collective-permute-start | bytes 786440 | tf_op jit(solution)/shard_map/ppermute | solution.py:23
  110.3 2.4 %collective-permute-done.15.refs_2_ = bf16[256,512]{1,0:T(8,128)(2,1)S(1)} collective-permute-done((bf16[256,512]{1,0:T(8,128)(2,1)S(1)}, bf16[256,512]{1,0:T(8,128)(2,1)S(1)}, u32[]{:S(2)}, u32[]{:S(2)}) %collective-permute-start.15) | collective-permute-done | bytes 262176 | tf_op jit(solution)/shard_map/ppermute | solution.py:23
  112.8 0.3 collective-permute-done.1.refs_2_
  113.1 2.9 %collective-permute-start.3 = (bf16[4,32,1024]{2,1,0:T(8,128)(2,1)S(1)}, bf16[4,32,1024]{2,1,0:T(8,128)(2,1)}, u32[]{:S(2)}, u32[]{:S(2)}) collective-permute-start(bf16[4,32,1024]{2,1,0:T(8,128)(2,1)S(1)} %collective-permute-done.1.refs_2_), channel_id=1, source_target_pairs={{0,7},{1,0},{2,1},{3,2},{4,3},{5,4},{6,5},{7,6},{8,15},{9,8},{10,9... | collective-permute-start | bytes 786440 | tf_op jit(solution)/shard_map/ppermute | solution.py:23
  116.0 2.4 %collective-permute-done.2.refs_3_ = bf16[4,32,1024]{2,1,0:T(8,128)(2,1)S(1)} collective-permute-done((bf16[4,32,1024]{2,1,0:T(8,128)(2,1)S(1)}, bf16[4,32,1024]{2,1,0:T(8,128)(2,1)S(1)}, u32[]{:S(2)}, u32[]{:S(2)}) %collective-permute-start.2) | collective-permute-done | bytes 262176 | tf_op jit(solution)/shard_map/ppermute | solution.py:23
  118.4 0.3 collective-permute-done.19.refs_6_
  118.7 2.9 %collective-permute-start.20 = (bf16[256,512]{1,0:T(8,128)(2,1)S(1)}, bf16[256,512]{1,0:T(8,128)(2,1)S(1)}, u32[]{:S(2)}, u32[]{:S(2)}) collective-permute-start(bf16[256,512]{1,0:T(8,128)(2,1)S(1)} %collective-permute-done.19.refs_6_), channel_id=1, source_target_pairs={{0,7},{1,0},{2,1},{3,2},{4,3},{5,4},{6,5},{7,6},{8,15},{9,8},{10,9... | collective-permute-start | bytes 786440 | tf_op jit(solution)/shard_map/ppermute | solution.py:23
  121.6 2.4 %collective-permute-done.16.refs_3_ = bf16[256,512]{1,0:T(8,128)(2,1)S(1)} collective-permute-done((bf16[256,512]{1,0:T(8,128)(2,1)S(1)}, bf16[256,512]{1,0:T(8,128)(2,1)S(1)}, u32[]{:S(2)}, u32[]{:S(2)}) %collective-permute-start.16) | collective-permute-done | bytes 262176 | tf_op jit(solution)/shard_map/ppermute | solution.py:23
  124.0 0.8 fusion
  124.8 2.7 %collective-permute-start.5 = (bf16[4,32,1024]{2,1,0:T(8,128)(2,1)}, bf16[4,32,1024]{2,1,0:T(8,128)(2,1)}, u32[]{:S(2)}, u32[]{:S(2)}) collective-permute-start(bf16[4,32,1024]{2,1,0:T(8,128)(2,1)} %collective-permute-done.3.refs_4_), channel_id=1, source_target_pairs={{0,7},{1,0},{2,1},{3,2},{4,3},{5,4},{6,5},{7,6},{8,15},{9,8},{10,9... | collective-permute-start | bytes 786440 | tf_op jit(solution)/shard_map/ppermute | solution.py:23
  127.4 2.1 %collective-permute-done.4.refs_0_ = bf16[4,32,1024]{2,1,0:T(8,128)(2,1)} collective-permute-done((bf16[4,32,1024]{2,1,0:T(8,128)(2,1)S(1)}, bf16[4,32,1024]{2,1,0:T(8,128)(2,1)}, u32[]{:S(2)}, u32[]{:S(2)}) %collective-permute-start.4) | collective-permute-done | bytes 262176 | tf_op jit(solution)/shard_map/ppermute | solution.py:23
  129.6 0.8 pad_maximum_fusion.3
  130.3 0.5 broadcast.108
  130.9 0.7 reduce.3
  131.6 0.6 reshape.153.refs_10_
  132.2 0.9 pad_maximum_fusion.1
  133.0 2.2 %collective-permute-done.17.refs_4_ = bf16[256,512]{1,0:T(8,128)(2,1)S(1)} collective-permute-done((bf16[256,512]{1,0:T(8,128)(2,1)S(1)}, bf16[256,512]{1,0:T(8,128)(2,1)S(1)}, u32[]{:S(2)}, u32[]{:S(2)}) %collective-permute-start.17) | collective-permute-done | bytes 262176 | tf_op jit(solution)/shard_map/ppermute | solution.py:23
  135.3 0.7 copy-done.8
  135.9 5.2 %shard_map.105.text_ref = bf16[256,512]{1,0:T(8,128)(2,1)} custom-call(s32[1]{0:T(128)} %bitcast.21.place_ref, bf16[256,512]{1,0:T(8,128)(2,1)} %get-tuple-element.26.refs_0_, bf16[256,512]{1,0:T(8,128)(2,1)} %copy-done.2, bf16[256,512]{1,0:T(8,128)(2,1)} %copy-done.4, bf16[256,512]{1,0:T(8,128)(2,1)} %copy-done.6, bf16[256,512]{1,0:T(8,128)(2,1)} %copy-done.8, ...), custom_call_target="tpu_custom_call" | custom-call | flops 1073741824 | bytes 6291456 | tf_op jit(solution)/shard_map/pallas_call | solution.py:213
  141.2 11.8 %shard_map.102.late_ref = bf16[3,4,32,512]{3,2,1,0:T(8,128)(2,1)} custom-call(bf16[4,32,1024]{2,1,0:T(8,128)(2,1)} %collective-permute-done.4.refs_0_, bf16[4,32,1024]{2,1,0:T(8,128)(2,1)} %collective-permute-done.5.refs_1_, bf16[4,32,1024]{2,1,0:T(8,128)(2,1)} %collective-permute-done.6.refs_2_, f32[3,32,128]{2,1,0:T(8,128)} %get-tuple-element.40.refs_3_, ...), custom_call_target="tpu_custom_call" | custom-call | flops 4831838208 | bytes 12582912 | tf_op jit(solution)/shard_map/pallas_call | solution.py:279
  153.0 13.9 %shard_map.101 = (bf16[5,4,32,512]{3,2,1,0:T(8,128)(2,1)}, bf16[128,4096]{1,0:T(8,128)(2,1)}) custom-call(bf16[4,32,1024]{2,1,0:T(8,128)(2,1)} %bitcast.36, bf16[4,32,1024]{2,1,0:T(8,128)(2,1)} %copy-done.20, bf16[4,32,1024]{2,1,0:T(8,128)(2,1)} %copy-done.21, bf16[4,32,1024]{2,1,0:T(8,128)(2,1)} %copy-done.22, ...), custom_call_target="tpu_custom_call" | custom-call | flops 8053063680 | bytes 12582912 | tf_op jit(solution)/shard_map/pallas_call | solution.py:279
  166.9 6.0 %shard_map.106 = bf16[8,4,32,256]{3,2,1,0:T(8,128)(2,1)} custom-call(s32[3,4]{1,0:T(4,128)} %add_add_fusion.counts_ref, bf16[5,4,32,512]{3,2,1,0:T(8,128)(2,1)} %get-tuple-element.17.early_ref, bf16[3,4,32,512]{3,2,1,0:T(8,128)(2,1)} %shard_map.102.late_ref, bf16[256,512]{1,0:T(8,128)(2,1)} %shard_map.105.text_ref), custom_call_target="tpu_custom_call" | custom-call | flops 335544320 | bytes 2097152 | tf_op jit(solution)/shard_map/pallas_call | solution.py:352
  172.9 4.3 %all-to-all-start.2 = ((bf16[8,128,256]{2,1,0:T(8,128)(2,1)}), bf16[8,128,256]{2,1,0:T(8,128)(2,1)S(1)}, u32[]{:S(2)}, u32[]{:S(2)}) async-start(bf16[8,128,256]{2,1,0:T(8,128)(2,1)} %bitcast.31), calls=%async_computation.2 | async-start | bytes 1048576 | tf_op jit(solution)/shard_map/all_to_all | solution.py:487
  177.2 2.5 %select_select_fusion = bf16[4,32,4096]{2,1,0:T(8,128)(2,1)} fusion(bf16[4,32,4096]{2,1,0:T(8,128)(2,1)} %bitcast.32, bf16[4,32,4096]{2,1,0:T(8,128)(2,1)S(1)} %copy-done, pred[4,32]{1,0:T(4,128)(4,1)S(1)} %get-tuple-element.36, pred[4,32]{1,0:T(4,128)(4,1)S(1)} %get-tuple-element.35), kind=kLoop, calls=%fused_computation | loop fusion | flops 1048576 | bytes 3145984 | tf_op jit(solution)/shard_map/jit(_where)/select_n | solution.py:478
  179.6 15.5 %all-to-all-done.2.att_ref = bf16[8,128,256]{2,1,0:T(8,128)(2,1)S(1)} async-done(((bf16[8,128,256]{2,1,0:T(8,128)(2,1)}), bf16[8,128,256]{2,1,0:T(8,128)(2,1)S(1)}, u32[]{:S(2)}, u32[]{:S(2)}) %all-to-all-start.2) | async-done | bytes 524320 | tf_op jit(solution)/shard_map/all_to_all | solution.py:487
  195.1 0.8 copy-done.1
  195.9 11.0 %shard_map.107 = bf16[128,4096]{1,0:T(8,128)(2,1)} custom-call(bf16[8,128,256]{2,1,0:T(8,128)(2,1)} %copy-done.1, bf16[32,2048,128]{2,1,0:T(8,128)(2,1)} %bitcast.26, bf16[128,4096]{1,0:T(8,128)(2,1)} %bitcast.27), custom_call_target="tpu_custom_call" | custom-call | flops 2147483648 | bytes 16777216 | tf_op jit(solution)/shard_map/pallas_call | solution.py:392
  (70 shorter events, 0.4 us)
Async XLA Ops:
  6.5 95.0 %copy-start.18 = (s32[4]{0:T(128)S(1)}, s32[4]{0:T(128)}, u32[]{:S(2)}) copy-start(s32[4]{0:T(128)} %param.11) | copy-start | bytes 52
  6.5 106.2 %copy-start.19 = (s32[4]{0:T(128)S(1)}, s32[4]{0:T(128)}, u32[]{:S(2)}) copy-start(s32[4]{0:T(128)} %param.12) | copy-start | bytes 52
  6.5 124.4 %copy-start.17 = (f32[1,4096]{1,0:T(1,128)S(1)}, f32[1,4096]{1,0:T(1,128)}, u32[]{:S(2)}) copy-start(f32[1,4096]{1,0:T(1,128)} %refs_7_.3) | copy-start | bytes 49156
  6.5 128.7 %all-gather.5.cloned.1.call-start = ((), (), s32[]{:S(2)}) async-start(), calls=%async_computation.3 | async-start | bytes 4325376 | tf_op jit(solution)/shard_map/all_gather | solution.py:433
  7.3 187.9 %all-gather.7.cloned.1.call-start = ((), (), s32[]{:S(2)}) async-start(), calls=%async_computation.4 | async-start | bytes 17301504 | tf_op jit(solution)/shard_map/all_gather | solution.py:438
  9.8 13.3 %collective-permute-start.10 = (bf16[128,768]{1,0:T(8,128)(2,1)}, bf16[128,768]{1,0:T(8,128)(2,1)S(1)}, u32[]{:S(2)}, u32[]{:S(2)}) collective-permute-start(bf16[128,768]{1,0:T(8,128)(2,1)} %get-tuple-element.22), channel_id=1, source_target_pairs={{0,4},{1,5},{2,6},{3,7},{4,0},{5,1},{6,2},{7,3},{8,12},{9,13},{10,... | collective-permute-start | bytes 589832 | tf_op jit(solution)/shard_map/ppermute | solution.py:23
  17.5 22.9 %collective-permute-start.11 = (bf16[128,768]{1,0:T(8,128)(2,1)}, bf16[128,768]{1,0:T(8,128)(2,1)S(1)}, u32[]{:S(2)}, u32[]{:S(2)}) collective-permute-start(bf16[128,768]{1,0:T(8,128)(2,1)} %get-tuple-element.23), channel_id=1, source_target_pairs={{0,5},{1,6},{2,7},{3,0},{4,1},{5,2},{6,3},{7,4},{8,13},{9,14},{10,... | collective-permute-start | bytes 589832 | tf_op jit(solution)/shard_map/ppermute | solution.py:23
  17.5 31.2 %collective-permute-start.12 = (bf16[128,768]{1,0:T(8,128)(2,1)}, bf16[128,768]{1,0:T(8,128)(2,1)S(1)}, u32[]{:S(2)}, u32[]{:S(2)}) collective-permute-start(bf16[128,768]{1,0:T(8,128)(2,1)} %get-tuple-element.24), channel_id=1, source_target_pairs={{0,6},{1,7},{2,0},{3,1},{4,2},{5,3},{6,4},{7,5},{8,14},{9,15},{10,... | collective-permute-start | bytes 589832 | tf_op jit(solution)/shard_map/ppermute | solution.py:23
  21.5 30.9 %collective-permute-start.13 = (bf16[128,768]{1,0:T(8,128)(2,1)}, bf16[128,768]{1,0:T(8,128)(2,1)S(1)}, u32[]{:S(2)}, u32[]{:S(2)}) collective-permute-start(bf16[128,768]{1,0:T(8,128)(2,1)} %get-tuple-element.25), channel_id=1, source_target_pairs={{0,7},{1,0},{2,1},{3,2},{4,3},{5,4},{6,5},{7,6},{8,15},{9,8},{10,9... | collective-permute-start | bytes 589832 | tf_op jit(solution)/shard_map/ppermute | solution.py:23
  22.3 30.2 %collective-permute-start.7 = (bf16[128,768]{1,0:T(8,128)(2,1)}, bf16[128,768]{1,0:T(8,128)(2,1)S(1)}, u32[]{:S(2)}, u32[]{:S(2)}) collective-permute-start(bf16[128,768]{1,0:T(8,128)(2,1)} %get-tuple-element.19), channel_id=1, source_target_pairs={{0,1},{1,2},{2,3},{3,4},{4,5},{5,6},{6,7},{7,0},{8,9},{9,10},{10,1... | collective-permute-start | bytes 589832 | tf_op jit(solution)/shard_map/ppermute | solution.py:23
  23.1 32.2 %copy-start.10 = (bf16[128,768]{1,0:T(8,128)(2,1)}, bf16[128,768]{1,0:T(8,128)(2,1)S(1)}, u32[]{:S(2)}) copy-start(bf16[128,768]{1,0:T(8,128)(2,1)S(1)} %collective-permute-done.10.refs_4_) | copy-start | bytes 589828
  23.1 29.4 %collective-permute-start.8 = (bf16[128,768]{1,0:T(8,128)(2,1)}, bf16[128,768]{1,0:T(8,128)(2,1)S(1)}, u32[]{:S(2)}, u32[]{:S(2)}) collective-permute-start(bf16[128,768]{1,0:T(8,128)(2,1)} %get-tuple-element.20), channel_id=1, source_target_pairs={{0,2},{1,3},{2,4},{3,5},{4,6},{5,7},{6,0},{7,1},{8,10},{9,11},{10,... | collective-permute-start | bytes 589832 | tf_op jit(solution)/shard_map/ppermute | solution.py:23
  40.4 14.9 %copy-start.11 = (bf16[128,768]{1,0:T(8,128)(2,1)}, bf16[128,768]{1,0:T(8,128)(2,1)S(1)}, u32[]{:S(2)}) copy-start(bf16[128,768]{1,0:T(8,128)(2,1)S(1)} %collective-permute-done.11.refs_5_) | copy-start | bytes 589828
  40.4 14.9 %collective-permute-start.9 = (bf16[128,768]{1,0:T(8,128)(2,1)}, bf16[128,768]{1,0:T(8,128)(2,1)S(1)}, u32[]{:S(2)}, u32[]{:S(2)}) collective-permute-start(bf16[128,768]{1,0:T(8,128)(2,1)} %get-tuple-element.21), channel_id=1, source_target_pairs={{0,3},{1,4},{2,5},{3,6},{4,7},{5,0},{6,1},{7,2},{8,11},{9,12},{10,... | collective-permute-start | bytes 589832 | tf_op jit(solution)/shard_map/ppermute | solution.py:23
  48.7 6.6 %copy-start.12 = (bf16[128,768]{1,0:T(8,128)(2,1)}, bf16[128,768]{1,0:T(8,128)(2,1)S(1)}, u32[]{:S(2)}) copy-start(bf16[128,768]{1,0:T(8,128)(2,1)S(1)} %collective-permute-done.12.refs_6_) | copy-start | bytes 589828
  52.5 2.8 %copy-start.13 = (bf16[128,768]{1,0:T(8,128)(2,1)}, bf16[128,768]{1,0:T(8,128)(2,1)S(1)}, u32[]{:S(2)}) copy-start(bf16[128,768]{1,0:T(8,128)(2,1)S(1)} %collective-permute-done.13.refs_7_) | copy-start | bytes 589828
  52.5 2.8 %copy-start.14 = (bf16[128,768]{1,0:T(8,128)(2,1)}, bf16[128,768]{1,0:T(8,128)(2,1)S(1)}, u32[]{:S(2)}) copy-start(bf16[128,768]{1,0:T(8,128)(2,1)S(1)} %collective-permute-done.7.refs_1_) | copy-start | bytes 589828
  52.5 2.8 %copy-start.15 = (bf16[128,768]{1,0:T(8,128)(2,1)}, bf16[128,768]{1,0:T(8,128)(2,1)S(1)}, u32[]{:S(2)}) copy-start(bf16[128,768]{1,0:T(8,128)(2,1)S(1)} %collective-permute-done.8.refs_2_) | copy-start | bytes 589828
  55.3 0.7 copy-start.16
  61.3 17.4 %all-to-all-start = ((bf16[32,4,1152]{2,1,0:T(4,128)(2,1)}), bf16[32,4,1152]{2,1,0:T(4,128)(2,1)S(1)}, u32[]{:S(2)}, u32[]{:S(2)}) async-start(bf16[32,4,1152]{2,1,0:T(4,128)(2,1)} %pad_maximum_fusion), calls=%async_computation | async-start | bytes 589824 | tf_op jit(solution)/shard_map/all_to_all | solution.py:81
  83.4 14.0 %all-to-all-start.1 = ((bf16[32,4,1024]{2,1,0:T(4,128)(2,1)}), bf16[32,4,1024]{2,1,0:T(4,128)(2,1)S(1)}, u32[]{:S(2)}, u32[]{:S(2)}) async-start(bf16[32,4,1024]{2,1,0:T(4,128)(2,1)} %reshape.150), calls=%async_computation.1 | async-start | bytes 524288 | tf_op jit(solution)/shard_map/all_to_all | solution.py:90
  87.2 14.3 %collective-permute-start.14 = (bf16[256,512]{1,0:T(8,128)(2,1)}, bf16[256,512]{1,0:T(8,128)(2,1)S(1)}, u32[]{:S(2)}, u32[]{:S(2)}) collective-permute-start(bf16[256,512]{1,0:T(8,128)(2,1)} %get-tuple-element.26.refs_0_), channel_id=1, source_target_pairs={{0,1},{1,2},{2,3},{3,4},{4,5},{5,6},{6,7},{7,0},{8,9},{9,10},{10,1... | collective-permute-start | bytes 786440 | tf_op jit(solution)/shard_map/ppermute | solution.py:23
  97.5 55.5 %copy-start.9 = (bf16[32,4,1024]{2,0,1:T(8,128)(2,1)}, bf16[32,4,1024]{2,0,1:T(8,128)(2,1)S(1)}, u32[]{:S(2)}) copy-start(bf16[32,4,1024]{2,0,1:T(8,128)(2,1)S(1)} %copy.18) | copy-start | bytes 786436
  97.5 9.5 %collective-permute-start = (bf16[4,32,1024]{2,1,0:T(8,128)(2,1)S(1)}, bf16[4,32,1024]{2,1,0:T(8,128)(2,1)S(1)}, u32[]{:S(2)}, u32[]{:S(2)}) collective-permute-start(bf16[4,32,1024]{2,1,0:T(8,128)(2,1)S(1)} %bitcast.34), channel_id=1, source_target_pairs={{0,1},{1,2},{2,3},{3,4},{4,5},{5,6},{6,7},{7,0},{8,9},{9,10},{10,1... | collective-permute-start | bytes 786440 | tf_op jit(solution)/shard_map/ppermute | solution.py:23
  99.9 7.7 %collective-permute-start.18 = (bf16[256,512]{1,0:T(8,128)(2,1)}, bf16[256,512]{1,0:T(8,128)(2,1)S(1)}, u32[]{:S(2)}, u32[]{:S(2)}) collective-permute-start(bf16[256,512]{1,0:T(8,128)(2,1)} %get-tuple-element.26.refs_0_), channel_id=1, source_target_pairs={{0,7},{1,0},{2,1},{3,2},{4,3},{5,4},{6,5},{7,6},{8,15},{9,8},{10,9... | collective-permute-start | bytes 786440 | tf_op jit(solution)/shard_map/ppermute | solution.py:23
  101.5 33.7 %copy-start.2 = (bf16[256,512]{1,0:T(8,128)(2,1)}, bf16[256,512]{1,0:T(8,128)(2,1)S(1)}, u32[]{:S(2)}) copy-start(bf16[256,512]{1,0:T(8,128)(2,1)S(1)} %collective-permute-done.14.refs_1_) | copy-start | bytes 786436
  101.5 11.2 %collective-permute-start.15 = (bf16[256,512]{1,0:T(8,128)(2,1)S(1)}, bf16[256,512]{1,0:T(8,128)(2,1)S(1)}, u32[]{:S(2)}, u32[]{:S(2)}) collective-permute-start(bf16[256,512]{1,0:T(8,128)(2,1)S(1)} %collective-permute-done.14.refs_1_), channel_id=1, source_target_pairs={{0,1},{1,2},{2,3},{3,4},{4,5},{5,6},{6,7},{7,0},{8,9},{9,10},{10,1... | collective-permute-start | bytes 786440 | tf_op jit(solution)/shard_map/ppermute | solution.py:23
  101.7 11.4 %collective-permute-start.1 = (bf16[4,32,1024]{2,1,0:T(8,128)(2,1)S(1)}, bf16[4,32,1024]{2,1,0:T(8,128)(2,1)S(1)}, u32[]{:S(2)}, u32[]{:S(2)}) collective-permute-start(bf16[4,32,1024]{2,1,0:T(8,128)(2,1)S(1)} %bitcast.35), channel_id=1, source_target_pairs={{0,7},{1,0},{2,1},{3,2},{4,3},{5,4},{6,5},{7,6},{8,15},{9,8},{10,9... | collective-permute-start | bytes 786440 | tf_op jit(solution)/shard_map/ppermute | solution.py:23
  107.0 46.0 %copy-start.20 = (bf16[4,32,1024]{2,1,0:T(8,128)(2,1)}, bf16[4,32,1024]{2,1,0:T(8,128)(2,1)S(1)}, u32[]{:S(2)}) copy-start(bf16[4,32,1024]{2,1,0:T(8,128)(2,1)S(1)} %collective-permute-done.refs_1_) | copy-start | bytes 786436
  107.0 11.3 %collective-permute-start.2 = (bf16[4,32,1024]{2,1,0:T(8,128)(2,1)S(1)}, bf16[4,32,1024]{2,1,0:T(8,128)(2,1)S(1)}, u32[]{:S(2)}, u32[]{:S(2)}) collective-permute-start(bf16[4,32,1024]{2,1,0:T(8,128)(2,1)S(1)} %collective-permute-done.refs_1_), channel_id=1, source_target_pairs={{0,1},{1,2},{2,3},{3,4},{4,5},{5,6},{6,7},{7,0},{8,9},{9,10},{10,1... | collective-permute-start | bytes 786440 | tf_op jit(solution)/shard_map/ppermute | solution.py:23
  107.6 27.6 %copy-start.3 = (bf16[256,512]{1,0:T(8,128)(2,1)}, bf16[256,512]{1,0:T(8,128)(2,1)S(1)}, u32[]{:S(2)}) copy-start(bf16[256,512]{1,0:T(8,128)(2,1)S(1)} %collective-permute-done.18.refs_7_) | copy-start | bytes 786436
  107.6 11.1 %collective-permute-start.19 = (bf16[256,512]{1,0:T(8,128)(2,1)S(1)}, bf16[256,512]{1,0:T(8,128)(2,1)S(1)}, u32[]{:S(2)}, u32[]{:S(2)}) collective-permute-start(bf16[256,512]{1,0:T(8,128)(2,1)S(1)} %collective-permute-done.18.refs_7_), channel_id=1, source_target_pairs={{0,7},{1,0},{2,1},{3,2},{4,3},{5,4},{6,5},{7,6},{8,15},{9,8},{10,9... | collective-permute-start | bytes 786440 | tf_op jit(solution)/shard_map/ppermute | solution.py:23
  112.7 22.5 %copy-start.4 = (bf16[256,512]{1,0:T(8,128)(2,1)}, bf16[256,512]{1,0:T(8,128)(2,1)S(1)}, u32[]{:S(2)}) copy-start(bf16[256,512]{1,0:T(8,128)(2,1)S(1)} %collective-permute-done.15.refs_2_) | copy-start | bytes 786436
  112.7 11.2 %collective-permute-start.16 = (bf16[256,512]{1,0:T(8,128)(2,1)S(1)}, bf16[256,512]{1,0:T(8,128)(2,1)S(1)}, u32[]{:S(2)}, u32[]{:S(2)}) collective-permute-start(bf16[256,512]{1,0:T(8,128)(2,1)S(1)} %collective-permute-done.15.refs_2_), channel_id=1, source_target_pairs={{0,1},{1,2},{2,3},{3,4},{4,5},{5,6},{6,7},{7,0},{8,9},{9,10},{10,1... | collective-permute-start | bytes 786440 | tf_op jit(solution)/shard_map/ppermute | solution.py:23
  113.1 39.9 %copy-start.21 = (bf16[4,32,1024]{2,1,0:T(8,128)(2,1)}, bf16[4,32,1024]{2,1,0:T(8,128)(2,1)S(1)}, u32[]{:S(2)}) copy-start(bf16[4,32,1024]{2,1,0:T(8,128)(2,1)S(1)} %collective-permute-done.1.refs_2_) | copy-start | bytes 786436
  113.1 11.7 %collective-permute-start.3 = (bf16[4,32,1024]{2,1,0:T(8,128)(2,1)S(1)}, bf16[4,32,1024]{2,1,0:T(8,128)(2,1)}, u32[]{:S(2)}, u32[]{:S(2)}) collective-permute-start(bf16[4,32,1024]{2,1,0:T(8,128)(2,1)S(1)} %collective-permute-done.1.refs_2_), channel_id=1, source_target_pairs={{0,7},{1,0},{2,1},{3,2},{4,3},{5,4},{6,5},{7,6},{8,15},{9,8},{10,9... | collective-permute-start | bytes 786440 | tf_op jit(solution)/shard_map/ppermute | solution.py:23
  118.4 6.4 %copy-start.22 = (bf16[4,32,1024]{2,1,0:T(8,128)(2,1)}, bf16[4,32,1024]{2,1,0:T(8,128)(2,1)S(1)}, u32[]{:S(2)}) copy-start(bf16[4,32,1024]{2,1,0:T(8,128)(2,1)S(1)} %collective-permute-done.2.refs_3_) | copy-start | bytes 786436
  118.4 11.2 %collective-permute-start.4 = (bf16[4,32,1024]{2,1,0:T(8,128)(2,1)S(1)}, bf16[4,32,1024]{2,1,0:T(8,128)(2,1)}, u32[]{:S(2)}, u32[]{:S(2)}) collective-permute-start(bf16[4,32,1024]{2,1,0:T(8,128)(2,1)S(1)} %collective-permute-done.2.refs_3_), channel_id=1, source_target_pairs={{0,1},{1,2},{2,3},{3,4},{4,5},{5,6},{6,7},{7,0},{8,9},{9,10},{10,1... | collective-permute-start | bytes 786440 | tf_op jit(solution)/shard_map/ppermute | solution.py:23
  118.7 16.5 %copy-start.5 = (bf16[256,512]{1,0:T(8,128)(2,1)}, bf16[256,512]{1,0:T(8,128)(2,1)S(1)}, u32[]{:S(2)}) copy-start(bf16[256,512]{1,0:T(8,128)(2,1)S(1)} %collective-permute-done.19.refs_6_) | copy-start | bytes 786436
  118.7 14.3 %collective-permute-start.20 = (bf16[256,512]{1,0:T(8,128)(2,1)S(1)}, bf16[256,512]{1,0:T(8,128)(2,1)S(1)}, u32[]{:S(2)}, u32[]{:S(2)}) collective-permute-start(bf16[256,512]{1,0:T(8,128)(2,1)S(1)} %collective-permute-done.19.refs_6_), channel_id=1, source_target_pairs={{0,7},{1,0},{2,1},{3,2},{4,3},{5,4},{6,5},{7,6},{8,15},{9,8},{10,9... | collective-permute-start | bytes 786440 | tf_op jit(solution)/shard_map/ppermute | solution.py:23
  124.0 11.3 %copy-start.6 = (bf16[256,512]{1,0:T(8,128)(2,1)}, bf16[256,512]{1,0:T(8,128)(2,1)S(1)}, u32[]{:S(2)}) copy-start(bf16[256,512]{1,0:T(8,128)(2,1)S(1)} %collective-permute-done.16.refs_3_) | copy-start | bytes 786436
  124.0 11.2 %collective-permute-start.17 = (bf16[256,512]{1,0:T(8,128)(2,1)S(1)}, bf16[256,512]{1,0:T(8,128)(2,1)S(1)}, u32[]{:S(2)}, u32[]{:S(2)}) collective-permute-start(bf16[256,512]{1,0:T(8,128)(2,1)S(1)} %collective-permute-done.16.refs_3_), channel_id=1, source_target_pairs={{0,1},{1,2},{2,3},{3,4},{4,5},{5,6},{6,7},{7,0},{8,9},{9,10},{10,1... | collective-permute-start | bytes 786440 | tf_op jit(solution)/shard_map/ppermute | solution.py:23
  124.8 16.4 %collective-permute-start.5 = (bf16[4,32,1024]{2,1,0:T(8,128)(2,1)}, bf16[4,32,1024]{2,1,0:T(8,128)(2,1)}, u32[]{:S(2)}, u32[]{:S(2)}) collective-permute-start(bf16[4,32,1024]{2,1,0:T(8,128)(2,1)} %collective-permute-done.3.refs_4_), channel_id=1, source_target_pairs={{0,7},{1,0},{2,1},{3,2},{4,3},{5,4},{6,5},{7,6},{8,15},{9,8},{10,9... | collective-permute-start | bytes 786440 | tf_op jit(solution)/shard_map/ppermute | solution.py:23
  129.6 11.6 %collective-permute-start.6 = (bf16[4,32,1024]{2,1,0:T(8,128)(2,1)}, bf16[4,32,1024]{2,1,0:T(8,128)(2,1)}, u32[]{:S(2)}, u32[]{:S(2)}) collective-permute-start(bf16[4,32,1024]{2,1,0:T(8,128)(2,1)} %collective-permute-done.4.refs_0_), channel_id=1, source_target_pairs={{0,1},{1,2},{2,3},{3,4},{4,5},{5,6},{6,7},{7,0},{8,9},{9,10},{10,1... | collective-permute-start | bytes 786440 | tf_op jit(solution)/shard_map/ppermute | solution.py:23
  133.0 2.2 %copy-start.7 = (bf16[256,512]{1,0:T(8,128)(2,1)}, bf16[256,512]{1,0:T(8,128)(2,1)S(1)}, u32[]{:S(2)}) copy-start(bf16[256,512]{1,0:T(8,128)(2,1)S(1)} %collective-permute-done.20.refs_5_) | copy-start | bytes 786436
  135.2 0.7 copy-start.8
  153.0 24.2 %copy-start = (bf16[4,32,4096]{2,1,0:T(8,128)(2,1)S(1)}, bf16[4,32,4096]{2,1,0:T(8,128)(2,1)}, u32[]{:S(2)}) copy-start(bf16[4,32,4096]{2,1,0:T(8,128)(2,1)} %text_ref.1) | copy-start | bytes 3145732
  172.9 22.3 %all-to-all-start.2 = ((bf16[8,128,256]{2,1,0:T(8,128)(2,1)}), bf16[8,128,256]{2,1,0:T(8,128)(2,1)S(1)}, u32[]{:S(2)}, u32[]{:S(2)}) async-start(bf16[8,128,256]{2,1,0:T(8,128)(2,1)} %bitcast.31), calls=%async_computation.2 | async-start | bytes 1048576 | tf_op jit(solution)/shard_map/all_to_all | solution.py:487
  195.1 0.8 copy-start.1
Sparse Core Ops, SparseCore 0:
  9.9 55.2 all-gather.4
  67.7 79.0 all-gather.6
where the time goes:
time: 215 us; the launch traced here: 214 us
  waiting for transfers between devices  68.5 us (32%)
  starting transfers between devices  59.5 us (28%)
  Pallas kernels  55.1 us (26%)
  between operations  13.7 us (6%)
  other arithmetic  9.59 us (4%)
  local copies, waits for them, and re-layouts  7.41 us (3%)
    ppermute x21, starting transfers between devices, shifted(): lax.ppermute(value, axis, [(i, (i + step) % size) for i in range(size)])  43.3 us
    ppermute x21, waiting for transfers between devices, shifted(): lax.ppermute(value, axis, [(i, (i + step) % size) for i in range(size)])  35.2 us
    pallas_call x2, Pallas kernels, image_qkv_of(): pl.pallas_call(functools.partial(image_kernel, groups=groups, with_hidden...  25.7 us
    all_to_all x1, waiting for transfers between devices, body(): lax.all_to_all(attended.reshape(parts, each, -1), 'mp', split_axis=0, con...  15.5 us
    pallas_call x1, Pallas kernels, project_out(): pl.pallas_call(out_kernel, grid=(blocks // step,), in_specs=[pl.BlockSpec...  11 us
    all_to_all x1, waiting for transfers between devices, exchange_tiles(): got = lax.all_to_all(sent, 'dp', split_axis=0, concat_axis=0, tiled=True)  9.19 us
    all_to_all x1, starting transfers between devices, exchange_tiles(): got = lax.all_to_all(sent, 'dp', split_axis=0, concat_axis=0, tiled=True)  8.1 us
    all_to_all x1, waiting for transfers between devices, exchange_tiles(): lax.all_to_all(ordered.reshape(ranks, image_count, width), 'dp', split_ax...  7.88 us
  transfers between devices with their start and end apart: 26, of which 15 were waited for; matrix products, arithmetic and copies ran while one was open for 7% of the time, Pallas kernels for 21%

commit v1 on v0

--- a/solution.py
+++ b/solution.py
@@ -12,24 +12,29 @@
 HS = 128
 GROUP = 2
 WINDOW = 64
+IMAGE_ROWS = 192
 EXTRA = 128
 
 rope_base = 500000.0
 epsilon = 1e-05
 
 
-def shifted(value, axis, step):
+def shifted(value, axis, step, sources=None):
     size = lax.axis_size(axis)
-    return lax.ppermute(value, axis, [(i, (i + step) % size) for i in range(size)])
-
-
-def ring_chunks(own, axis):
+    pairs = [(i, (i + step) % size) for i in range(size) if sources is None or i in sources]
+    return lax.ppermute(value, axis, pairs)
+
+
+def ring_chunks(own, axis, useful=None):
     size = lax.axis_size(axis)
+    useful = size if useful is None else useful
     chunks = [own] + [None] * (size - 1)
     for s in range(1, size // 2 + 1):
-        chunks[s] = shifted(chunks[s - 1], axis, 1)
+        holders = [(o + s - 1) % size for o in range(useful)]
+        chunks[s] = shifted(chunks[s - 1], axis, 1, holders)
         if s < size - s:
-            chunks[size - s] = shifted(chunks[(size - s + 1) % size], axis, -1)
+            holders = [(o - s + 1) % size for o in range(useful)]
+            chunks[size - s] = shifted(chunks[(size - s + 1) % size], axis, -1, holders)
     return chunks
 
 
@@ -438,7 +443,7 @@
     all_out = lax.all_gather(all_heads[None], "dp", axis=0, tiled=True)
 
     arrived = exchange_tiles(vit_features, tile_dest)
-    chunks = ring_chunks(arrived, "mp")
+    chunks = ring_chunks(arrived, "mp", -(-IMAGE_ROWS // local_rows))
     text_chunks = ring_chunks(window, "mp")
 
     text_places = patch_counts[:, None] + jnp.arange(WINDOW, dtype=jnp.int32)[None, :]

time: 215 us -> 215 us (level)
  waiting for transfers between devices: 68.5 us -> 56 us
  starting transfers between devices: 59.5 us -> 70.8 us
    ppermute x21, waiting for transfers between devices: 35.2 us -> 26 us  [shifted(): return lax.ppermute(value, axis, pairs)]
    ppermute x21, starting transfers between devices: 43.3 us -> 52.2 us  [shifted(): return lax.ppermute(value, axis, pairs)]
    all_to_all x1, waiting for transfers between devices: 15.5 us -> 12.2 us  [body(): lax.all_to_all(attended.reshape(parts, each, -1), 'mp', split_axis=0, con...]
    all_to_all x1, starting transfers between devices: 4.3 us -> 6.72 us  [body(): lax.all_to_all(attended.reshape(parts, each, -1), 'mp', split_axis=0, con...]
  transfers between devices with their start and end apart: 26 -> 26, of which waited for: 15 -> 12; matrix products, arithmetic and copies ran while one was open for 7% -> 7% of each run, Pallas kernels for 21% -> 21%
where the time goes in v1:
time: 215 us; the launch traced here: 213 us
  starting transfers between devices  70.8 us (33%)
  waiting for transfers between devices  56 us (26%)
  Pallas kernels  55 us (26%)
  between operations  13.7 us (6%)
  other arithmetic  9.59 us (4%)
  local copies, waits for them, and re-layouts  7.46 us (3%)
    ppermute x21, starting transfers between devices, shifted(): return lax.ppermute(value, axis, pairs)  52.2 us
    ppermute x21, waiting for transfers between devices, shifted(): return lax.ppermute(value, axis, pairs)  26 us
    pallas_call x2, Pallas kernels, image_qkv_of(): pl.pallas_call(functools.partial(image_kernel, groups=groups, with_hidden...  25.6 us
    all_to_all x1, waiting for transfers between devices, body(): lax.all_to_all(attended.reshape(parts, each, -1), 'mp', split_axis=0, con...  12.2 us
    pallas_call x1, Pallas kernels, project_out(): pl.pallas_call(out_kernel, grid=(blocks // step,), in_specs=[pl.BlockSpec...  11 us
    all_to_all x1, waiting for transfers between devices, exchange_tiles(): got = lax.all_to_all(sent, 'dp', split_axis=0, concat_axis=0, tiled=True)  9.19 us
    all_to_all x1, starting transfers between devices, exchange_tiles(): got = lax.all_to_all(sent, 'dp', split_axis=0, concat_axis=0, tiled=True)  8.1 us
    all_to_all x1, waiting for transfers between devices, exchange_tiles(): lax.all_to_all(ordered.reshape(ranks, image_count, width), 'dp', split_ax...  7.88 us
  transfers between devices with their start and end apart: 26, of which 12 were waited for; matrix products, arithmetic and copies ran while one was open for 7% of the time, Pallas kernels for 21%

profile of v1, /device:TPU:1, one launch (start us, length us, event | category | flops | bytes accessed | tf_op | source)
XLA Modules:
  0.0 212.5 jit_solution(17295632665221165991)
XLA Ops:
  6.5 0.7 all-gather.5.cloned.1.call-update
  7.3 2.5 %shard_map.103 = (bf16[128,768]{1,0:T(8,128)(2,1)}, bf16[128,768]{1,0:T(8,128)(2,1)}, bf16[128,768]{1,0:T(8,128)(2,1)}, bf16[128,768]{1,0:T(8,128)(2,1)}, bf16[1...) custom-call(s32[1]{0:T(128)} %bitcast.21.place_ref, ...), custom_call_target="tpu_custom_call" | custom-call | flops 1048576 | bytes 3145728 | tf_op jit(solution)/shard_map/pallas_call | solution.py:127
  9.8 7.7 %collective-permute-start.10 = (bf16[128,768]{1,0:T(8,128)(2,1)}, bf16[128,768]{1,0:T(8,128)(2,1)S(1)}, u32[]{:S(2)}, u32[]{:S(2)}) collective-permute-start(bf16[128,768]{1,0:T(8,128)(2,1)} %get-tuple-element.22), channel_id=1, source_target_pairs={{0,4},{1,5},{2,6},{3,7},{4,0},{5,1},{6,2},{7,3},{8,12},{9,13},{10,... | collective-permute-start | bytes 589832 | tf_op jit(solution)/shard_map/ppermute | solution.py:25
  17.5 4.0 %collective-permute-start.12 = (bf16[128,768]{1,0:T(8,128)(2,1)}, bf16[128,768]{1,0:T(8,128)(2,1)S(1)}, u32[]{:S(2)}, u32[]{:S(2)}) collective-permute-start(bf16[128,768]{1,0:T(8,128)(2,1)} %get-tuple-element.24), channel_id=1, source_target_pairs={{0,6},{1,7},{2,0},{3,1},{4,2},{5,3},{6,4},{7,5},{8,14},{9,15},{10,... | collective-permute-start | bytes 589832 | tf_op jit(solution)/shard_map/ppermute | solution.py:25
  21.5 0.7 collective-permute-start.13
  22.3 0.7 collective-permute-start.7
  23.1 5.0 %collective-permute-start.8 = (bf16[128,768]{1,0:T(8,128)(2,1)}, bf16[128,768]{1,0:T(8,128)(2,1)S(1)}, u32[]{:S(2)}, u32[]{:S(2)}) collective-permute-start(bf16[128,768]{1,0:T(8,128)(2,1)} %get-tuple-element.20), channel_id=1, source_target_pairs={{0,2},{1,3},{2,4},{3,5},{4,6},{5,7},{6,0},{7,1},{8,10},{9,11},{10,... | collective-permute-start | bytes 589832 | tf_op jit(solution)/shard_map/ppermute | solution.py:25
  28.1 12.2 %collective-permute-done.11.refs_5_ = bf16[128,768]{1,0:T(8,128)(2,1)S(1)} collective-permute-done((bf16[128,768]{1,0:T(8,128)(2,1)}, bf16[128,768]{1,0:T(8,128)(2,1)S(1)}, u32[]{:S(2)}, u32[]{:S(2)}) %collective-permute-start.11) | collective-permute-done | bytes 196640 | tf_op jit(solution)/shard_map/ppermute | solution.py:25
  40.4 5.3 %collective-permute-start.9 = (bf16[128,768]{1,0:T(8,128)(2,1)}, bf16[128,768]{1,0:T(8,128)(2,1)S(1)}, u32[]{:S(2)}, u32[]{:S(2)}) collective-permute-start(bf16[128,768]{1,0:T(8,128)(2,1)} %get-tuple-element.21), channel_id=1, source_target_pairs={{0,3},{1,4},{2,5},{3,6},{4,7},{5,0},{6,1},{7,2},{8,11},{9,12},{10,... | collective-permute-start | bytes 589832 | tf_op jit(solution)/shard_map/ppermute | solution.py:25
  45.6 1.3 add_add_fusion.counts_ref
  46.9 1.8 collective-permute-done.12.refs_6_
  48.7 3.8 %collective-permute-done.13.refs_7_ = bf16[128,768]{1,0:T(8,128)(2,1)S(1)} collective-permute-done((bf16[128,768]{1,0:T(8,128)(2,1)}, bf16[128,768]{1,0:T(8,128)(2,1)S(1)}, u32[]{:S(2)}, u32[]{:S(2)}) %collective-permute-start.13) | collective-permute-done | bytes 196640 | tf_op jit(solution)/shard_map/ppermute | solution.py:25
  52.5 2.8 %collective-permute-done.9.refs_3_ = bf16[128,768]{1,0:T(8,128)(2,1)S(1)} collective-permute-done((bf16[128,768]{1,0:T(8,128)(2,1)}, bf16[128,768]{1,0:T(8,128)(2,1)S(1)}, u32[]{:S(2)}, u32[]{:S(2)}) %collective-permute-start.9) | collective-permute-done | bytes 196640 | tf_op jit(solution)/shard_map/ppermute | solution.py:25
  55.3 0.6 copy-done.16
  55.9 2.6 %shard_map.104 = (bf16[256,512]{1,0:T(8,128)(2,1)}, bf16[2048,128]{1,0:T(8,128)(2,1)}) custom-call(s32[3,4]{1,0:T(4,128)} %add_add_fusion.counts_ref, bf16[128,768]{1,0:T(8,128)(2,1)} %get-tuple-element.18.refs_0_, bf16[128,768]{1,0:T(8,128)(2,1)} %copy-done.14, bf16[128,768]{1,0:T(8,128)(2,1)} %copy-done.15, bf16[128,768]{1,0:T(8,128)(2,1)} %copy-done.16, ...), custom_call_target="tpu_custom_call" | custom-call | flops 67108864 | bytes 1572864 | tf_op jit(solution)/shard_map/pallas_call | solution.py:171
  58.6 1.2 copy.19
  59.8 0.7 convert_element_type.20
  60.5 0.8 pad_maximum_fusion
  61.3 8.1 %all-to-all-start = ((bf16[32,4,1152]{2,1,0:T(4,128)(2,1)}), bf16[32,4,1152]{2,1,0:T(4,128)(2,1)S(1)}, u32[]{:S(2)}, u32[]{:S(2)}) async-start(bf16[32,4,1152]{2,1,0:T(4,128)(2,1)} %pad_maximum_fusion), calls=%async_computation | async-start | bytes 589824 | tf_op jit(solution)/shard_map/all_to_all | solution.py:86
  69.5 0.1 stack.47
  69.6 9.2 %all-to-all-done = bf16[32,4,1152]{2,1,0:T(4,128)(2,1)S(1)} async-done(((bf16[32,4,1152]{2,1,0:T(4,128)(2,1)}), bf16[32,4,1152]{2,1,0:T(4,128)(2,1)S(1)}, u32[]{:S(2)}, u32[]{:S(2)}) %all-to-all-start) | async-done | bytes 294944 | tf_op jit(solution)/shard_map/all_to_all | solution.py:86
  78.8 0.8 reshape.149.got_ref
  79.5 2.1 shard_map.100
  81.6 1.8 reshape.150
  83.4 3.7 %all-to-all-start.1 = ((bf16[32,4,1024]{2,1,0:T(4,128)(2,1)}), bf16[32,4,1024]{2,1,0:T(4,128)(2,1)S(1)}, u32[]{:S(2)}, u32[]{:S(2)}) async-start(bf16[32,4,1024]{2,1,0:T(4,128)(2,1)} %reshape.150), calls=%async_computation.1 | async-start | bytes 524288 | tf_op jit(solution)/shard_map/all_to_all | solution.py:95
  87.2 2.3 %collective-permute-start.14 = (bf16[256,512]{1,0:T(8,128)(2,1)}, bf16[256,512]{1,0:T(8,128)(2,1)S(1)}, u32[]{:S(2)}, u32[]{:S(2)}) collective-permute-start(bf16[256,512]{1,0:T(8,128)(2,1)} %get-tuple-element.26.refs_0_), channel_id=1, source_target_pairs={{0,1},{1,2},{2,3},{3,4},{4,5},{5,6},{6,7},{7,0},{8,9},{9,10},{10,1... | collective-permute-start | bytes 786440 | tf_op jit(solution)/shard_map/ppermute | solution.py:25
  89.5 7.9 %all-to-all-done.1 = bf16[32,4,1024]{2,1,0:T(4,128)(2,1)S(1)} async-done(((bf16[32,4,1024]{2,1,0:T(4,128)(2,1)}), bf16[32,4,1024]{2,1,0:T(4,128)(2,1)S(1)}, u32[]{:S(2)}, u32[]{:S(2)}) %all-to-all-start.1) | async-done | bytes 262176 | tf_op jit(solution)/shard_map/all_to_all | solution.py:95
  97.5 3.7 %collective-permute-start = (bf16[4,32,1024]{2,1,0:T(8,128)(2,1)S(1)}, bf16[4,32,1024]{2,1,0:T(8,128)(2,1)S(1)}, u32[]{:S(2)}, u32[]{:S(2)}) collective-permute-start(bf16[4,32,1024]{2,1,0:T(8,128)(2,1)S(1)} %bitcast.34), channel_id=1, source_target_pairs={{0,1},{1,2},{2,3},{3,4},{4,5},{5,6},{8,9},{9,10},{10,11},{11,12},{... | collective-permute-start | bytes 786440 | tf_op jit(solution)/shard_map/ppermute | solution.py:25
  101.2 0.5 multiply_sine_fusion.1
  101.7 0.4 collective-permute-start.18
  102.1 1.2 collective-permute-start.15
  103.4 3.4 %collective-permute-start.1 = (bf16[4,32,1024]{2,1,0:T(8,128)(2,1)S(1)}, bf16[4,32,1024]{2,1,0:T(8,128)(2,1)S(1)}, u32[]{:S(2)}, u32[]{:S(2)}) collective-permute-start(bf16[4,32,1024]{2,1,0:T(8,128)(2,1)S(1)} %bitcast.35), channel_id=1, source_target_pairs={{0,7},{1,0},{2,1},{3,2},{4,3},{5,4},{8,15},{9,8},{10,9},{11,10},{1... | collective-permute-start | bytes 786440 | tf_op jit(solution)/shard_map/ppermute | solution.py:25
  106.9 0.7 collective-permute-start.2
  107.5 0.5 fusion.2
  108.1 1.1 collective-permute-done.18.refs_7_
  109.2 1.6 collective-permute-start.19
  110.8 1.2 collective-permute-done.15.refs_2_
  112.0 2.3 %collective-permute-start.16 = (bf16[256,512]{1,0:T(8,128)(2,1)S(1)}, bf16[256,512]{1,0:T(8,128)(2,1)S(1)}, u32[]{:S(2)}, u32[]{:S(2)}) collective-permute-start(bf16[256,512]{1,0:T(8,128)(2,1)S(1)} %collective-permute-done.15.refs_2_), channel_id=1, source_target_pairs={{0,1},{1,2},{2,3},{3,4},{4,5},{5,6},{6,7},{7,0},{8,9},{9,10},{10,1... | collective-permute-start | bytes 786440 | tf_op jit(solution)/shard_map/ppermute | solution.py:25
  114.4 0.6 collective-permute-done.1.refs_2_
  114.9 3.5 %collective-permute-start.3 = (bf16[4,32,1024]{2,1,0:T(8,128)(2,1)S(1)}, bf16[4,32,1024]{2,1,0:T(8,128)(2,1)}, u32[]{:S(2)}, u32[]{:S(2)}) collective-permute-start(bf16[4,32,1024]{2,1,0:T(8,128)(2,1)S(1)} %collective-permute-done.1.refs_2_), channel_id=1, source_target_pairs={{0,7},{1,0},{2,1},{3,2},{4,3},{7,6},{8,15},{9,8},{10,9},{11,10},{1... | collective-permute-start | bytes 786440 | tf_op jit(solution)/shard_map/ppermute | solution.py:25
  118.5 1.3 collective-permute-start.4
  119.9 0.7 collective-permute-done.19.refs_6_
  120.6 2.7 %collective-permute-start.20 = (bf16[256,512]{1,0:T(8,128)(2,1)S(1)}, bf16[256,512]{1,0:T(8,128)(2,1)S(1)}, u32[]{:S(2)}, u32[]{:S(2)}) collective-permute-start(bf16[256,512]{1,0:T(8,128)(2,1)S(1)} %collective-permute-done.19.refs_6_), channel_id=1, source_target_pairs={{0,7},{1,0},{2,1},{3,2},{4,3},{5,4},{6,5},{7,6},{8,15},{9,8},{10,9... | collective-permute-start | bytes 786440 | tf_op jit(solution)/shard_map/ppermute | solution.py:25
  123.3 0.3 collective-permute-start.17
  123.6 0.8 fusion
  124.4 1.8 collective-permute-done.3.refs_4_
  126.2 2.5 %collective-permute-start.5 = (bf16[4,32,1024]{2,1,0:T(8,128)(2,1)}, bf16[4,32,1024]{2,1,0:T(8,128)(2,1)}, u32[]{:S(2)}, u32[]{:S(2)}) collective-permute-start(bf16[4,32,1024]{2,1,0:T(8,128)(2,1)} %collective-permute-done.3.refs_4_), channel_id=1, source_target_pairs={{0,7},{1,0},{2,1},{3,2},{6,5},{7,6},{8,15},{9,8},{10,9},{11,10},{1... | collective-permute-start | bytes 786440 | tf_op jit(solution)/shard_map/ppermute | solution.py:25
  128.7 2.8 %collective-permute-start.6 = (bf16[4,32,1024]{2,1,0:T(8,128)(2,1)}, bf16[4,32,1024]{2,1,0:T(8,128)(2,1)}, u32[]{:S(2)}, u32[]{:S(2)}) collective-permute-start(bf16[4,32,1024]{2,1,0:T(8,128)(2,1)} %collective-permute-done.4.refs_0_), channel_id=1, source_target_pairs={{0,1},{3,4},{4,5},{5,6},{6,7},{7,0},{8,9},{11,12},{12,13},{13,14},... | collective-permute-start | bytes 786440 | tf_op jit(solution)/shard_map/ppermute | solution.py:25
  131.5 0.8 pad_maximum_fusion.3
  132.2 0.5 broadcast.108
  132.8 0.7 reduce.3
  133.4 0.6 reshape.153.refs_10_
  134.1 0.9 pad_maximum_fusion.1
  135.0 0.6 copy-done.7
  135.6 0.1 copy-done.8
  135.7 5.2 %shard_map.105.text_ref = bf16[256,512]{1,0:T(8,128)(2,1)} custom-call(s32[1]{0:T(128)} %bitcast.21.place_ref, bf16[256,512]{1,0:T(8,128)(2,1)} %get-tuple-element.26.refs_0_, bf16[256,512]{1,0:T(8,128)(2,1)} %copy-done.2, bf16[256,512]{1,0:T(8,128)(2,1)} %copy-done.4, bf16[256,512]{1,0:T(8,128)(2,1)} %copy-done.6, bf16[256,512]{1,0:T(8,128)(2,1)} %copy-done.8, ...), custom_call_target="tpu_custom_call" | custom-call | flops 1073741824 | bytes 6291456 | tf_op jit(solution)/shard_map/pallas_call | solution.py:218
  140.9 11.7 %shard_map.102.late_ref = bf16[3,4,32,512]{3,2,1,0:T(8,128)(2,1)} custom-call(bf16[4,32,1024]{2,1,0:T(8,128)(2,1)} %collective-permute-done.4.refs_0_, bf16[4,32,1024]{2,1,0:T(8,128)(2,1)} %collective-permute-done.5.refs_1_, bf16[4,32,1024]{2,1,0:T(8,128)(2,1)} %collective-permute-done.6.refs_2_, f32[3,32,128]{2,1,0:T(8,128)} %get-tuple-element.40.refs_3_, ...), custom_call_target="tpu_custom_call" | custom-call | flops 4831838208 | bytes 12582912 | tf_op jit(solution)/shard_map/pallas_call | solution.py:284
  152.7 13.9 %shard_map.101 = (bf16[5,4,32,512]{3,2,1,0:T(8,128)(2,1)}, bf16[128,4096]{1,0:T(8,128)(2,1)}) custom-call(bf16[4,32,1024]{2,1,0:T(8,128)(2,1)} %bitcast.36, bf16[4,32,1024]{2,1,0:T(8,128)(2,1)} %copy-done.20, bf16[4,32,1024]{2,1,0:T(8,128)(2,1)} %copy-done.21, bf16[4,32,1024]{2,1,0:T(8,128)(2,1)} %copy-done.22, ...), custom_call_target="tpu_custom_call" | custom-call | flops 8053063680 | bytes 12582912 | tf_op jit(solution)/shard_map/pallas_call | solution.py:284
  166.6 6.0 %shard_map.106 = bf16[8,4,32,256]{3,2,1,0:T(8,128)(2,1)} custom-call(s32[3,4]{1,0:T(4,128)} %add_add_fusion.counts_ref, bf16[5,4,32,512]{3,2,1,0:T(8,128)(2,1)} %get-tuple-element.17.early_ref, bf16[3,4,32,512]{3,2,1,0:T(8,128)(2,1)} %shard_map.102.late_ref, bf16[256,512]{1,0:T(8,128)(2,1)} %shard_map.105.text_ref), custom_call_target="tpu_custom_call" | custom-call | flops 335544320 | bytes 2097152 | tf_op jit(solution)/shard_map/pallas_call | solution.py:357
  172.6 6.7 %all-to-all-start.2 = ((bf16[8,128,256]{2,1,0:T(8,128)(2,1)}), bf16[8,128,256]{2,1,0:T(8,128)(2,1)S(1)}, u32[]{:S(2)}, u32[]{:S(2)}) async-start(bf16[8,128,256]{2,1,0:T(8,128)(2,1)} %bitcast.31), calls=%async_computation.2 | async-start | bytes 1048576 | tf_op jit(solution)/shard_map/all_to_all | solution.py:492
  179.3 2.5 %select_select_fusion = bf16[4,32,4096]{2,1,0:T(8,128)(2,1)} fusion(bf16[4,32,4096]{2,1,0:T(8,128)(2,1)} %bitcast.32, bf16[4,32,4096]{2,1,0:T(8,128)(2,1)S(1)} %copy-done, pred[4,32]{1,0:T(4,128)(4,1)S(1)} %get-tuple-element.36, pred[4,32]{1,0:T(4,128)(4,1)S(1)} %get-tuple-element.35), kind=kLoop, calls=%fused_computation | loop fusion | flops 1048576 | bytes 3145984 | tf_op jit(solution)/shard_map/jit(_where)/select_n | solution.py:483
  181.8 12.2 %all-to-all-done.2.att_ref = bf16[8,128,256]{2,1,0:T(8,128)(2,1)S(1)} async-done(((bf16[8,128,256]{2,1,0:T(8,128)(2,1)}), bf16[8,128,256]{2,1,0:T(8,128)(2,1)S(1)}, u32[]{:S(2)}, u32[]{:S(2)}) %all-to-all-start.2) | async-done | bytes 524320 | tf_op jit(solution)/shard_map/all_to_all | solution.py:492
  193.9 0.8 copy-done.1
  194.7 11.0 %shard_map.107 = bf16[128,4096]{1,0:T(8,128)(2,1)} custom-call(bf16[8,128,256]{2,1,0:T(8,128)(2,1)} %copy-done.1, bf16[32,2048,128]{2,1,0:T(8,128)(2,1)} %bitcast.26, bf16[128,4096]{1,0:T(8,128)(2,1)} %bitcast.27), custom_call_target="tpu_custom_call" | custom-call | flops 2147483648 | bytes 16777216 | tf_op jit(solution)/shard_map/pallas_call | solution.py:397
  (70 shorter events, 0.8 us)
Async XLA Ops:
  6.5 96.7 %copy-start.18 = (s32[4]{0:T(128)S(1)}, s32[4]{0:T(128)}, u32[]{:S(2)}) copy-start(s32[4]{0:T(128)} %param.11) | copy-start | bytes 52
  6.5 107.8 %copy-start.19 = (s32[4]{0:T(128)S(1)}, s32[4]{0:T(128)}, u32[]{:S(2)}) copy-start(s32[4]{0:T(128)} %param.12) | copy-start | bytes 52
  6.5 126.2 %copy-start.17 = (f32[1,4096]{1,0:T(1,128)S(1)}, f32[1,4096]{1,0:T(1,128)}, u32[]{:S(2)}) copy-start(f32[1,4096]{1,0:T(1,128)} %refs_7_.3) | copy-start | bytes 49156
  6.5 128.4 %all-gather.5.cloned.1.call-start = ((), (), s32[]{:S(2)}) async-start(), calls=%async_computation.3 | async-start | bytes 4325376 | tf_op jit(solution)/shard_map/all_gather | solution.py:438
  7.3 186.7 %all-gather.7.cloned.1.call-start = ((), (), s32[]{:S(2)}) async-start(), calls=%async_computation.4 | async-start | bytes 17301504 | tf_op jit(solution)/shard_map/all_gather | solution.py:443
  9.8 13.3 %collective-permute-start.10 = (bf16[128,768]{1,0:T(8,128)(2,1)}, bf16[128,768]{1,0:T(8,128)(2,1)S(1)}, u32[]{:S(2)}, u32[]{:S(2)}) collective-permute-start(bf16[128,768]{1,0:T(8,128)(2,1)} %get-tuple-element.22), channel_id=1, source_target_pairs={{0,4},{1,5},{2,6},{3,7},{4,0},{5,1},{6,2},{7,3},{8,12},{9,13},{10,... | collective-permute-start | bytes 589832 | tf_op jit(solution)/shard_map/ppermute | solution.py:25
  17.5 22.9 %collective-permute-start.11 = (bf16[128,768]{1,0:T(8,128)(2,1)}, bf16[128,768]{1,0:T(8,128)(2,1)S(1)}, u32[]{:S(2)}, u32[]{:S(2)}) collective-permute-start(bf16[128,768]{1,0:T(8,128)(2,1)} %get-tuple-element.23), channel_id=1, source_target_pairs={{0,5},{1,6},{2,7},{3,0},{4,1},{5,2},{6,3},{7,4},{8,13},{9,14},{10,... | collective-permute-start | bytes 589832 | tf_op jit(solution)/shard_map/ppermute | solution.py:25
  17.5 31.2 %collective-permute-start.12 = (bf16[128,768]{1,0:T(8,128)(2,1)}, bf16[128,768]{1,0:T(8,128)(2,1)S(1)}, u32[]{:S(2)}, u32[]{:S(2)}) collective-permute-start(bf16[128,768]{1,0:T(8,128)(2,1)} %get-tuple-element.24), channel_id=1, source_target_pairs={{0,6},{1,7},{2,0},{3,1},{4,2},{5,3},{6,4},{7,5},{8,14},{9,15},{10,... | collective-permute-start | bytes 589832 | tf_op jit(solution)/shard_map/ppermute | solution.py:25
  21.5 30.9 %collective-permute-start.13 = (bf16[128,768]{1,0:T(8,128)(2,1)}, bf16[128,768]{1,0:T(8,128)(2,1)S(1)}, u32[]{:S(2)}, u32[]{:S(2)}) collective-permute-start(bf16[128,768]{1,0:T(8,128)(2,1)} %get-tuple-element.25), channel_id=1, source_target_pairs={{0,7},{1,0},{2,1},{3,2},{4,3},{5,4},{6,5},{7,6},{8,15},{9,8},{10,9... | collective-permute-start | bytes 589832 | tf_op jit(solution)/shard_map/ppermute | solution.py:25
  22.3 30.2 %collective-permute-start.7 = (bf16[128,768]{1,0:T(8,128)(2,1)}, bf16[128,768]{1,0:T(8,128)(2,1)S(1)}, u32[]{:S(2)}, u32[]{:S(2)}) collective-permute-start(bf16[128,768]{1,0:T(8,128)(2,1)} %get-tuple-element.19), channel_id=1, source_target_pairs={{0,1},{1,2},{2,3},{3,4},{4,5},{5,6},{6,7},{7,0},{8,9},{9,10},{10,1... | collective-permute-start | bytes 589832 | tf_op jit(solution)/shard_map/ppermute | solution.py:25
  23.1 32.2 %copy-start.10 = (bf16[128,768]{1,0:T(8,128)(2,1)}, bf16[128,768]{1,0:T(8,128)(2,1)S(1)}, u32[]{:S(2)}) copy-start(bf16[128,768]{1,0:T(8,128)(2,1)S(1)} %collective-permute-done.10.refs_4_) | copy-start | bytes 589828
  23.1 29.4 %collective-permute-start.8 = (bf16[128,768]{1,0:T(8,128)(2,1)}, bf16[128,768]{1,0:T(8,128)(2,1)S(1)}, u32[]{:S(2)}, u32[]{:S(2)}) collective-permute-start(bf16[128,768]{1,0:T(8,128)(2,1)} %get-tuple-element.20), channel_id=1, source_target_pairs={{0,2},{1,3},{2,4},{3,5},{4,6},{5,7},{6,0},{7,1},{8,10},{9,11},{10,... | collective-permute-start | bytes 589832 | tf_op jit(solution)/shard_map/ppermute | solution.py:25
  40.4 14.9 %copy-start.11 = (bf16[128,768]{1,0:T(8,128)(2,1)}, bf16[128,768]{1,0:T(8,128)(2,1)S(1)}, u32[]{:S(2)}) copy-start(bf16[128,768]{1,0:T(8,128)(2,1)S(1)} %collective-permute-done.11.refs_5_) | copy-start | bytes 589828
  40.4 14.9 %collective-permute-start.9 = (bf16[128,768]{1,0:T(8,128)(2,1)}, bf16[128,768]{1,0:T(8,128)(2,1)S(1)}, u32[]{:S(2)}, u32[]{:S(2)}) collective-permute-start(bf16[128,768]{1,0:T(8,128)(2,1)} %get-tuple-element.21), channel_id=1, source_target_pairs={{0,3},{1,4},{2,5},{3,6},{4,7},{5,0},{6,1},{7,2},{8,11},{9,12},{10,... | collective-permute-start | bytes 589832 | tf_op jit(solution)/shard_map/ppermute | solution.py:25
  48.7 6.6 %copy-start.12 = (bf16[128,768]{1,0:T(8,128)(2,1)}, bf16[128,768]{1,0:T(8,128)(2,1)S(1)}, u32[]{:S(2)}) copy-start(bf16[128,768]{1,0:T(8,128)(2,1)S(1)} %collective-permute-done.12.refs_6_) | copy-start | bytes 589828
  52.5 2.8 %copy-start.13 = (bf16[128,768]{1,0:T(8,128)(2,1)}, bf16[128,768]{1,0:T(8,128)(2,1)S(1)}, u32[]{:S(2)}) copy-start(bf16[128,768]{1,0:T(8,128)(2,1)S(1)} %collective-permute-done.13.refs_7_) | copy-start | bytes 589828
  52.5 2.8 %copy-start.14 = (bf16[128,768]{1,0:T(8,128)(2,1)}, bf16[128,768]{1,0:T(8,128)(2,1)S(1)}, u32[]{:S(2)}) copy-start(bf16[128,768]{1,0:T(8,128)(2,1)S(1)} %collective-permute-done.7.refs_1_) | copy-start | bytes 589828
  52.5 2.8 %copy-start.15 = (bf16[128,768]{1,0:T(8,128)(2,1)}, bf16[128,768]{1,0:T(8,128)(2,1)S(1)}, u32[]{:S(2)}) copy-start(bf16[128,768]{1,0:T(8,128)(2,1)S(1)} %collective-permute-done.8.refs_2_) | copy-start | bytes 589828
  55.3 0.7 copy-start.16
  61.3 17.4 %all-to-all-start = ((bf16[32,4,1152]{2,1,0:T(4,128)(2,1)}), bf16[32,4,1152]{2,1,0:T(4,128)(2,1)S(1)}, u32[]{:S(2)}, u32[]{:S(2)}) async-start(bf16[32,4,1152]{2,1,0:T(4,128)(2,1)} %pad_maximum_fusion), calls=%async_computation | async-start | bytes 589824 | tf_op jit(solution)/shard_map/all_to_all | solution.py:86
  83.4 14.0 %all-to-all-start.1 = ((bf16[32,4,1024]{2,1,0:T(4,128)(2,1)}), bf16[32,4,1024]{2,1,0:T(4,128)(2,1)S(1)}, u32[]{:S(2)}, u32[]{:S(2)}) async-start(bf16[32,4,1024]{2,1,0:T(4,128)(2,1)} %reshape.150), calls=%async_computation.1 | async-start | bytes 524288 | tf_op jit(solution)/shard_map/all_to_all | solution.py:95
  87.2 14.9 %collective-permute-start.14 = (bf16[256,512]{1,0:T(8,128)(2,1)}, bf16[256,512]{1,0:T(8,128)(2,1)S(1)}, u32[]{:S(2)}, u32[]{:S(2)}) collective-permute-start(bf16[256,512]{1,0:T(8,128)(2,1)} %get-tuple-element.26.refs_0_), channel_id=1, source_target_pairs={{0,1},{1,2},{2,3},{3,4},{4,5},{5,6},{6,7},{7,0},{8,9},{9,10},{10,1... | collective-permute-start | bytes 786440 | tf_op jit(solution)/shard_map/ppermute | solution.py:25
  97.5 55.2 %copy-start.9 = (bf16[32,4,1024]{2,0,1:T(8,128)(2,1)}, bf16[32,4,1024]{2,0,1:T(8,128)(2,1)S(1)}, u32[]{:S(2)}) copy-start(bf16[32,4,1024]{2,0,1:T(8,128)(2,1)S(1)} %copy.18) | copy-start | bytes 786436
  97.5 9.4 %collective-permute-start = (bf16[4,32,1024]{2,1,0:T(8,128)(2,1)S(1)}, bf16[4,32,1024]{2,1,0:T(8,128)(2,1)S(1)}, u32[]{:S(2)}, u32[]{:S(2)}) collective-permute-start(bf16[4,32,1024]{2,1,0:T(8,128)(2,1)S(1)} %bitcast.34), channel_id=1, source_target_pairs={{0,1},{1,2},{2,3},{3,4},{4,5},{5,6},{8,9},{9,10},{10,11},{11,12},{... | collective-permute-start | bytes 786440 | tf_op jit(solution)/shard_map/ppermute | solution.py:25
  101.7 7.5 %collective-permute-start.18 = (bf16[256,512]{1,0:T(8,128)(2,1)}, bf16[256,512]{1,0:T(8,128)(2,1)S(1)}, u32[]{:S(2)}, u32[]{:S(2)}) collective-permute-start(bf16[256,512]{1,0:T(8,128)(2,1)} %get-tuple-element.26.refs_0_), channel_id=1, source_target_pairs={{0,7},{1,0},{2,1},{3,2},{4,3},{5,4},{6,5},{7,6},{8,15},{9,8},{10,9... | collective-permute-start | bytes 786440 | tf_op jit(solution)/shard_map/ppermute | solution.py:25
  102.1 32.9 %copy-start.2 = (bf16[256,512]{1,0:T(8,128)(2,1)}, bf16[256,512]{1,0:T(8,128)(2,1)S(1)}, u32[]{:S(2)}) copy-start(bf16[256,512]{1,0:T(8,128)(2,1)S(1)} %collective-permute-done.14.refs_1_) | copy-start | bytes 786436
  102.1 9.9 %collective-permute-start.15 = (bf16[256,512]{1,0:T(8,128)(2,1)S(1)}, bf16[256,512]{1,0:T(8,128)(2,1)S(1)}, u32[]{:S(2)}, u32[]{:S(2)}) collective-permute-start(bf16[256,512]{1,0:T(8,128)(2,1)S(1)} %collective-permute-done.14.refs_1_), channel_id=1, source_target_pairs={{0,1},{1,2},{2,3},{3,4},{4,5},{5,6},{6,7},{7,0},{8,9},{9,10},{10,1... | collective-permute-start | bytes 786440 | tf_op jit(solution)/shard_map/ppermute | solution.py:25
  103.4 11.5 %collective-permute-start.1 = (bf16[4,32,1024]{2,1,0:T(8,128)(2,1)S(1)}, bf16[4,32,1024]{2,1,0:T(8,128)(2,1)S(1)}, u32[]{:S(2)}, u32[]{:S(2)}) collective-permute-start(bf16[4,32,1024]{2,1,0:T(8,128)(2,1)S(1)} %bitcast.35), channel_id=1, source_target_pairs={{0,7},{1,0},{2,1},{3,2},{4,3},{5,4},{8,15},{9,8},{10,9},{11,10},{1... | collective-permute-start | bytes 786440 | tf_op jit(solution)/shard_map/ppermute | solution.py:25
  106.9 45.8 %copy-start.20 = (bf16[4,32,1024]{2,1,0:T(8,128)(2,1)}, bf16[4,32,1024]{2,1,0:T(8,128)(2,1)S(1)}, u32[]{:S(2)}) copy-start(bf16[4,32,1024]{2,1,0:T(8,128)(2,1)S(1)} %collective-permute-done.refs_1_) | copy-start | bytes 786436
  106.9 11.6 %collective-permute-start.2 = (bf16[4,32,1024]{2,1,0:T(8,128)(2,1)S(1)}, bf16[4,32,1024]{2,1,0:T(8,128)(2,1)S(1)}, u32[]{:S(2)}, u32[]{:S(2)}) collective-permute-start(bf16[4,32,1024]{2,1,0:T(8,128)(2,1)S(1)} %collective-permute-done.refs_1_), channel_id=1, source_target_pairs={{1,2},{2,3},{3,4},{4,5},{5,6},{6,7},{9,10},{10,11},{11,12},{12,13}... | collective-permute-start | bytes 786440 | tf_op jit(solution)/shard_map/ppermute | solution.py:25
  109.2 25.8 %copy-start.3 = (bf16[256,512]{1,0:T(8,128)(2,1)}, bf16[256,512]{1,0:T(8,128)(2,1)S(1)}, u32[]{:S(2)}) copy-start(bf16[256,512]{1,0:T(8,128)(2,1)S(1)} %collective-permute-done.18.refs_7_) | copy-start | bytes 786436
  109.2 11.3 %collective-permute-start.19 = (bf16[256,512]{1,0:T(8,128)(2,1)S(1)}, bf16[256,512]{1,0:T(8,128)(2,1)S(1)}, u32[]{:S(2)}, u32[]{:S(2)}) collective-permute-start(bf16[256,512]{1,0:T(8,128)(2,1)S(1)} %collective-permute-done.18.refs_7_), channel_id=1, source_target_pairs={{0,7},{1,0},{2,1},{3,2},{4,3},{5,4},{6,5},{7,6},{8,15},{9,8},{10,9... | collective-permute-start | bytes 786440 | tf_op jit(solution)/shard_map/ppermute | solution.py:25
  112.0 22.9 %copy-start.4 = (bf16[256,512]{1,0:T(8,128)(2,1)}, bf16[256,512]{1,0:T(8,128)(2,1)S(1)}, u32[]{:S(2)}) copy-start(bf16[256,512]{1,0:T(8,128)(2,1)S(1)} %collective-permute-done.15.refs_2_) | copy-start | bytes 786436
  112.0 11.2 %collective-permute-start.16 = (bf16[256,512]{1,0:T(8,128)(2,1)S(1)}, bf16[256,512]{1,0:T(8,128)(2,1)S(1)}, u32[]{:S(2)}, u32[]{:S(2)}) collective-permute-start(bf16[256,512]{1,0:T(8,128)(2,1)S(1)} %collective-permute-done.15.refs_2_), channel_id=1, source_target_pairs={{0,1},{1,2},{2,3},{3,4},{4,5},{5,6},{6,7},{7,0},{8,9},{9,10},{10,1... | collective-permute-start | bytes 786440 | tf_op jit(solution)/shard_map/ppermute | solution.py:25
  114.9 37.8 %copy-start.21 = (bf16[4,32,1024]{2,1,0:T(8,128)(2,1)}, bf16[4,32,1024]{2,1,0:T(8,128)(2,1)S(1)}, u32[]{:S(2)}) copy-start(bf16[4,32,1024]{2,1,0:T(8,128)(2,1)S(1)} %collective-permute-done.1.refs_2_) | copy-start | bytes 786436
  114.9 11.2 %collective-permute-start.3 = (bf16[4,32,1024]{2,1,0:T(8,128)(2,1)S(1)}, bf16[4,32,1024]{2,1,0:T(8,128)(2,1)}, u32[]{:S(2)}, u32[]{:S(2)}) collective-permute-start(bf16[4,32,1024]{2,1,0:T(8,128)(2,1)S(1)} %collective-permute-done.1.refs_2_), channel_id=1, source_target_pairs={{0,7},{1,0},{2,1},{3,2},{4,3},{7,6},{8,15},{9,8},{10,9},{11,10},{1... | collective-permute-start | bytes 786440 | tf_op jit(solution)/shard_map/ppermute | solution.py:25
  118.5 7.7 %copy-start.22 = (bf16[4,32,1024]{2,1,0:T(8,128)(2,1)}, bf16[4,32,1024]{2,1,0:T(8,128)(2,1)S(1)}, u32[]{:S(2)}) copy-start(bf16[4,32,1024]{2,1,0:T(8,128)(2,1)S(1)} %collective-permute-done.2.refs_3_) | copy-start | bytes 786436
  118.5 10.2 %collective-permute-start.4 = (bf16[4,32,1024]{2,1,0:T(8,128)(2,1)S(1)}, bf16[4,32,1024]{2,1,0:T(8,128)(2,1)}, u32[]{:S(2)}, u32[]{:S(2)}) collective-permute-start(bf16[4,32,1024]{2,1,0:T(8,128)(2,1)S(1)} %collective-permute-done.2.refs_3_), channel_id=1, source_target_pairs={{2,3},{3,4},{4,5},{5,6},{6,7},{7,0},{10,11},{11,12},{12,13},{13,14... | collective-permute-start | bytes 786440 | tf_op jit(solution)/shard_map/ppermute | solution.py:25
  120.6 14.4 %copy-start.5 = (bf16[256,512]{1,0:T(8,128)(2,1)}, bf16[256,512]{1,0:T(8,128)(2,1)S(1)}, u32[]{:S(2)}) copy-start(bf16[256,512]{1,0:T(8,128)(2,1)S(1)} %collective-permute-done.19.refs_6_) | copy-start | bytes 786436
  120.6 14.3 %collective-permute-start.20 = (bf16[256,512]{1,0:T(8,128)(2,1)S(1)}, bf16[256,512]{1,0:T(8,128)(2,1)S(1)}, u32[]{:S(2)}, u32[]{:S(2)}) collective-permute-start(bf16[256,512]{1,0:T(8,128)(2,1)S(1)} %collective-permute-done.19.refs_6_), channel_id=1, source_target_pairs={{0,7},{1,0},{2,1},{3,2},{4,3},{5,4},{6,5},{7,6},{8,15},{9,8},{10,9... | collective-permute-start | bytes 786440 | tf_op jit(solution)/shard_map/ppermute | solution.py:25
  123.3 11.7 %copy-start.6 = (bf16[256,512]{1,0:T(8,128)(2,1)}, bf16[256,512]{1,0:T(8,128)(2,1)S(1)}, u32[]{:S(2)}) copy-start(bf16[256,512]{1,0:T(8,128)(2,1)S(1)} %collective-permute-done.16.refs_3_) | copy-start | bytes 786436
  123.3 11.7 %collective-permute-start.17 = (bf16[256,512]{1,0:T(8,128)(2,1)S(1)}, bf16[256,512]{1,0:T(8,128)(2,1)S(1)}, u32[]{:S(2)}, u32[]{:S(2)}) collective-permute-start(bf16[256,512]{1,0:T(8,128)(2,1)S(1)} %collective-permute-done.16.refs_3_), channel_id=1, source_target_pairs={{0,1},{1,2},{2,3},{3,4},{4,5},{5,6},{6,7},{7,0},{8,9},{9,10},{10,1... | collective-permute-start | bytes 786440 | tf_op jit(solution)/shard_map/ppermute | solution.py:25
  126.2 14.8 %collective-permute-start.5 = (bf16[4,32,1024]{2,1,0:T(8,128)(2,1)}, bf16[4,32,1024]{2,1,0:T(8,128)(2,1)}, u32[]{:S(2)}, u32[]{:S(2)}) collective-permute-start(bf16[4,32,1024]{2,1,0:T(8,128)(2,1)} %collective-permute-done.3.refs_4_), channel_id=1, source_target_pairs={{0,7},{1,0},{2,1},{3,2},{6,5},{7,6},{8,15},{9,8},{10,9},{11,10},{1... | collective-permute-start | bytes 786440 | tf_op jit(solution)/shard_map/ppermute | solution.py:25
  128.7 12.3 %collective-permute-start.6 = (bf16[4,32,1024]{2,1,0:T(8,128)(2,1)}, bf16[4,32,1024]{2,1,0:T(8,128)(2,1)}, u32[]{:S(2)}, u32[]{:S(2)}) collective-permute-start(bf16[4,32,1024]{2,1,0:T(8,128)(2,1)} %collective-permute-done.4.refs_0_), channel_id=1, source_target_pairs={{0,1},{3,4},{4,5},{5,6},{6,7},{7,0},{8,9},{11,12},{12,13},{13,14},... | collective-permute-start | bytes 786440 | tf_op jit(solution)/shard_map/ppermute | solution.py:25
  134.9 0.7 copy-start.7
  134.9 0.8 copy-start.8
  152.7 26.6 %copy-start = (bf16[4,32,4096]{2,1,0:T(8,128)(2,1)S(1)}, bf16[4,32,4096]{2,1,0:T(8,128)(2,1)}, u32[]{:S(2)}) copy-start(bf16[4,32,4096]{2,1,0:T(8,128)(2,1)} %text_ref.1) | copy-start | bytes 3145732
  172.6 21.4 %all-to-all-start.2 = ((bf16[8,128,256]{2,1,0:T(8,128)(2,1)}), bf16[8,128,256]{2,1,0:T(8,128)(2,1)S(1)}, u32[]{:S(2)}, u32[]{:S(2)}) async-start(bf16[8,128,256]{2,1,0:T(8,128)(2,1)} %bitcast.31), calls=%async_computation.2 | async-start | bytes 1048576 | tf_op jit(solution)/shard_map/all_to_all | solution.py:492
  193.9 0.8 copy-start.1
Sparse Core Ops, SparseCore 0:
  9.9 55.2 all-gather.4
  67.7 79.1 all-gather.6

commit v2 on v1

--- a/solution.py
+++ b/solution.py
@@ -228,12 +228,10 @@
     )(mine.reshape(1), *chunks, cosine, sine, gain.reshape(parts, width), all_qkv)
 
 
-def image_kernel(*refs, groups, with_hidden):
+def image_kernel(*refs, groups):
     chunk_refs = refs[:groups]
     cos_ref, sin_ref, proj_ref, bias_ref, gain_ref, qkv_ref = refs[groups : groups + 6]
-    out_ref = refs[groups + 6]
-    hidden_ref = refs[groups + 7] if with_hidden else None
-    rows_ref, sum_ref, squares_ref = refs[-3:]
+    out_ref, hidden_ref, rows_ref, sum_ref, squares_ref = refs[groups + 6 :]
     tiles, local_rows, depth = chunk_refs[0].shape
     each = tiles * local_rows
     step = pl.program_id(0)
@@ -248,8 +246,7 @@
     projected = (
         jnp.dot(rows_ref[...], proj_ref[...], preferred_element_type=jnp.float32) + bias_ref[...]
     ).astype(jnp.bfloat16)
-    if with_hidden:
-        hidden_ref[...] = projected[:each]
+    hidden_ref[...] = projected[:each]
     wide = projected.astype(jnp.float32)
     squares_ref[...] += jnp.sum(wide * wide, axis=1, keepdims=True)
     scaled = (wide * gain_ref[...]).astype(jnp.bfloat16)
@@ -269,20 +266,23 @@
         rotate_store(sum_ref[...] * scale, cosine, sine, store)
 
 
-def image_qkv_of(chunks, cosine, sine, w_proj, bias, gain, all_qkv, with_hidden):
+def image_qkv_of(chunks, cosine, sine, w_proj, bias, gain, all_qkv):
     groups = len(chunks)
     tiles, local_rows, depth = chunks[0].shape
     model_width, outs = all_qkv.shape
     each = tiles * local_rows
-    block = 512
+    block = 1024
     fixed = lambda *shape: pl.BlockSpec(shape, lambda i: (0,) * len(shape))
-    out_specs = [fixed(groups, tiles, local_rows, outs)]
-    out_shape = [jax.ShapeDtypeStruct((groups, tiles, local_rows, outs), jnp.bfloat16)]
-    if with_hidden:
-        out_specs.append(pl.BlockSpec((each, block), lambda i: (0, i)))
-        out_shape.append(jax.ShapeDtypeStruct((each, model_width), jnp.bfloat16))
+    out_specs = [
+        fixed(groups, tiles, local_rows, outs),
+        pl.BlockSpec((each, block), lambda i: (0, i)),
+    ]
+    out_shape = [
+        jax.ShapeDtypeStruct((groups, tiles, local_rows, outs), jnp.bfloat16),
+        jax.ShapeDtypeStruct((each, model_width), jnp.bfloat16),
+    ]
     return pl.pallas_call(
-        functools.partial(image_kernel, groups=groups, with_hidden=with_hidden),
+        functools.partial(image_kernel, groups=groups),
         grid=(model_width // block,),
         in_specs=[fixed(tiles, local_rows, depth)] * groups
         + [
@@ -309,16 +309,15 @@
     )(*chunks, cosine, sine, w_proj, bias, gain, all_qkv)
 
 
-def attend_kernel(counts_ref, early_ref, late_ref, text_ref, out_ref, rows_ref, *, orders):
+def attend_kernel(counts_ref, image_ref, text_ref, out_ref, rows_ref, *, order):
     tile = pl.program_id(0)
     patch = counts_ref[0, tile]
     texts = counts_ref[1, tile]
     mine = counts_ref[2, 0]
     length = patch + texts
     parts, local_rows, outs = rows_ref.shape
-    for ref, order in zip((early_ref, late_ref), orders):
-        for at, s in enumerate(order):
-            rows_ref[lax.rem(mine + (parts - s), parts)] = ref[at, 0]
+    for at, s in enumerate(order):
+        rows_ref[lax.rem(mine + (parts - s), parts)] = image_ref[at, 0]
     rows = parts * local_rows
     row = lax.broadcasted_iota(jnp.int32, (rows, WINDOW), 0)
     place = lax.broadcasted_iota(jnp.int32, (rows, WINDOW), 1)
@@ -350,18 +349,16 @@
         )
 
 
-def attend(early, late, orders, text_qkv, counts):
-    tiles, local_rows, outs = early.shape[1:]
-    parts = early.shape[0] + late.shape[0]
+def attend(image_qkv, order, text_qkv, counts):
+    parts, tiles, local_rows, outs = image_qkv.shape
     rows = parts * local_rows
     return pl.pallas_call(
-        functools.partial(attend_kernel, orders=orders),
+        functools.partial(attend_kernel, order=order),
         grid_spec=pltpu.PrefetchScalarGridSpec(
             num_scalar_prefetch=1,
             grid=(tiles,),
             in_specs=[
-                pl.BlockSpec((early.shape[0], 1, local_rows, outs), lambda t, c: (0, t, 0, 0)),
-                pl.BlockSpec((late.shape[0], 1, local_rows, outs), lambda t, c: (0, t, 0, 0)),
+                pl.BlockSpec((parts, 1, local_rows, outs), lambda t, c: (0, t, 0, 0)),
                 pl.BlockSpec((WINDOW, outs), lambda t, c: (t, 0)),
             ],
             out_specs=pl.BlockSpec((parts, 1, local_rows, GROUP * HS), lambda t, c: (0, t, 0, 0)),
@@ -374,38 +371,48 @@
             bytes_accessed=4 * tiles * rows * outs,
             transcendentals=tiles * GROUP * rows * rows,
         ),
-    )(counts, early, late, text_qkv)
-
-
-def out_kernel(att_ref, weight_ref, hidden_ref, out_ref, rows_ref):
+    )(counts, image_qkv, text_qkv)
+
+
+def out_kernel(att_ref, weight_hbm, hidden_ref, out_ref, rows_ref, weight_ref, sems):
     heads, _, head_width = att_ref.shape
-
-    @pl.when(pl.program_id(0) == 0)
-    def _():
-        for h in range(heads):
-            rows_ref[:, h * head_width : (h + 1) * head_width] = att_ref[h]
-
-    weights = jnp.concatenate([weight_ref[j] for j in range(weight_ref.shape[0])], axis=1)
-    total = jnp.dot(rows_ref[...], weights, preferred_element_type=jnp.float32)
-    out_ref[...] = (hidden_ref[...].astype(jnp.float32) + total).astype(jnp.bfloat16)
+    blocks, _, width = weight_ref.shape
+    pieces = sems.shape[0]
+    each = blocks // pieces
+    copies = [
+        pltpu.make_async_copy(
+            weight_hbm.at[i * each : (i + 1) * each],
+            weight_ref.at[i * each : (i + 1) * each],
+            sems.at[i],
+        )
+        for i in range(pieces)
+    ]
+    for copy in copies:
+        copy.start()
+    for h in range(heads):
+        rows_ref[:, h * head_width : (h + 1) * head_width] = att_ref[h]
+    for i, copy in enumerate(copies):
+        copy.wait()
+        weights = jnp.concatenate([weight_ref[i * each + j] for j in range(each)], axis=1)
+        total = jnp.dot(rows_ref[...], weights, preferred_element_type=jnp.float32)
+        cols = slice(i * each * width, (i + 1) * each * width)
+        out_ref[:, cols] = (hidden_ref[:, cols].astype(jnp.float32) + total).astype(jnp.bfloat16)
 
 
 def project_out(attended, weight_blocks, hidden):
-    heads, rows, head_width = attended.shape
+    _, rows, _ = attended.shape
     blocks, depth, width = weight_blocks.shape
-    step = 4
+    whole = pl.BlockSpec(memory_space=pltpu.VMEM)
     return pl.pallas_call(
         out_kernel,
-        grid=(blocks // step,),
-        in_specs=[
-            pl.BlockSpec((heads, rows, head_width), lambda i: (0, 0, 0)),
-            pl.BlockSpec((step, depth, width), lambda i: (i, 0, 0)),
-            pl.BlockSpec((rows, step * width), lambda i: (0, i)),
+        in_specs=[whole, pl.BlockSpec(memory_space=pl.ANY), whole],
+        out_specs=whole,
+        out_shape=jax.ShapeDtypeStruct((rows, blocks * width), jnp.bfloat16),
+        scratch_shapes=[
+            pltpu.VMEM((rows, depth), jnp.bfloat16),
+            pltpu.VMEM((blocks, depth, width), jnp.bfloat16),
+            pltpu.SemaphoreType.DMA((blocks // 4,)),
         ],
-        out_specs=pl.BlockSpec((rows, step * width), lambda i: (0, i)),
-        out_shape=jax.ShapeDtypeStruct((rows, blocks * width), jnp.bfloat16),
-        scratch_shapes=[pltpu.VMEM((rows, depth), jnp.bfloat16)],
-        compiler_params=pltpu.CompilerParams(dimension_semantics=("arbitrary",)),
         cost_estimate=pl.CostEstimate(
             flops=2 * rows * depth * blocks * width,
             bytes_accessed=2 * depth * blocks * width,
@@ -448,34 +455,14 @@
 
     text_places = patch_counts[:, None] + jnp.arange(WINDOW, dtype=jnp.int32)[None, :]
     text_cos, text_sin = rotation_tables(text_places.reshape(-1))
-    half = parts // 2
-    near = [0] + [s for k in range(1, half - 1) for s in (k, parts - k)]
-    far = [half - 1, half + 1, half]
-    orders = (tuple(near), tuple(far))
+    order = (0, *[s for k in range(1, parts // 2) for s in (k, parts - k)], parts // 2)
     local = jnp.arange(local_rows, dtype=jnp.int32)
-    begins = jnp.stack([lax.rem(mine + (parts - s), parts) * local_rows for s in near + far])
+    begins = jnp.stack([lax.rem(mine + (parts - s), parts) * local_rows for s in order])
     chunk_cos, chunk_sin = rotation_tables(begins[:, None] + local[None, :])
 
     bias = b_proj.reshape(1, model_width)
-    early, own_projected = image_qkv_of(
-        [chunks[s] for s in near],
-        chunk_cos[: len(near)],
-        chunk_sin[: len(near)],
-        w_proj,
-        bias,
-        norm_gain,
-        all_qkv,
-        True,
-    )
-    (late,) = image_qkv_of(
-        [chunks[s] for s in far],
-        chunk_cos[len(near) :],
-        chunk_sin[len(near) :],
-        w_proj,
-        bias,
-        norm_gain,
-        all_qkv,
-        False,
+    image_qkv, own_projected = image_qkv_of(
+        [chunks[s] for s in order], chunk_cos, chunk_sin, w_proj, bias, norm_gain, all_qkv
     )
     text_qkv = text_qkv_of(text_chunks, mine, text_cos, text_sin, norm_gain, all_qkv)
 
@@ -488,7 +475,7 @@
         ),
     ).reshape(each, model_width)
 
-    attended = attend(early, late, orders, text_qkv, counts)
+    attended = attend(image_qkv, order, text_qkv, counts)
     returned = lax.all_to_all(
         attended.reshape(parts, each, -1), "mp", split_axis=0, concat_axis=0, tiled=True
     )

time: 215 us -> 207 us (0.963)
  blocking collectives: 0 us -> 17.2 us
  Pallas kernels: 55 us -> 45.8 us
  waiting for transfers between devices: 56 us -> 48.7 us
  starting transfers between devices: 70.8 us -> 64.8 us
    all_to_all x0 -> x1, blocking collectives: none -> 17.2 us  [exchange_tiles(): got = lax.all_to_all(sent, 'dp', split_axis=0, concat_axis=0, tiled=True)]
    pallas_call x4 -> x3, Pallas kernels: 42.6 us -> 33.4 us  [the longest x1 18.8 us: image_qkv_of(): pl.pallas_call(functools.partial(image_kernel, groups=groups), grid=(mode...]
    all_to_all x1 -> x0, waiting for transfers between devices: 9.19 us -> none  [exchange_tiles(): got = lax.all_to_all(sent, 'dp', split_axis=0, concat_axis=0, tiled=True)]
    all_to_all x1 -> x0, starting transfers between devices: 8.1 us -> none  [exchange_tiles(): got = lax.all_to_all(sent, 'dp', split_axis=0, concat_axis=0, tiled=True)]
    all_to_all x1, waiting for transfers between devices: 12.2 us -> 14.5 us  [body(): lax.all_to_all(attended.reshape(parts, each, -1), 'mp', split_axis=0, con...]
  transfers between devices with their start and end apart: 26 -> 25, of which waited for: 12 -> 9; matrix products, arithmetic and copies ran while one was open for 7% -> 6% of each run, Pallas kernels for 21% -> 18%
where the time goes in v2:
time: 207 us; the launch traced here: 206 us
  starting transfers between devices  64.8 us (31%)
  waiting for transfers between devices  48.7 us (24%)
  Pallas kernels  45.8 us (22%)
  blocking collectives  17.2 us (8%)
  between operations  13.8 us (7%)
  other arithmetic  8.15 us (4%)
  local copies, waits for them, and re-layouts  7.43 us (4%)
    ppermute x21, starting transfers between devices, shifted(): return lax.ppermute(value, axis, pairs)  53.4 us
    ppermute x21, waiting for transfers between devices, shifted(): return lax.ppermute(value, axis, pairs)  24.8 us
    pallas_call x1, Pallas kernels, image_qkv_of(): pl.pallas_call(functools.partial(image_kernel, groups=groups), grid=(mode...  18.8 us
    all_to_all x1, blocking collectives, exchange_tiles(): got = lax.all_to_all(sent, 'dp', split_axis=0, concat_axis=0, tiled=True)  17.2 us
    all_to_all x1, waiting for transfers between devices, body(): lax.all_to_all(attended.reshape(parts, each, -1), 'mp', split_axis=0, con...  14.5 us
    pallas_call x1, Pallas kernels, project_out(): pl.pallas_call(out_kernel, in_specs=[whole, pl.BlockSpec(memory_space=pl....  8.73 us
    all_to_all x1, waiting for transfers between devices, exchange_tiles(): lax.all_to_all(ordered.reshape(ranks, image_count, width), 'dp', split_ax...  8.66 us
    all_to_all x1, starting transfers between devices, body(): lax.all_to_all(attended.reshape(parts, each, -1), 'mp', split_axis=0, con...  7.72 us
  transfers between devices with their start and end apart: 25, of which 9 were waited for; matrix products, arithmetic and copies ran while one was open for 6% of the time, Pallas kernels for 18%

profile of v2, /device:TPU:1, one launch (start us, length us, event | category | flops | bytes accessed | tf_op | source)
XLA Modules:
  0.0 205.9 jit_solution(6131969830256043402)
XLA Ops:
  6.5 0.7 all-gather.5.cloned.1.call-update
  7.3 2.5 %shard_map.102 = (bf16[128,768]{1,0:T(8,128)(2,1)}, bf16[128,768]{1,0:T(8,128)(2,1)}, bf16[128,768]{1,0:T(8,128)(2,1)}, bf16[128,768]{1,0:T(8,128)(2,1)}, bf16[1...) custom-call(s32[1]{0:T(128)} %bitcast.21.place_ref, ...), custom_call_target="tpu_custom_call" | custom-call | flops 1048576 | bytes 3145728 | tf_op jit(solution)/shard_map/pallas_call | solution.py:127
  9.8 7.7 %collective-permute-start.10 = (bf16[128,768]{1,0:T(8,128)(2,1)}, bf16[128,768]{1,0:T(8,128)(2,1)S(1)}, u32[]{:S(2)}, u32[]{:S(2)}) collective-permute-start(bf16[128,768]{1,0:T(8,128)(2,1)} %get-tuple-element.22), channel_id=1, source_target_pairs={{0,4},{1,5},{2,6},{3,7},{4,0},{5,1},{6,2},{7,3},{8,12},{9,13},{10,... | collective-permute-start | bytes 589832 | tf_op jit(solution)/shard_map/ppermute | solution.py:25
  17.5 4.0 %collective-permute-start.12 = (bf16[128,768]{1,0:T(8,128)(2,1)}, bf16[128,768]{1,0:T(8,128)(2,1)S(1)}, u32[]{:S(2)}, u32[]{:S(2)}) collective-permute-start(bf16[128,768]{1,0:T(8,128)(2,1)} %get-tuple-element.24), channel_id=1, source_target_pairs={{0,6},{1,7},{2,0},{3,1},{4,2},{5,3},{6,4},{7,5},{8,14},{9,15},{10,... | collective-permute-start | bytes 589832 | tf_op jit(solution)/shard_map/ppermute | solution.py:25
  21.5 0.7 collective-permute-start.13
  22.3 0.7 collective-permute-start.7
  23.0 0.1 pad.12.clone
  23.1 5.0 %collective-permute-start.8 = (bf16[128,768]{1,0:T(8,128)(2,1)}, bf16[128,768]{1,0:T(8,128)(2,1)S(1)}, u32[]{:S(2)}, u32[]{:S(2)}) collective-permute-start(bf16[128,768]{1,0:T(8,128)(2,1)} %get-tuple-element.20), channel_id=1, source_target_pairs={{0,2},{1,3},{2,4},{3,5},{4,6},{5,7},{6,0},{7,1},{8,10},{9,11},{10,... | collective-permute-start | bytes 589832 | tf_op jit(solution)/shard_map/ppermute | solution.py:25
  28.1 12.2 %collective-permute-done.11.refs_5_ = bf16[128,768]{1,0:T(8,128)(2,1)S(1)} collective-permute-done((bf16[128,768]{1,0:T(8,128)(2,1)}, bf16[128,768]{1,0:T(8,128)(2,1)S(1)}, u32[]{:S(2)}, u32[]{:S(2)}) %collective-permute-start.11) | collective-permute-done | bytes 196640 | tf_op jit(solution)/shard_map/ppermute | solution.py:25
  40.4 5.3 %collective-permute-start.9 = (bf16[128,768]{1,0:T(8,128)(2,1)}, bf16[128,768]{1,0:T(8,128)(2,1)S(1)}, u32[]{:S(2)}, u32[]{:S(2)}) collective-permute-start(bf16[128,768]{1,0:T(8,128)(2,1)} %get-tuple-element.21), channel_id=1, source_target_pairs={{0,3},{1,4},{2,5},{3,6},{4,7},{5,0},{6,1},{7,2},{8,11},{9,12},{10,... | collective-permute-start | bytes 589832 | tf_op jit(solution)/shard_map/ppermute | solution.py:25
  45.6 1.3 add_add_fusion.counts_ref
  46.9 1.8 collective-permute-done.12.refs_6_
  48.7 3.8 %collective-permute-done.13.refs_7_ = bf16[128,768]{1,0:T(8,128)(2,1)S(1)} collective-permute-done((bf16[128,768]{1,0:T(8,128)(2,1)}, bf16[128,768]{1,0:T(8,128)(2,1)S(1)}, u32[]{:S(2)}, u32[]{:S(2)}) %collective-permute-start.13) | collective-permute-done | bytes 196640 | tf_op jit(solution)/shard_map/ppermute | solution.py:25
  52.5 2.8 %collective-permute-done.9.refs_3_ = bf16[128,768]{1,0:T(8,128)(2,1)S(1)} collective-permute-done((bf16[128,768]{1,0:T(8,128)(2,1)}, bf16[128,768]{1,0:T(8,128)(2,1)S(1)}, u32[]{:S(2)}, u32[]{:S(2)}) %collective-permute-start.9) | collective-permute-done | bytes 196640 | tf_op jit(solution)/shard_map/ppermute | solution.py:25
  55.3 0.6 copy-done.16
  56.0 2.6 %shard_map.103 = (bf16[256,512]{1,0:T(8,128)(2,1)}, bf16[2048,128]{1,0:T(8,128)(2,1)}) custom-call(s32[3,4]{1,0:T(4,128)} %add_add_fusion.counts_ref, bf16[128,768]{1,0:T(8,128)(2,1)} %get-tuple-element.18.refs_0_, bf16[128,768]{1,0:T(8,128)(2,1)} %copy-done.14, bf16[128,768]{1,0:T(8,128)(2,1)} %copy-done.15, bf16[128,768]{1,0:T(8,128)(2,1)} %copy-done.16, ...), custom_call_target="tpu_custom_call" | custom-call | flops 67108864 | bytes 1572864 | tf_op jit(solution)/shard_map/pallas_call | solution.py:171
  58.6 1.2 copy.19
  59.8 0.7 convert_element_type.20
  60.4 0.1 broadcast_in_dim.16
  60.5 0.1 pad_maximum_fusion
  60.6 17.2 %all_to_all.15 = bf16[32,4,1152]{2,1,0:T(4,128)(2,1)S(1)} all-to-all(bf16[32,4,1152]{2,1,0:T(4,128)(2,1)S(1)} %pad_maximum_fusion), channel_id=1, replica_groups=mesh['dp'=32,'mp'=8] {'dp'}, dimensions={0} | all-to-all | bytes 589824 | tf_op jit(solution)/shard_map/all_to_all | solution.py:86
  77.8 0.8 reshape.149.got_ref
  78.6 2.1 %shard_map.100 = bf16[128,1024]{1,0:T(8,128)(2,1)} custom-call(bf16[128,1152]{1,0:T(8,128)(2,1)} %reshape.149.got_ref), custom_call_target="tpu_custom_call" | custom-call | flops 33554432 | bytes 524288 | tf_op jit(solution)/shard_map/pallas_call | solution.py:88
  80.7 1.8 reshape.150
  82.5 3.7 %all-to-all-start.1 = ((bf16[32,4,1024]{2,1,0:T(4,128)(2,1)}), bf16[32,4,1024]{2,1,0:T(4,128)(2,1)S(1)}, u32[]{:S(2)}, u32[]{:S(2)}) async-start(bf16[32,4,1024]{2,1,0:T(4,128)(2,1)} %reshape.150), calls=%async_computation.1 | async-start | bytes 524288 | tf_op jit(solution)/shard_map/all_to_all | solution.py:95
  86.2 0.1 stack.47
  86.3 2.3 %collective-permute-start.14 = (bf16[256,512]{1,0:T(8,128)(2,1)}, bf16[256,512]{1,0:T(8,128)(2,1)S(1)}, u32[]{:S(2)}, u32[]{:S(2)}) collective-permute-start(bf16[256,512]{1,0:T(8,128)(2,1)} %get-tuple-element.26.refs_0_), channel_id=1, source_target_pairs={{0,1},{1,2},{2,3},{3,4},{4,5},{5,6},{6,7},{7,0},{8,9},{9,10},{10,1... | collective-permute-start | bytes 786440 | tf_op jit(solution)/shard_map/ppermute | solution.py:25
  88.6 8.7 %all-to-all-done.1 = bf16[32,4,1024]{2,1,0:T(4,128)(2,1)S(1)} async-done(((bf16[32,4,1024]{2,1,0:T(4,128)(2,1)}), bf16[32,4,1024]{2,1,0:T(4,128)(2,1)S(1)}, u32[]{:S(2)}, u32[]{:S(2)}) %all-to-all-start.1) | async-done | bytes 262176 | tf_op jit(solution)/shard_map/all_to_all | solution.py:95
  97.3 0.1 copy.18
  97.4 3.3 %collective-permute-start = (bf16[4,32,1024]{2,1,0:T(8,128)(2,1)S(1)}, bf16[4,32,1024]{2,1,0:T(8,128)(2,1)S(1)}, u32[]{:S(2)}, u32[]{:S(2)}) collective-permute-start(bf16[4,32,1024]{2,1,0:T(8,128)(2,1)S(1)} %bitcast.33), channel_id=1, source_target_pairs={{0,1},{1,2},{2,3},{3,4},{4,5},{5,6},{8,9},{9,10},{10,11},{11,12},{... | collective-permute-start | bytes 786440 | tf_op jit(solution)/shard_map/ppermute | solution.py:25
  100.7 0.6 collective-permute-start.18
  101.3 0.9 collective-permute-start.15
  102.2 0.5 fusion.1
  102.8 3.7 %collective-permute-start.1 = (bf16[4,32,1024]{2,1,0:T(8,128)(2,1)S(1)}, bf16[4,32,1024]{2,1,0:T(8,128)(2,1)S(1)}, u32[]{:S(2)}, u32[]{:S(2)}) collective-permute-start(bf16[4,32,1024]{2,1,0:T(8,128)(2,1)S(1)} %bitcast.34), channel_id=1, source_target_pairs={{0,7},{1,0},{2,1},{3,2},{4,3},{5,4},{8,15},{9,8},{10,9},{11,10},{1... | collective-permute-start | bytes 786440 | tf_op jit(solution)/shard_map/ppermute | solution.py:25
  106.5 0.7 collective-permute-start.2
  107.3 0.1 convert_element_type.23
  107.3 1.1 collective-permute-done.18.refs_7_
  108.4 2.3 %collective-permute-start.19 = (bf16[256,512]{1,0:T(8,128)(2,1)S(1)}, bf16[256,512]{1,0:T(8,128)(2,1)S(1)}, u32[]{:S(2)}, u32[]{:S(2)}) collective-permute-start(bf16[256,512]{1,0:T(8,128)(2,1)S(1)} %collective-permute-done.18.refs_7_), channel_id=1, source_target_pairs={{0,7},{1,0},{2,1},{3,2},{4,3},{5,4},{6,5},{7,6},{8,15},{9,8},{10,9... | collective-permute-start | bytes 786440 | tf_op jit(solution)/shard_map/ppermute | solution.py:25
  110.7 1.1 collective-permute-done.15.refs_2_
  111.8 2.3 %collective-permute-start.16 = (bf16[256,512]{1,0:T(8,128)(2,1)S(1)}, bf16[256,512]{1,0:T(8,128)(2,1)S(1)}, u32[]{:S(2)}, u32[]{:S(2)}) collective-permute-start(bf16[256,512]{1,0:T(8,128)(2,1)S(1)} %collective-permute-done.15.refs_2_), channel_id=1, source_target_pairs={{0,1},{1,2},{2,3},{3,4},{4,5},{5,6},{6,7},{7,0},{8,9},{9,10},{10,1... | collective-permute-start | bytes 786440 | tf_op jit(solution)/shard_map/ppermute | solution.py:25
  114.1 0.5 fusion
  114.6 3.7 %collective-permute-start.3 = (bf16[4,32,1024]{2,1,0:T(8,128)(2,1)S(1)}, bf16[4,32,1024]{2,1,0:T(8,128)(2,1)}, u32[]{:S(2)}, u32[]{:S(2)}) collective-permute-start(bf16[4,32,1024]{2,1,0:T(8,128)(2,1)S(1)} %collective-permute-done.1.refs_2_), channel_id=1, source_target_pairs={{0,7},{1,0},{2,1},{3,2},{4,3},{7,6},{8,15},{9,8},{10,9},{11,10},{1... | collective-permute-start | bytes 786440 | tf_op jit(solution)/shard_map/ppermute | solution.py:25
  118.4 1.3 collective-permute-start.4
  119.8 3.3 %collective-permute-start.20 = (bf16[256,512]{1,0:T(8,128)(2,1)S(1)}, bf16[256,512]{1,0:T(8,128)(2,1)S(1)}, u32[]{:S(2)}, u32[]{:S(2)}) collective-permute-start(bf16[256,512]{1,0:T(8,128)(2,1)S(1)} %collective-permute-done.19.refs_6_), channel_id=1, source_target_pairs={{0,7},{1,0},{2,1},{3,2},{4,3},{5,4},{6,5},{7,6},{8,15},{9,8},{10,9... | collective-permute-start | bytes 786440 | tf_op jit(solution)/shard_map/ppermute | solution.py:25
  123.1 0.2 collective-permute-start.17
  123.3 0.1 broadcast_compare_fusion.1
  123.4 2.0 collective-permute-done.3.refs_4_
  125.4 3.2 %collective-permute-start.5 = (bf16[4,32,1024]{2,1,0:T(8,128)(2,1)}, bf16[4,32,1024]{2,1,0:T(8,128)(2,1)}, u32[]{:S(2)}, u32[]{:S(2)}) collective-permute-start(bf16[4,32,1024]{2,1,0:T(8,128)(2,1)} %collective-permute-done.3.refs_4_), channel_id=1, source_target_pairs={{0,7},{1,0},{2,1},{3,2},{6,5},{7,6},{8,15},{9,8},{10,9},{11,10},{1... | collective-permute-start | bytes 786440 | tf_op jit(solution)/shard_map/ppermute | solution.py:25
  128.6 2.1 %collective-permute-start.6 = (bf16[4,32,1024]{2,1,0:T(8,128)(2,1)}, bf16[4,32,1024]{2,1,0:T(8,128)(2,1)}, u32[]{:S(2)}, u32[]{:S(2)}) collective-permute-start(bf16[4,32,1024]{2,1,0:T(8,128)(2,1)} %collective-permute-done.4.refs_5_), channel_id=1, source_target_pairs={{0,1},{3,4},{4,5},{5,6},{6,7},{7,0},{8,9},{11,12},{12,13},{13,14},... | collective-permute-start | bytes 786440 | tf_op jit(solution)/shard_map/ppermute | solution.py:25
  130.7 0.8 pad_maximum_fusion.3
  131.5 0.5 broadcast.108
  132.0 0.7 reduce.3
  132.7 0.6 reshape.153.refs_10_
  133.3 0.8 pad_maximum_fusion.1
  134.2 0.6 copy-done.7
  134.8 0.1 copy-done.8
  134.9 5.2 %shard_map.104.text_ref = bf16[256,512]{1,0:T(8,128)(2,1)} custom-call(s32[1]{0:T(128)} %bitcast.21.place_ref, bf16[256,512]{1,0:T(8,128)(2,1)} %get-tuple-element.26.refs_0_, bf16[256,512]{1,0:T(8,128)(2,1)} %copy-done.2, bf16[256,512]{1,0:T(8,128)(2,1)} %copy-done.4, bf16[256,512]{1,0:T(8,128)(2,1)} %copy-done.6, bf16[256,512]{1,0:T(8,128)(2,1)} %copy-done.8, ...), custom_call_target="tpu_custom_call" | custom-call | flops 1073741824 | bytes 6291456 | tf_op jit(solution)/shard_map/pallas_call | solution.py:218
  140.3 18.8 %shard_map.101 = (bf16[8,4,32,512]{3,2,1,0:T(8,128)(2,1)}, bf16[128,4096]{1,0:T(8,128)(2,1)}) custom-call(bf16[4,32,1024]{2,1,0:T(8,128)(2,1)} %bitcast.35, bf16[4,32,1024]{2,1,0:T(8,128)(2,1)} %copy-done.20, bf16[4,32,1024]{2,1,0:T(8,128)(2,1)} %copy-done.21, bf16[4,32,1024]{2,1,0:T(8,128)(2,1)} %copy-done.22, ...), custom_call_target="tpu_custom_call" | custom-call | flops 12884901888 | bytes 12582912 | tf_op jit(solution)/shard_map/pallas_call | solution.py:284
  159.0 5.9 %shard_map.105 = bf16[8,4,32,256]{3,2,1,0:T(8,128)(2,1)} custom-call(s32[3,4]{1,0:T(4,128)} %add_add_fusion.counts_ref, bf16[8,4,32,512]{3,2,1,0:T(8,128)(2,1)} %get-tuple-element.17.image_ref, bf16[256,512]{1,0:T(8,128)(2,1)} %shard_map.104.text_ref), custom_call_target="tpu_custom_call" | custom-call | flops 335544320 | bytes 2097152 | tf_op jit(solution)/shard_map/pallas_call | solution.py:355
  164.9 7.7 %all-to-all-start.2 = ((bf16[8,128,256]{2,1,0:T(8,128)(2,1)}), bf16[8,128,256]{2,1,0:T(8,128)(2,1)S(1)}, u32[]{:S(2)}, u32[]{:S(2)}) async-start(bf16[8,128,256]{2,1,0:T(8,128)(2,1)} %bitcast.30), calls=%async_computation.2 | async-start | bytes 1048576 | tf_op jit(solution)/shard_map/all_to_all | solution.py:479
  172.6 2.4 %select_select_fusion = bf16[4,32,4096]{2,1,0:T(8,128)(2,1)} fusion(bf16[4,32,4096]{2,1,0:T(8,128)(2,1)} %bitcast.31, bf16[4,32,4096]{2,1,0:T(8,128)(2,1)S(1)} %copy-done, pred[4,32]{1,0:T(4,128)(4,1)S(1)} %get-tuple-element.36, pred[4,32]{1,0:T(4,128)(4,1)S(1)} %get-tuple-element.35), kind=kLoop, calls=%fused_computation | loop fusion | flops 1048576 | bytes 3145984 | tf_op jit(solution)/shard_map/jit(_where)/select_n | solution.py:470
  175.0 14.5 %all-to-all-done.2.att_ref = bf16[8,128,256]{2,1,0:T(8,128)(2,1)S(1)} async-done(((bf16[8,128,256]{2,1,0:T(8,128)(2,1)}), bf16[8,128,256]{2,1,0:T(8,128)(2,1)S(1)}, u32[]{:S(2)}, u32[]{:S(2)}) %all-to-all-start.2) | async-done | bytes 524320 | tf_op jit(solution)/shard_map/all_to_all | solution.py:479
  189.6 0.8 copy-done.1
  190.4 8.7 %shard_map.106 = bf16[128,4096]{1,0:T(8,128)(2,1)} custom-call(bf16[8,128,256]{2,1,0:T(8,128)(2,1)} %copy-done.1, bf16[32,2048,128]{2,1,0:T(8,128)(2,1)} %bitcast.26, bf16[128,4096]{1,0:T(8,128)(2,1)} %bitcast.27), custom_call_target="tpu_custom_call" | custom-call | flops 2147483648 | bytes 16777216 | tf_op jit(solution)/shard_map/pallas_call | solution.py:406
  (67 shorter events, 0.4 us)
Async XLA Ops:
  6.5 100.6 %copy-start.18 = (s32[4]{0:T(128)S(1)}, s32[4]{0:T(128)}, u32[]{:S(2)}) copy-start(s32[4]{0:T(128)} %param.11) | copy-start | bytes 52
  6.5 113.2 %copy-start.19 = (s32[4]{0:T(128)S(1)}, s32[4]{0:T(128)}, u32[]{:S(2)}) copy-start(s32[4]{0:T(128)} %param.12) | copy-start | bytes 52
  6.5 125.5 %copy-start.17 = (f32[1,4096]{1,0:T(1,128)S(1)}, f32[1,4096]{1,0:T(1,128)}, u32[]{:S(2)}) copy-start(f32[1,4096]{1,0:T(1,128)} %refs_12_.1) | copy-start | bytes 49156
  6.5 127.6 %all-gather.5.cloned.1.call-start = ((), (), s32[]{:S(2)}) async-start(), calls=%async_computation.3 | async-start | bytes 4325376 | tf_op jit(solution)/shard_map/all_gather | solution.py:445
  7.3 182.3 %all-gather.7.cloned.1.call-start = ((), (), s32[]{:S(2)}) async-start(), calls=%async_computation.4 | async-start | bytes 17301504 | tf_op jit(solution)/shard_map/all_gather | solution.py:450
  9.8 13.3 %collective-permute-start.10 = (bf16[128,768]{1,0:T(8,128)(2,1)}, bf16[128,768]{1,0:T(8,128)(2,1)S(1)}, u32[]{:S(2)}, u32[]{:S(2)}) collective-permute-start(bf16[128,768]{1,0:T(8,128)(2,1)} %get-tuple-element.22), channel_id=1, source_target_pairs={{0,4},{1,5},{2,6},{3,7},{4,0},{5,1},{6,2},{7,3},{8,12},{9,13},{10,... | collective-permute-start | bytes 589832 | tf_op jit(solution)/shard_map/ppermute | solution.py:25
  17.5 22.9 %collective-permute-start.11 = (bf16[128,768]{1,0:T(8,128)(2,1)}, bf16[128,768]{1,0:T(8,128)(2,1)S(1)}, u32[]{:S(2)}, u32[]{:S(2)}) collective-permute-start(bf16[128,768]{1,0:T(8,128)(2,1)} %get-tuple-element.23), channel_id=1, source_target_pairs={{0,5},{1,6},{2,7},{3,0},{4,1},{5,2},{6,3},{7,4},{8,13},{9,14},{10,... | collective-permute-start | bytes 589832 | tf_op jit(solution)/shard_map/ppermute | solution.py:25
  17.5 31.2 %collective-permute-start.12 = (bf16[128,768]{1,0:T(8,128)(2,1)}, bf16[128,768]{1,0:T(8,128)(2,1)S(1)}, u32[]{:S(2)}, u32[]{:S(2)}) collective-permute-start(bf16[128,768]{1,0:T(8,128)(2,1)} %get-tuple-element.24), channel_id=1, source_target_pairs={{0,6},{1,7},{2,0},{3,1},{4,2},{5,3},{6,4},{7,5},{8,14},{9,15},{10,... | collective-permute-start | bytes 589832 | tf_op jit(solution)/shard_map/ppermute | solution.py:25
  21.5 30.9 %collective-permute-start.13 = (bf16[128,768]{1,0:T(8,128)(2,1)}, bf16[128,768]{1,0:T(8,128)(2,1)S(1)}, u32[]{:S(2)}, u32[]{:S(2)}) collective-permute-start(bf16[128,768]{1,0:T(8,128)(2,1)} %get-tuple-element.25), channel_id=1, source_target_pairs={{0,7},{1,0},{2,1},{3,2},{4,3},{5,4},{6,5},{7,6},{8,15},{9,8},{10,9... | collective-permute-start | bytes 589832 | tf_op jit(solution)/shard_map/ppermute | solution.py:25
  22.3 30.2 %collective-permute-start.7 = (bf16[128,768]{1,0:T(8,128)(2,1)}, bf16[128,768]{1,0:T(8,128)(2,1)S(1)}, u32[]{:S(2)}, u32[]{:S(2)}) collective-permute-start(bf16[128,768]{1,0:T(8,128)(2,1)} %get-tuple-element.19), channel_id=1, source_target_pairs={{0,1},{1,2},{2,3},{3,4},{4,5},{5,6},{6,7},{7,0},{8,9},{9,10},{10,1... | collective-permute-start | bytes 589832 | tf_op jit(solution)/shard_map/ppermute | solution.py:25
  23.1 32.2 %copy-start.10 = (bf16[128,768]{1,0:T(8,128)(2,1)}, bf16[128,768]{1,0:T(8,128)(2,1)S(1)}, u32[]{:S(2)}) copy-start(bf16[128,768]{1,0:T(8,128)(2,1)S(1)} %collective-permute-done.10.refs_4_) | copy-start | bytes 589828
  23.1 29.4 %collective-permute-start.8 = (bf16[128,768]{1,0:T(8,128)(2,1)}, bf16[128,768]{1,0:T(8,128)(2,1)S(1)}, u32[]{:S(2)}, u32[]{:S(2)}) collective-permute-start(bf16[128,768]{1,0:T(8,128)(2,1)} %get-tuple-element.20), channel_id=1, source_target_pairs={{0,2},{1,3},{2,4},{3,5},{4,6},{5,7},{6,0},{7,1},{8,10},{9,11},{10,... | collective-permute-start | bytes 589832 | tf_op jit(solution)/shard_map/ppermute | solution.py:25
  40.4 14.9 %copy-start.11 = (bf16[128,768]{1,0:T(8,128)(2,1)}, bf16[128,768]{1,0:T(8,128)(2,1)S(1)}, u32[]{:S(2)}) copy-start(bf16[128,768]{1,0:T(8,128)(2,1)S(1)} %collective-permute-done.11.refs_5_) | copy-start | bytes 589828
  40.4 14.9 %collective-permute-start.9 = (bf16[128,768]{1,0:T(8,128)(2,1)}, bf16[128,768]{1,0:T(8,128)(2,1)S(1)}, u32[]{:S(2)}, u32[]{:S(2)}) collective-permute-start(bf16[128,768]{1,0:T(8,128)(2,1)} %get-tuple-element.21), channel_id=1, source_target_pairs={{0,3},{1,4},{2,5},{3,6},{4,7},{5,0},{6,1},{7,2},{8,11},{9,12},{10,... | collective-permute-start | bytes 589832 | tf_op jit(solution)/shard_map/ppermute | solution.py:25
  48.7 6.6 %copy-start.12 = (bf16[128,768]{1,0:T(8,128)(2,1)}, bf16[128,768]{1,0:T(8,128)(2,1)S(1)}, u32[]{:S(2)}) copy-start(bf16[128,768]{1,0:T(8,128)(2,1)S(1)} %collective-permute-done.12.refs_6_) | copy-start | bytes 589828
  52.5 2.8 %copy-start.13 = (bf16[128,768]{1,0:T(8,128)(2,1)}, bf16[128,768]{1,0:T(8,128)(2,1)S(1)}, u32[]{:S(2)}) copy-start(bf16[128,768]{1,0:T(8,128)(2,1)S(1)} %collective-permute-done.13.refs_7_) | copy-start | bytes 589828
  52.5 2.8 %copy-start.14 = (bf16[128,768]{1,0:T(8,128)(2,1)}, bf16[128,768]{1,0:T(8,128)(2,1)S(1)}, u32[]{:S(2)}) copy-start(bf16[128,768]{1,0:T(8,128)(2,1)S(1)} %collective-permute-done.7.refs_1_) | copy-start | bytes 589828
  52.5 2.8 %copy-start.15 = (bf16[128,768]{1,0:T(8,128)(2,1)}, bf16[128,768]{1,0:T(8,128)(2,1)S(1)}, u32[]{:S(2)}) copy-start(bf16[128,768]{1,0:T(8,128)(2,1)S(1)} %collective-permute-done.8.refs_2_) | copy-start | bytes 589828
  55.3 0.7 copy-start.16
  82.5 14.8 %all-to-all-start.1 = ((bf16[32,4,1024]{2,1,0:T(4,128)(2,1)}), bf16[32,4,1024]{2,1,0:T(4,128)(2,1)S(1)}, u32[]{:S(2)}, u32[]{:S(2)}) async-start(bf16[32,4,1024]{2,1,0:T(4,128)(2,1)} %reshape.150), calls=%async_computation.1 | async-start | bytes 524288 | tf_op jit(solution)/shard_map/all_to_all | solution.py:95
  86.3 15.1 %collective-permute-start.14 = (bf16[256,512]{1,0:T(8,128)(2,1)}, bf16[256,512]{1,0:T(8,128)(2,1)S(1)}, u32[]{:S(2)}, u32[]{:S(2)}) collective-permute-start(bf16[256,512]{1,0:T(8,128)(2,1)} %get-tuple-element.26.refs_0_), channel_id=1, source_target_pairs={{0,1},{1,2},{2,3},{3,4},{4,5},{5,6},{6,7},{7,0},{8,9},{9,10},{10,1... | collective-permute-start | bytes 786440 | tf_op jit(solution)/shard_map/ppermute | solution.py:25
  97.4 42.8 %copy-start.9 = (bf16[32,4,1024]{2,0,1:T(8,128)(2,1)}, bf16[32,4,1024]{2,0,1:T(8,128)(2,1)S(1)}, u32[]{:S(2)}) copy-start(bf16[32,4,1024]{2,0,1:T(8,128)(2,1)S(1)} %copy.18) | copy-start | bytes 786436
  97.4 9.1 %collective-permute-start = (bf16[4,32,1024]{2,1,0:T(8,128)(2,1)S(1)}, bf16[4,32,1024]{2,1,0:T(8,128)(2,1)S(1)}, u32[]{:S(2)}, u32[]{:S(2)}) collective-permute-start(bf16[4,32,1024]{2,1,0:T(8,128)(2,1)S(1)} %bitcast.33), channel_id=1, source_target_pairs={{0,1},{1,2},{2,3},{3,4},{4,5},{5,6},{8,9},{9,10},{10,11},{11,12},{... | collective-permute-start | bytes 786440 | tf_op jit(solution)/shard_map/ppermute | solution.py:25
  100.7 7.7 %collective-permute-start.18 = (bf16[256,512]{1,0:T(8,128)(2,1)}, bf16[256,512]{1,0:T(8,128)(2,1)S(1)}, u32[]{:S(2)}, u32[]{:S(2)}) collective-permute-start(bf16[256,512]{1,0:T(8,128)(2,1)} %get-tuple-element.26.refs_0_), channel_id=1, source_target_pairs={{0,7},{1,0},{2,1},{3,2},{4,3},{5,4},{6,5},{7,6},{8,15},{9,8},{10,9... | collective-permute-start | bytes 786440 | tf_op jit(solution)/shard_map/ppermute | solution.py:25
  101.3 32.9 %copy-start.2 = (bf16[256,512]{1,0:T(8,128)(2,1)}, bf16[256,512]{1,0:T(8,128)(2,1)S(1)}, u32[]{:S(2)}) copy-start(bf16[256,512]{1,0:T(8,128)(2,1)S(1)} %collective-permute-done.14.refs_1_) | copy-start | bytes 786436
  101.3 10.4 %collective-permute-start.15 = (bf16[256,512]{1,0:T(8,128)(2,1)S(1)}, bf16[256,512]{1,0:T(8,128)(2,1)S(1)}, u32[]{:S(2)}, u32[]{:S(2)}) collective-permute-start(bf16[256,512]{1,0:T(8,128)(2,1)S(1)} %collective-permute-done.14.refs_1_), channel_id=1, source_target_pairs={{0,1},{1,2},{2,3},{3,4},{4,5},{5,6},{6,7},{7,0},{8,9},{9,10},{10,1... | collective-permute-start | bytes 786440 | tf_op jit(solution)/shard_map/ppermute | solution.py:25
  102.8 11.8 %collective-permute-start.1 = (bf16[4,32,1024]{2,1,0:T(8,128)(2,1)S(1)}, bf16[4,32,1024]{2,1,0:T(8,128)(2,1)S(1)}, u32[]{:S(2)}, u32[]{:S(2)}) collective-permute-start(bf16[4,32,1024]{2,1,0:T(8,128)(2,1)S(1)} %bitcast.34), channel_id=1, source_target_pairs={{0,7},{1,0},{2,1},{3,2},{4,3},{5,4},{8,15},{9,8},{10,9},{11,10},{1... | collective-permute-start | bytes 786440 | tf_op jit(solution)/shard_map/ppermute | solution.py:25
  106.5 33.7 %copy-start.20 = (bf16[4,32,1024]{2,1,0:T(8,128)(2,1)}, bf16[4,32,1024]{2,1,0:T(8,128)(2,1)S(1)}, u32[]{:S(2)}) copy-start(bf16[4,32,1024]{2,1,0:T(8,128)(2,1)S(1)} %collective-permute-done.refs_1_) | copy-start | bytes 786436
  106.5 11.9 %collective-permute-start.2 = (bf16[4,32,1024]{2,1,0:T(8,128)(2,1)S(1)}, bf16[4,32,1024]{2,1,0:T(8,128)(2,1)S(1)}, u32[]{:S(2)}, u32[]{:S(2)}) collective-permute-start(bf16[4,32,1024]{2,1,0:T(8,128)(2,1)S(1)} %collective-permute-done.refs_1_), channel_id=1, source_target_pairs={{1,2},{2,3},{3,4},{4,5},{5,6},{6,7},{9,10},{10,11},{11,12},{12,13}... | collective-permute-start | bytes 786440 | tf_op jit(solution)/shard_map/ppermute | solution.py:25
  108.4 25.8 %copy-start.3 = (bf16[256,512]{1,0:T(8,128)(2,1)}, bf16[256,512]{1,0:T(8,128)(2,1)S(1)}, u32[]{:S(2)}) copy-start(bf16[256,512]{1,0:T(8,128)(2,1)S(1)} %collective-permute-done.18.refs_7_) | copy-start | bytes 786436
  108.4 11.3 %collective-permute-start.19 = (bf16[256,512]{1,0:T(8,128)(2,1)S(1)}, bf16[256,512]{1,0:T(8,128)(2,1)S(1)}, u32[]{:S(2)}, u32[]{:S(2)}) collective-permute-start(bf16[256,512]{1,0:T(8,128)(2,1)S(1)} %collective-permute-done.18.refs_7_), channel_id=1, source_target_pairs={{0,7},{1,0},{2,1},{3,2},{4,3},{5,4},{6,5},{7,6},{8,15},{9,8},{10,9... | collective-permute-start | bytes 786440 | tf_op jit(solution)/shard_map/ppermute | solution.py:25
  111.8 22.4 %copy-start.4 = (bf16[256,512]{1,0:T(8,128)(2,1)}, bf16[256,512]{1,0:T(8,128)(2,1)S(1)}, u32[]{:S(2)}) copy-start(bf16[256,512]{1,0:T(8,128)(2,1)S(1)} %collective-permute-done.15.refs_2_) | copy-start | bytes 786436
  111.8 11.3 %collective-permute-start.16 = (bf16[256,512]{1,0:T(8,128)(2,1)S(1)}, bf16[256,512]{1,0:T(8,128)(2,1)S(1)}, u32[]{:S(2)}, u32[]{:S(2)}) collective-permute-start(bf16[256,512]{1,0:T(8,128)(2,1)S(1)} %collective-permute-done.15.refs_2_), channel_id=1, source_target_pairs={{0,1},{1,2},{2,3},{3,4},{4,5},{5,6},{6,7},{7,0},{8,9},{9,10},{10,1... | collective-permute-start | bytes 786440 | tf_op jit(solution)/shard_map/ppermute | solution.py:25
  114.6 25.6 %copy-start.21 = (bf16[4,32,1024]{2,1,0:T(8,128)(2,1)}, bf16[4,32,1024]{2,1,0:T(8,128)(2,1)S(1)}, u32[]{:S(2)}) copy-start(bf16[4,32,1024]{2,1,0:T(8,128)(2,1)S(1)} %collective-permute-done.1.refs_2_) | copy-start | bytes 786436
  114.6 10.7 %collective-permute-start.3 = (bf16[4,32,1024]{2,1,0:T(8,128)(2,1)S(1)}, bf16[4,32,1024]{2,1,0:T(8,128)(2,1)}, u32[]{:S(2)}, u32[]{:S(2)}) collective-permute-start(bf16[4,32,1024]{2,1,0:T(8,128)(2,1)S(1)} %collective-permute-done.1.refs_2_), channel_id=1, source_target_pairs={{0,7},{1,0},{2,1},{3,2},{4,3},{7,6},{8,15},{9,8},{10,9},{11,10},{1... | collective-permute-start | bytes 786440 | tf_op jit(solution)/shard_map/ppermute | solution.py:25
  118.4 21.9 %copy-start.22 = (bf16[4,32,1024]{2,1,0:T(8,128)(2,1)}, bf16[4,32,1024]{2,1,0:T(8,128)(2,1)S(1)}, u32[]{:S(2)}) copy-start(bf16[4,32,1024]{2,1,0:T(8,128)(2,1)S(1)} %collective-permute-done.2.refs_3_) | copy-start | bytes 786436
  118.4 10.2 %collective-permute-start.4 = (bf16[4,32,1024]{2,1,0:T(8,128)(2,1)S(1)}, bf16[4,32,1024]{2,1,0:T(8,128)(2,1)}, u32[]{:S(2)}, u32[]{:S(2)}) collective-permute-start(bf16[4,32,1024]{2,1,0:T(8,128)(2,1)S(1)} %collective-permute-done.2.refs_3_), channel_id=1, source_target_pairs={{2,3},{3,4},{4,5},{5,6},{6,7},{7,0},{10,11},{11,12},{12,13},{13,14... | collective-permute-start | bytes 786440 | tf_op jit(solution)/shard_map/ppermute | solution.py:25
  119.8 14.5 %copy-start.5 = (bf16[256,512]{1,0:T(8,128)(2,1)}, bf16[256,512]{1,0:T(8,128)(2,1)S(1)}, u32[]{:S(2)}) copy-start(bf16[256,512]{1,0:T(8,128)(2,1)S(1)} %collective-permute-done.19.refs_6_) | copy-start | bytes 786436
  119.8 14.4 %collective-permute-start.20 = (bf16[256,512]{1,0:T(8,128)(2,1)S(1)}, bf16[256,512]{1,0:T(8,128)(2,1)S(1)}, u32[]{:S(2)}, u32[]{:S(2)}) collective-permute-start(bf16[256,512]{1,0:T(8,128)(2,1)S(1)} %collective-permute-done.19.refs_6_), channel_id=1, source_target_pairs={{0,7},{1,0},{2,1},{3,2},{4,3},{5,4},{6,5},{7,6},{8,15},{9,8},{10,9... | collective-permute-start | bytes 786440 | tf_op jit(solution)/shard_map/ppermute | solution.py:25
  123.1 11.1 %copy-start.6 = (bf16[256,512]{1,0:T(8,128)(2,1)}, bf16[256,512]{1,0:T(8,128)(2,1)S(1)}, u32[]{:S(2)}) copy-start(bf16[256,512]{1,0:T(8,128)(2,1)S(1)} %collective-permute-done.16.refs_3_) | copy-start | bytes 786436
  123.1 11.0 %collective-permute-start.17 = (bf16[256,512]{1,0:T(8,128)(2,1)S(1)}, bf16[256,512]{1,0:T(8,128)(2,1)S(1)}, u32[]{:S(2)}, u32[]{:S(2)}) collective-permute-start(bf16[256,512]{1,0:T(8,128)(2,1)S(1)} %collective-permute-done.16.refs_3_), channel_id=1, source_target_pairs={{0,1},{1,2},{2,3},{3,4},{4,5},{5,6},{6,7},{7,0},{8,9},{9,10},{10,1... | collective-permute-start | bytes 786440 | tf_op jit(solution)/shard_map/ppermute | solution.py:25
  125.4 14.8 %collective-permute-start.5 = (bf16[4,32,1024]{2,1,0:T(8,128)(2,1)}, bf16[4,32,1024]{2,1,0:T(8,128)(2,1)}, u32[]{:S(2)}, u32[]{:S(2)}) collective-permute-start(bf16[4,32,1024]{2,1,0:T(8,128)(2,1)} %collective-permute-done.3.refs_4_), channel_id=1, source_target_pairs={{0,7},{1,0},{2,1},{3,2},{6,5},{7,6},{8,15},{9,8},{10,9},{11,10},{1... | collective-permute-start | bytes 786440 | tf_op jit(solution)/shard_map/ppermute | solution.py:25
  128.6 11.6 %collective-permute-start.6 = (bf16[4,32,1024]{2,1,0:T(8,128)(2,1)}, bf16[4,32,1024]{2,1,0:T(8,128)(2,1)}, u32[]{:S(2)}, u32[]{:S(2)}) collective-permute-start(bf16[4,32,1024]{2,1,0:T(8,128)(2,1)} %collective-permute-done.4.refs_5_), channel_id=1, source_target_pairs={{0,1},{3,4},{4,5},{5,6},{6,7},{7,0},{8,9},{11,12},{12,13},{13,14},... | collective-permute-start | bytes 786440 | tf_op jit(solution)/shard_map/ppermute | solution.py:25
  134.1 0.7 copy-start.7
  134.2 0.8 copy-start.8
  140.2 32.4 %copy-start = (bf16[4,32,4096]{2,1,0:T(8,128)(2,1)S(1)}, bf16[4,32,4096]{2,1,0:T(8,128)(2,1)}, u32[]{:S(2)}) copy-start(bf16[4,32,4096]{2,1,0:T(8,128)(2,1)} %text_ref.1) | copy-start | bytes 3145732
  164.9 24.7 %all-to-all-start.2 = ((bf16[8,128,256]{2,1,0:T(8,128)(2,1)}), bf16[8,128,256]{2,1,0:T(8,128)(2,1)S(1)}, u32[]{:S(2)}, u32[]{:S(2)}) async-start(bf16[8,128,256]{2,1,0:T(8,128)(2,1)} %bitcast.30), calls=%async_computation.2 | async-start | bytes 1048576 | tf_op jit(solution)/shard_map/all_to_all | solution.py:479
  189.6 0.8 copy-start.1
Sparse Core Ops, SparseCore 0:
  9.9 55.2 all-gather.4
  67.7 78.2 all-gather.6

commit v3 on v2

--- a/solution.py
+++ b/solution.py
@@ -228,25 +228,41 @@
     )(mine.reshape(1), *chunks, cosine, sine, gain.reshape(parts, width), all_qkv)
 
 
-def image_kernel(*refs, groups):
+def image_kernel(place_ref, *refs, groups, useful):
     chunk_refs = refs[:groups]
     cos_ref, sin_ref, proj_ref, bias_ref, gain_ref, qkv_ref = refs[groups : groups + 6]
     out_ref, hidden_ref, rows_ref, sum_ref, squares_ref = refs[groups + 6 :]
     tiles, local_rows, depth = chunk_refs[0].shape
     each = tiles * local_rows
     step = pl.program_id(0)
+    mine = place_ref[0]
 
     @pl.when(step == 0)
     def _():
-        for g, chunk_ref in enumerate(chunk_refs):
-            rows_ref[g * each : (g + 1) * each, :] = chunk_ref[...].reshape(each, depth)
+        for s, chunk_ref in enumerate(chunk_refs):
+            at = lax.rem(mine + (groups - s), groups)
+
+            @pl.when(at < useful)
+            def _(at=at, chunk_ref=chunk_ref):
+                begin = pl.multiple_of(at * each, each)
+                rows_ref[pl.ds(begin, each), :] = chunk_ref[...].reshape(each, depth)
+
         sum_ref[...] = jnp.zeros_like(sum_ref)
         squares_ref[...] = jnp.zeros_like(squares_ref)
 
     projected = (
         jnp.dot(rows_ref[...], proj_ref[...], preferred_element_type=jnp.float32) + bias_ref[...]
     ).astype(jnp.bfloat16)
-    hidden_ref[...] = projected[:each]
+    for at in range(useful):
+
+        @pl.when(mine == at)
+        def _(at=at):
+            hidden_ref[...] = projected[at * each : (at + 1) * each]
+
+    @pl.when(mine >= useful)
+    def _():
+        hidden_ref[...] = jnp.zeros_like(hidden_ref)
+
     wide = projected.astype(jnp.float32)
     squares_ref[...] += jnp.sum(wide * wide, axis=1, keepdims=True)
     scaled = (wide * gain_ref[...]).astype(jnp.bfloat16)
@@ -256,9 +272,9 @@
     def _():
         model_width = proj_ref.shape[1] * pl.num_programs(0)
         scale = lax.rsqrt(squares_ref[...] * (1.0 / model_width) + epsilon)
-        shape = (groups, tiles, local_rows, HS)
-        cosine = jnp.broadcast_to(cos_ref[...][:, None], shape).reshape(groups * each, HS)
-        sine = jnp.broadcast_to(sin_ref[...][:, None], shape).reshape(groups * each, HS)
+        shape = (useful, tiles, local_rows, HS)
+        cosine = jnp.broadcast_to(cos_ref[...][:, None], shape).reshape(useful * each, HS)
+        sine = jnp.broadcast_to(sin_ref[...][:, None], shape).reshape(useful * each, HS)
 
         def store(p, value):
             out_ref[:, :, :, p * HS : (p + 1) * HS] = value.reshape(shape)
@@ -266,66 +282,68 @@
         rotate_store(sum_ref[...] * scale, cosine, sine, store)
 
 
-def image_qkv_of(chunks, cosine, sine, w_proj, bias, gain, all_qkv):
+def image_qkv_of(chunks, mine, cosine, sine, w_proj, bias, gain, all_qkv):
     groups = len(chunks)
+    useful = cosine.shape[0]
     tiles, local_rows, depth = chunks[0].shape
     model_width, outs = all_qkv.shape
     each = tiles * local_rows
     block = 1024
-    fixed = lambda *shape: pl.BlockSpec(shape, lambda i: (0,) * len(shape))
-    out_specs = [
-        fixed(groups, tiles, local_rows, outs),
-        pl.BlockSpec((each, block), lambda i: (0, i)),
-    ]
-    out_shape = [
-        jax.ShapeDtypeStruct((groups, tiles, local_rows, outs), jnp.bfloat16),
-        jax.ShapeDtypeStruct((each, model_width), jnp.bfloat16),
-    ]
+    fixed = lambda *shape: pl.BlockSpec(shape, lambda i, c: (0,) * len(shape))
     return pl.pallas_call(
-        functools.partial(image_kernel, groups=groups),
-        grid=(model_width // block,),
-        in_specs=[fixed(tiles, local_rows, depth)] * groups
-        + [
-            fixed(groups, local_rows, HS),
-            fixed(groups, local_rows, HS),
-            pl.BlockSpec((depth, block), lambda i: (0, i)),
-            pl.BlockSpec((1, block), lambda i: (0, i)),
-            pl.BlockSpec((1, block), lambda i: (0, i)),
-            pl.BlockSpec((block, outs), lambda i: (i, 0)),
-        ],
-        out_specs=out_specs,
-        out_shape=out_shape,
-        scratch_shapes=[
-            pltpu.VMEM((groups * each, depth), jnp.bfloat16),
-            pltpu.VMEM((groups * each, outs), jnp.float32),
-            pltpu.VMEM((groups * each, 1), jnp.float32),
+        functools.partial(image_kernel, groups=groups, useful=useful),
+        grid_spec=pltpu.PrefetchScalarGridSpec(
+            num_scalar_prefetch=1,
+            grid=(model_width // block,),
+            in_specs=[fixed(tiles, local_rows, depth)] * groups
+            + [
+                fixed(useful, local_rows, HS),
+                fixed(useful, local_rows, HS),
+                pl.BlockSpec((depth, block), lambda i, c: (0, i)),
+                pl.BlockSpec((1, block), lambda i, c: (0, i)),
+                pl.BlockSpec((1, block), lambda i, c: (0, i)),
+                pl.BlockSpec((block, outs), lambda i, c: (i, 0)),
+            ],
+            out_specs=[
+                fixed(useful, tiles, local_rows, outs),
+                pl.BlockSpec((each, block), lambda i, c: (0, i)),
+            ],
+            scratch_shapes=[
+                pltpu.VMEM((useful * each, depth), jnp.bfloat16),
+                pltpu.VMEM((useful * each, outs), jnp.float32),
+                pltpu.VMEM((useful * each, 1), jnp.float32),
+            ],
+        ),
+        out_shape=[
+            jax.ShapeDtypeStruct((useful, tiles, local_rows, outs), jnp.bfloat16),
+            jax.ShapeDtypeStruct((each, model_width), jnp.bfloat16),
         ],
         compiler_params=pltpu.CompilerParams(dimension_semantics=("arbitrary",)),
         cost_estimate=pl.CostEstimate(
-            flops=2 * groups * each * model_width * (depth + outs),
+            flops=2 * useful * each * model_width * (depth + outs),
             bytes_accessed=2 * model_width * (depth + outs),
             transcendentals=0,
         ),
-    )(*chunks, cosine, sine, w_proj, bias, gain, all_qkv)
-
-
-def attend_kernel(counts_ref, image_ref, text_ref, out_ref, rows_ref, *, order):
+    )(mine.reshape(1), *chunks, cosine, sine, w_proj, bias, gain, all_qkv)
+
+
+def attend_kernel(counts_ref, image_ref, text_ref, out_ref):
     tile = pl.program_id(0)
     patch = counts_ref[0, tile]
     texts = counts_ref[1, tile]
-    mine = counts_ref[2, 0]
     length = patch + texts
-    parts, local_rows, outs = rows_ref.shape
-    for at, s in enumerate(order):
-        rows_ref[lax.rem(mine + (parts - s), parts)] = image_ref[at, 0]
+    useful, _, local_rows, outs = image_ref.shape
+    parts = out_ref.shape[0]
     rows = parts * local_rows
     row = lax.broadcasted_iota(jnp.int32, (rows, WINDOW), 0)
     place = lax.broadcasted_iota(jnp.int32, (rows, WINDOW), 1)
     placing = jnp.where((row == patch + place) & (place < texts), 1.0, 0.0).astype(jnp.bfloat16)
     placed = jnp.dot(placing, text_ref[...], preferred_element_type=jnp.float32)
-    image_row = lax.broadcasted_iota(jnp.int32, (rows, outs), 0) < patch
-    qkv = jnp.where(
-        image_row, rows_ref[...].reshape(rows, outs).astype(jnp.float32), placed
+    first = useful * local_rows
+    image_row = lax.broadcasted_iota(jnp.int32, (first, outs), 0) < patch
+    image = image_ref[...].reshape(first, outs).astype(jnp.float32)
+    qkv = jnp.concatenate(
+        [jnp.where(image_row, image, placed[:first]), placed[first:]], axis=0
     ).astype(jnp.bfloat16)
     keys = qkv[:, GROUP * HS : (GROUP + 1) * HS]
     values = qkv[:, (GROUP + 1) * HS :]
@@ -349,20 +367,19 @@
         )
 
 
-def attend(image_qkv, order, text_qkv, counts):
-    parts, tiles, local_rows, outs = image_qkv.shape
+def attend(image_qkv, text_qkv, counts, parts):
+    useful, tiles, local_rows, outs = image_qkv.shape
     rows = parts * local_rows
     return pl.pallas_call(
-        functools.partial(attend_kernel, order=order),
+        attend_kernel,
         grid_spec=pltpu.PrefetchScalarGridSpec(
             num_scalar_prefetch=1,
             grid=(tiles,),
             in_specs=[
-                pl.BlockSpec((parts, 1, local_rows, outs), lambda t, c: (0, t, 0, 0)),
+                pl.BlockSpec((useful, 1, local_rows, outs), lambda t, c: (0, t, 0, 0)),
                 pl.BlockSpec((WINDOW, outs), lambda t, c: (t, 0)),
             ],
             out_specs=pl.BlockSpec((parts, 1, local_rows, GROUP * HS), lambda t, c: (0, t, 0, 0)),
-            scratch_shapes=[pltpu.VMEM((parts, local_rows, outs), jnp.bfloat16)],
         ),
         out_shape=jax.ShapeDtypeStruct((parts, tiles, local_rows, GROUP * HS), jnp.bfloat16),
         compiler_params=pltpu.CompilerParams(dimension_semantics=("arbitrary",)),
@@ -455,14 +472,15 @@
 
     text_places = patch_counts[:, None] + jnp.arange(WINDOW, dtype=jnp.int32)[None, :]
     text_cos, text_sin = rotation_tables(text_places.reshape(-1))
-    order = (0, *[s for k in range(1, parts // 2) for s in (k, parts - k)], parts // 2)
     local = jnp.arange(local_rows, dtype=jnp.int32)
-    begins = jnp.stack([lax.rem(mine + (parts - s), parts) * local_rows for s in order])
-    chunk_cos, chunk_sin = rotation_tables(begins[:, None] + local[None, :])
+    useful = -(-IMAGE_ROWS // local_rows)
+    chunk_cos, chunk_sin = rotation_tables(
+        jnp.arange(useful * local_rows, dtype=jnp.int32).reshape(useful, local_rows)
+    )
 
     bias = b_proj.reshape(1, model_width)
     image_qkv, own_projected = image_qkv_of(
-        [chunks[s] for s in order], chunk_cos, chunk_sin, w_proj, bias, norm_gain, all_qkv
+        chunks, mine, chunk_cos, chunk_sin, w_proj, bias, norm_gain, all_qkv
     )
     text_qkv = text_qkv_of(text_chunks, mine, text_cos, text_sin, norm_gain, all_qkv)
 
@@ -475,7 +493,7 @@
         ),
     ).reshape(each, model_width)
 
-    attended = attend(image_qkv, order, text_qkv, counts)
+    attended = attend(image_qkv, text_qkv, counts, parts)
     returned = lax.all_to_all(
         attended.reshape(parts, each, -1), "mp", split_axis=0, concat_axis=0, tiled=True
     )

time: 207 us -> 204 us (0.986)
  Pallas kernels: 45.8 us -> 43 us
    pallas_call x2, Pallas kernels: 24.6 us -> 21.9 us  [the longest x1 16 us: image_qkv_of(): pl.pallas_call(functools.partial(image_kernel, groups=groups, useful=usef...]
  transfers between devices with their start and end apart: 25 -> 25, of which waited for: 9 -> 10; matrix products, arithmetic and copies ran while one was open for 6% -> 7% of each run, Pallas kernels for 18% -> 17%
where the time goes in v3:
time: 204 us; the launch traced here: 203 us
  starting transfers between devices  64.5 us (32%)
  waiting for transfers between devices  48.4 us (24%)
  Pallas kernels  43 us (21%)
  blocking collectives  17.2 us (8%)
  between operations  13.8 us (7%)
  other arithmetic  8.57 us (4%)
  local copies, waits for them, and re-layouts  7.32 us (4%)
    ppermute x21, starting transfers between devices, shifted(): return lax.ppermute(value, axis, pairs)  53.2 us
    ppermute x21, waiting for transfers between devices, shifted(): return lax.ppermute(value, axis, pairs)  25.3 us
    all_to_all x1, blocking collectives, exchange_tiles(): got = lax.all_to_all(sent, 'dp', split_axis=0, concat_axis=0, tiled=True)  17.2 us
    pallas_call x1, Pallas kernels, image_qkv_of(): pl.pallas_call(functools.partial(image_kernel, groups=groups, useful=usef...  16 us
    all_to_all x1, waiting for transfers between devices, body(): lax.all_to_all(attended.reshape(parts, each, -1), 'mp', split_axis=0, con...  14.3 us
    pallas_call x1, Pallas kernels, project_out(): pl.pallas_call(out_kernel, in_specs=[whole, pl.BlockSpec(memory_space=pl....  8.73 us
    all_to_all x1, waiting for transfers between devices, exchange_tiles(): lax.all_to_all(ordered.reshape(ranks, image_count, width), 'dp', split_ax...  8.09 us
    all_to_all x1, starting transfers between devices, body(): lax.all_to_all(attended.reshape(parts, each, -1), 'mp', split_axis=0, con...  7.58 us
  transfers between devices with their start and end apart: 25, of which 10 were waited for; matrix products, arithmetic and copies ran while one was open for 7% of the time, Pallas kernels for 17%

profile of v3, /device:TPU:1, one launch (start us, length us, event | category | flops | bytes accessed | tf_op | source)
XLA Modules:
  0.0 202.8 jit_solution(14574506839473813042)
XLA Ops:
  6.5 0.7 all-gather.5.cloned.1.call-update
  7.3 2.4 %shard_map.102 = (bf16[128,768]{1,0:T(8,128)(2,1)}, bf16[128,768]{1,0:T(8,128)(2,1)}, bf16[128,768]{1,0:T(8,128)(2,1)}, bf16[128,768]{1,0:T(8,128)(2,1)}, bf16[1...) custom-call(s32[1]{0:T(128)} %bitcast.13.place_ref, ...), custom_call_target="tpu_custom_call" | custom-call | flops 1048576 | bytes 3145728 | tf_op jit(solution)/shard_map/pallas_call | solution.py:127
  9.7 7.7 %collective-permute-start.10 = (bf16[128,768]{1,0:T(8,128)(2,1)}, bf16[128,768]{1,0:T(8,128)(2,1)S(1)}, u32[]{:S(2)}, u32[]{:S(2)}) collective-permute-start(bf16[128,768]{1,0:T(8,128)(2,1)} %get-tuple-element.22), channel_id=1, source_target_pairs={{0,4},{1,5},{2,6},{3,7},{4,0},{5,1},{6,2},{7,3},{8,12},{9,13},{10,... | collective-permute-start | bytes 589832 | tf_op jit(solution)/shard_map/ppermute | solution.py:25
  17.5 4.0 %collective-permute-start.12 = (bf16[128,768]{1,0:T(8,128)(2,1)}, bf16[128,768]{1,0:T(8,128)(2,1)S(1)}, u32[]{:S(2)}, u32[]{:S(2)}) collective-permute-start(bf16[128,768]{1,0:T(8,128)(2,1)} %get-tuple-element.24), channel_id=1, source_target_pairs={{0,6},{1,7},{2,0},{3,1},{4,2},{5,3},{6,4},{7,5},{8,14},{9,15},{10,... | collective-permute-start | bytes 589832 | tf_op jit(solution)/shard_map/ppermute | solution.py:25
  21.5 0.7 collective-permute-start.13
  22.2 0.7 collective-permute-start.7
  23.0 0.1 pad.12.clone
  23.1 5.0 %collective-permute-start.8 = (bf16[128,768]{1,0:T(8,128)(2,1)}, bf16[128,768]{1,0:T(8,128)(2,1)S(1)}, u32[]{:S(2)}, u32[]{:S(2)}) collective-permute-start(bf16[128,768]{1,0:T(8,128)(2,1)} %get-tuple-element.20), channel_id=1, source_target_pairs={{0,2},{1,3},{2,4},{3,5},{4,6},{5,7},{6,0},{7,1},{8,10},{9,11},{10,... | collective-permute-start | bytes 589832 | tf_op jit(solution)/shard_map/ppermute | solution.py:25
  28.1 12.2 %collective-permute-done.11.refs_5_ = bf16[128,768]{1,0:T(8,128)(2,1)S(1)} collective-permute-done((bf16[128,768]{1,0:T(8,128)(2,1)}, bf16[128,768]{1,0:T(8,128)(2,1)S(1)}, u32[]{:S(2)}, u32[]{:S(2)}) %collective-permute-start.11) | collective-permute-done | bytes 196640 | tf_op jit(solution)/shard_map/ppermute | solution.py:25
  40.3 5.3 %collective-permute-start.9 = (bf16[128,768]{1,0:T(8,128)(2,1)}, bf16[128,768]{1,0:T(8,128)(2,1)S(1)}, u32[]{:S(2)}, u32[]{:S(2)}) collective-permute-start(bf16[128,768]{1,0:T(8,128)(2,1)} %get-tuple-element.21), channel_id=1, source_target_pairs={{0,3},{1,4},{2,5},{3,6},{4,7},{5,0},{6,1},{7,2},{8,11},{9,12},{10,... | collective-permute-start | bytes 589832 | tf_op jit(solution)/shard_map/ppermute | solution.py:25
  45.6 1.3 add_add_fusion.counts_ref
  46.9 1.7 collective-permute-done.12.refs_6_
  48.7 3.8 %collective-permute-done.13.refs_7_ = bf16[128,768]{1,0:T(8,128)(2,1)S(1)} collective-permute-done((bf16[128,768]{1,0:T(8,128)(2,1)}, bf16[128,768]{1,0:T(8,128)(2,1)S(1)}, u32[]{:S(2)}, u32[]{:S(2)}) %collective-permute-start.13) | collective-permute-done | bytes 196640 | tf_op jit(solution)/shard_map/ppermute | solution.py:25
  52.5 2.8 %collective-permute-done.9.refs_3_ = bf16[128,768]{1,0:T(8,128)(2,1)S(1)} collective-permute-done((bf16[128,768]{1,0:T(8,128)(2,1)}, bf16[128,768]{1,0:T(8,128)(2,1)S(1)}, u32[]{:S(2)}, u32[]{:S(2)}) %collective-permute-start.9) | collective-permute-done | bytes 196640 | tf_op jit(solution)/shard_map/ppermute | solution.py:25
  55.3 0.6 copy-done.16
  55.9 2.6 %shard_map.103 = (bf16[256,512]{1,0:T(8,128)(2,1)}, bf16[2048,128]{1,0:T(8,128)(2,1)}) custom-call(s32[3,4]{1,0:T(4,128)} %add_add_fusion.counts_ref, bf16[128,768]{1,0:T(8,128)(2,1)} %get-tuple-element.18.refs_0_, bf16[128,768]{1,0:T(8,128)(2,1)} %copy-done.14, bf16[128,768]{1,0:T(8,128)(2,1)} %copy-done.15, bf16[128,768]{1,0:T(8,128)(2,1)} %copy-done.16, ...), custom_call_target="tpu_custom_call" | custom-call | flops 67108864 | bytes 1572864 | tf_op jit(solution)/shard_map/pallas_call | solution.py:171
  58.5 1.2 copy.19
  59.7 0.7 convert_element_type.26
  60.4 0.1 broadcast_in_dim.16
  60.5 0.1 pad_maximum_fusion
  60.6 17.2 %all_to_all.15 = bf16[32,4,1152]{2,1,0:T(4,128)(2,1)S(1)} all-to-all(bf16[32,4,1152]{2,1,0:T(4,128)(2,1)S(1)} %pad_maximum_fusion), channel_id=1, replica_groups=mesh['dp'=32,'mp'=8] {'dp'}, dimensions={0} | all-to-all | bytes 589824 | tf_op jit(solution)/shard_map/all_to_all | solution.py:86
  77.8 0.8 reshape.157.got_ref
  78.6 2.1 %shard_map.100 = bf16[128,1024]{1,0:T(8,128)(2,1)} custom-call(bf16[128,1152]{1,0:T(8,128)(2,1)} %reshape.157.got_ref), custom_call_target="tpu_custom_call" | custom-call | flops 33554432 | bytes 524288 | tf_op jit(solution)/shard_map/pallas_call | solution.py:88
  80.7 1.8 reshape.158
  82.4 3.7 %all-to-all-start.1 = ((bf16[32,4,1024]{2,1,0:T(4,128)(2,1)}), bf16[32,4,1024]{2,1,0:T(4,128)(2,1)S(1)}, u32[]{:S(2)}, u32[]{:S(2)}) async-start(bf16[32,4,1024]{2,1,0:T(4,128)(2,1)} %reshape.158), calls=%async_computation.1 | async-start | bytes 524288 | tf_op jit(solution)/shard_map/all_to_all | solution.py:95
  86.1 2.4 %collective-permute-start.14 = (bf16[256,512]{1,0:T(8,128)(2,1)}, bf16[256,512]{1,0:T(8,128)(2,1)S(1)}, u32[]{:S(2)}, u32[]{:S(2)}) collective-permute-start(bf16[256,512]{1,0:T(8,128)(2,1)} %get-tuple-element.26.refs_0_), channel_id=1, source_target_pairs={{0,1},{1,2},{2,3},{3,4},{4,5},{5,6},{6,7},{7,0},{8,9},{9,10},{10,1... | collective-permute-start | bytes 786440 | tf_op jit(solution)/shard_map/ppermute | solution.py:25
  88.5 0.7 add_convert_fusion.1
  89.2 8.1 %all-to-all-done.1 = bf16[32,4,1024]{2,1,0:T(4,128)(2,1)S(1)} async-done(((bf16[32,4,1024]{2,1,0:T(4,128)(2,1)}), bf16[32,4,1024]{2,1,0:T(4,128)(2,1)S(1)}, u32[]{:S(2)}, u32[]{:S(2)}) %all-to-all-start.1) | async-done | bytes 262176 | tf_op jit(solution)/shard_map/all_to_all | solution.py:95
  97.3 0.1 copy.18
  97.4 3.3 %collective-permute-start = (bf16[4,32,1024]{2,1,0:T(8,128)(2,1)S(1)}, bf16[4,32,1024]{2,1,0:T(8,128)(2,1)S(1)}, u32[]{:S(2)}, u32[]{:S(2)}) collective-permute-start(bf16[4,32,1024]{2,1,0:T(8,128)(2,1)S(1)} %bitcast.25), channel_id=1, source_target_pairs={{0,1},{1,2},{2,3},{3,4},{4,5},{5,6},{8,9},{9,10},{10,11},{11,12},{... | collective-permute-start | bytes 786440 | tf_op jit(solution)/shard_map/ppermute | solution.py:25
  100.7 0.1 convert_element_type.29
  100.8 0.5 collective-permute-start.18
  101.3 1.0 collective-permute-start.15
  102.3 0.5 fusion
  102.8 3.6 %collective-permute-start.4 = (bf16[4,32,1024]{2,1,0:T(8,128)(2,1)S(1)}, bf16[4,32,1024]{2,1,0:T(8,128)(2,1)S(1)}, u32[]{:S(2)}, u32[]{:S(2)}) collective-permute-start(bf16[4,32,1024]{2,1,0:T(8,128)(2,1)S(1)} %bitcast.26), channel_id=1, source_target_pairs={{0,7},{1,0},{2,1},{3,2},{4,3},{5,4},{8,15},{9,8},{10,9},{11,10},{1... | collective-permute-start | bytes 786440 | tf_op jit(solution)/shard_map/ppermute | solution.py:25
  106.5 0.7 collective-permute-start.1
  107.2 1.4 collective-permute-done.18.refs_7_
  108.5 2.2 %collective-permute-start.19 = (bf16[256,512]{1,0:T(8,128)(2,1)S(1)}, bf16[256,512]{1,0:T(8,128)(2,1)S(1)}, u32[]{:S(2)}, u32[]{:S(2)}) collective-permute-start(bf16[256,512]{1,0:T(8,128)(2,1)S(1)} %collective-permute-done.18.refs_7_), channel_id=1, source_target_pairs={{0,7},{1,0},{2,1},{3,2},{4,3},{5,4},{6,5},{7,6},{8,15},{9,8},{10,9... | collective-permute-start | bytes 786440 | tf_op jit(solution)/shard_map/ppermute | solution.py:25
  110.7 1.2 collective-permute-done.15.refs_2_
  111.9 2.3 %collective-permute-start.16 = (bf16[256,512]{1,0:T(8,128)(2,1)S(1)}, bf16[256,512]{1,0:T(8,128)(2,1)S(1)}, u32[]{:S(2)}, u32[]{:S(2)}) collective-permute-start(bf16[256,512]{1,0:T(8,128)(2,1)S(1)} %collective-permute-done.15.refs_2_), channel_id=1, source_target_pairs={{0,1},{1,2},{2,3},{3,4},{4,5},{5,6},{6,7},{7,0},{8,9},{9,10},{10,1... | collective-permute-start | bytes 786440 | tf_op jit(solution)/shard_map/ppermute | solution.py:25
  114.2 0.4 fusion.1
  114.6 3.7 %collective-permute-start.5 = (bf16[4,32,1024]{2,1,0:T(8,128)(2,1)S(1)}, bf16[4,32,1024]{2,1,0:T(8,128)(2,1)}, u32[]{:S(2)}, u32[]{:S(2)}) collective-permute-start(bf16[4,32,1024]{2,1,0:T(8,128)(2,1)S(1)} %collective-permute-done.4.refs_7_), channel_id=1, source_target_pairs={{0,7},{1,0},{2,1},{3,2},{4,3},{7,6},{8,15},{9,8},{10,9},{11,10},{1... | collective-permute-start | bytes 786440 | tf_op jit(solution)/shard_map/ppermute | solution.py:25
  118.3 1.3 collective-permute-start.2
  119.7 0.2 collective-permute-done.19.refs_6_
  119.9 3.2 %collective-permute-start.20 = (bf16[256,512]{1,0:T(8,128)(2,1)S(1)}, bf16[256,512]{1,0:T(8,128)(2,1)S(1)}, u32[]{:S(2)}, u32[]{:S(2)}) collective-permute-start(bf16[256,512]{1,0:T(8,128)(2,1)S(1)} %collective-permute-done.19.refs_6_), channel_id=1, source_target_pairs={{0,7},{1,0},{2,1},{3,2},{4,3},{5,4},{6,5},{7,6},{8,15},{9,8},{10,9... | collective-permute-start | bytes 786440 | tf_op jit(solution)/shard_map/ppermute | solution.py:25
  123.1 0.3 collective-permute-start.17
  123.5 2.0 collective-permute-done.5.refs_6_
  125.5 3.0 %collective-permute-start.6 = (bf16[4,32,1024]{2,1,0:T(8,128)(2,1)}, bf16[4,32,1024]{2,1,0:T(8,128)(2,1)}, u32[]{:S(2)}, u32[]{:S(2)}) collective-permute-start(bf16[4,32,1024]{2,1,0:T(8,128)(2,1)} %collective-permute-done.5.refs_6_), channel_id=1, source_target_pairs={{0,7},{1,0},{2,1},{3,2},{6,5},{7,6},{8,15},{9,8},{10,9},{11,10},{1... | collective-permute-start | bytes 786440 | tf_op jit(solution)/shard_map/ppermute | solution.py:25
  128.5 2.2 %collective-permute-start.3 = (bf16[4,32,1024]{2,1,0:T(8,128)(2,1)}, bf16[4,32,1024]{2,1,0:T(8,128)(2,1)}, u32[]{:S(2)}, u32[]{:S(2)}) collective-permute-start(bf16[4,32,1024]{2,1,0:T(8,128)(2,1)} %collective-permute-done.2.refs_3_), channel_id=1, source_target_pairs={{0,1},{3,4},{4,5},{5,6},{6,7},{7,0},{8,9},{11,12},{12,13},{13,14},... | collective-permute-start | bytes 786440 | tf_op jit(solution)/shard_map/ppermute | solution.py:25
  130.8 0.8 pad_maximum_fusion.3
  131.6 0.5 broadcast.91
  132.1 0.6 reduce.3
  132.7 0.6 reshape.163.refs_10_
  133.3 0.8 pad_maximum_fusion.1
  134.2 0.6 copy-done.7
  134.8 0.1 copy-done.8
  134.9 5.2 %shard_map.104.text_ref = bf16[256,512]{1,0:T(8,128)(2,1)} custom-call(s32[1]{0:T(128)} %bitcast.13.place_ref, bf16[256,512]{1,0:T(8,128)(2,1)} %get-tuple-element.26.refs_0_, bf16[256,512]{1,0:T(8,128)(2,1)} %copy-done.2, bf16[256,512]{1,0:T(8,128)(2,1)} %copy-done.4, bf16[256,512]{1,0:T(8,128)(2,1)} %copy-done.6, bf16[256,512]{1,0:T(8,128)(2,1)} %copy-done.8, ...), custom_call_target="tpu_custom_call" | custom-call | flops 1073741824 | bytes 6291456 | tf_op jit(solution)/shard_map/pallas_call | solution.py:218
  140.2 16.0 %shard_map.101 = (bf16[6,4,32,512]{3,2,1,0:T(8,128)(2,1)}, bf16[128,4096]{1,0:T(8,128)(2,1)}) custom-call(s32[1]{0:T(128)} %bitcast.13.place_ref, bf16[4,32,1024]{2,1,0:T(8,128)(2,1)} %bitcast.27, bf16[4,32,1024]{2,1,0:T(8,128)(2,1)} %copy-done.20, bf16[4,32,1024]{2,1,0:T(8,128)(2,1)} %copy-done.22, bf16[4,32,1024]{2,1,0:T(8,128)(2,1)} %collective-permute-done.2.refs_3_, ...), custom_call_target="tpu_custom_call" | custom-call | flops 9663676416 | bytes 12582912 | tf_op jit(solution)/shard_map/pallas_call | solution.py:293
  156.3 5.8 %shard_map.105 = bf16[8,4,32,256]{3,2,1,0:T(8,128)(2,1)} custom-call(s32[3,4]{1,0:T(4,128)} %add_add_fusion.counts_ref, bf16[6,4,32,512]{3,2,1,0:T(8,128)(2,1)} %get-tuple-element.17.image_ref, bf16[256,512]{1,0:T(8,128)(2,1)} %shard_map.104.text_ref), custom_call_target="tpu_custom_call" | custom-call | flops 335544320 | bytes 2097152 | tf_op jit(solution)/shard_map/pallas_call | solution.py:373
  162.1 7.6 %all-to-all-start.2 = ((bf16[8,128,256]{2,1,0:T(8,128)(2,1)}), bf16[8,128,256]{2,1,0:T(8,128)(2,1)S(1)}, u32[]{:S(2)}, u32[]{:S(2)}) async-start(bf16[8,128,256]{2,1,0:T(8,128)(2,1)} %bitcast.22), calls=%async_computation.2 | async-start | bytes 1048576 | tf_op jit(solution)/shard_map/all_to_all | solution.py:497
  169.7 2.4 %select_select_fusion = bf16[4,32,4096]{2,1,0:T(8,128)(2,1)} fusion(bf16[4,32,4096]{2,1,0:T(8,128)(2,1)} %bitcast.23, bf16[4,32,4096]{2,1,0:T(8,128)(2,1)S(1)} %copy-done, pred[4,32]{1,0:T(4,128)(4,1)S(1)} %get-tuple-element.36, pred[4,32]{1,0:T(4,128)(4,1)S(1)} %get-tuple-element.35), kind=kLoop, calls=%fused_computation | loop fusion | flops 1048576 | bytes 3145984 | tf_op jit(solution)/shard_map/jit(_where)/select_n | solution.py:488
  172.1 14.3 %all-to-all-done.2.att_ref = bf16[8,128,256]{2,1,0:T(8,128)(2,1)S(1)} async-done(((bf16[8,128,256]{2,1,0:T(8,128)(2,1)}), bf16[8,128,256]{2,1,0:T(8,128)(2,1)S(1)}, u32[]{:S(2)}, u32[]{:S(2)}) %all-to-all-start.2) | async-done | bytes 524320 | tf_op jit(solution)/shard_map/all_to_all | solution.py:497
  186.4 0.8 copy-done.1
  187.2 8.7 %shard_map.106 = bf16[128,4096]{1,0:T(8,128)(2,1)} custom-call(bf16[8,128,256]{2,1,0:T(8,128)(2,1)} %copy-done.1, bf16[32,2048,128]{2,1,0:T(8,128)(2,1)} %bitcast.18, bf16[128,4096]{1,0:T(8,128)(2,1)} %bitcast.19), custom_call_target="tpu_custom_call" | custom-call | flops 2147483648 | bytes 16777216 | tf_op jit(solution)/shard_map/pallas_call | solution.py:423
  (66 shorter events, 0.3 us)
Async XLA Ops:
  6.5 113.1 %copy-start.18 = (s32[4]{0:T(128)S(1)}, s32[4]{0:T(128)}, u32[]{:S(2)}) copy-start(s32[4]{0:T(128)} %param.11) | copy-start | bytes 52
  6.5 113.1 %copy-start.19 = (s32[4]{0:T(128)S(1)}, s32[4]{0:T(128)}, u32[]{:S(2)}) copy-start(s32[4]{0:T(128)} %param.12) | copy-start | bytes 52
  6.5 125.5 %copy-start.17 = (f32[1,4096]{1,0:T(1,128)S(1)}, f32[1,4096]{1,0:T(1,128)}, u32[]{:S(2)}) copy-start(f32[1,4096]{1,0:T(1,128)} %refs_12_.1) | copy-start | bytes 49156
  6.5 127.6 %all-gather.5.cloned.1.call-start = ((), (), s32[]{:S(2)}) async-start(), calls=%async_computation.3 | async-start | bytes 4325376 | tf_op jit(solution)/shard_map/all_gather | solution.py:462
  7.3 179.2 %all-gather.7.cloned.1.call-start = ((), (), s32[]{:S(2)}) async-start(), calls=%async_computation.4 | async-start | bytes 17301504 | tf_op jit(solution)/shard_map/all_gather | solution.py:467
  9.7 13.3 %collective-permute-start.10 = (bf16[128,768]{1,0:T(8,128)(2,1)}, bf16[128,768]{1,0:T(8,128)(2,1)S(1)}, u32[]{:S(2)}, u32[]{:S(2)}) collective-permute-start(bf16[128,768]{1,0:T(8,128)(2,1)} %get-tuple-element.22), channel_id=1, source_target_pairs={{0,4},{1,5},{2,6},{3,7},{4,0},{5,1},{6,2},{7,3},{8,12},{9,13},{10,... | collective-permute-start | bytes 589832 | tf_op jit(solution)/shard_map/ppermute | solution.py:25
  17.5 22.9 %collective-permute-start.11 = (bf16[128,768]{1,0:T(8,128)(2,1)}, bf16[128,768]{1,0:T(8,128)(2,1)S(1)}, u32[]{:S(2)}, u32[]{:S(2)}) collective-permute-start(bf16[128,768]{1,0:T(8,128)(2,1)} %get-tuple-element.23), channel_id=1, source_target_pairs={{0,5},{1,6},{2,7},{3,0},{4,1},{5,2},{6,3},{7,4},{8,13},{9,14},{10,... | collective-permute-start | bytes 589832 | tf_op jit(solution)/shard_map/ppermute | solution.py:25
  17.5 31.2 %collective-permute-start.12 = (bf16[128,768]{1,0:T(8,128)(2,1)}, bf16[128,768]{1,0:T(8,128)(2,1)S(1)}, u32[]{:S(2)}, u32[]{:S(2)}) collective-permute-start(bf16[128,768]{1,0:T(8,128)(2,1)} %get-tuple-element.24), channel_id=1, source_target_pairs={{0,6},{1,7},{2,0},{3,1},{4,2},{5,3},{6,4},{7,5},{8,14},{9,15},{10,... | collective-permute-start | bytes 589832 | tf_op jit(solution)/shard_map/ppermute | solution.py:25
  21.5 30.9 %collective-permute-start.13 = (bf16[128,768]{1,0:T(8,128)(2,1)}, bf16[128,768]{1,0:T(8,128)(2,1)S(1)}, u32[]{:S(2)}, u32[]{:S(2)}) collective-permute-start(bf16[128,768]{1,0:T(8,128)(2,1)} %get-tuple-element.25), channel_id=1, source_target_pairs={{0,7},{1,0},{2,1},{3,2},{4,3},{5,4},{6,5},{7,6},{8,15},{9,8},{10,9... | collective-permute-start | bytes 589832 | tf_op jit(solution)/shard_map/ppermute | solution.py:25
  22.2 30.2 %collective-permute-start.7 = (bf16[128,768]{1,0:T(8,128)(2,1)}, bf16[128,768]{1,0:T(8,128)(2,1)S(1)}, u32[]{:S(2)}, u32[]{:S(2)}) collective-permute-start(bf16[128,768]{1,0:T(8,128)(2,1)} %get-tuple-element.19), channel_id=1, source_target_pairs={{0,1},{1,2},{2,3},{3,4},{4,5},{5,6},{6,7},{7,0},{8,9},{9,10},{10,1... | collective-permute-start | bytes 589832 | tf_op jit(solution)/shard_map/ppermute | solution.py:25
  23.1 32.2 %copy-start.10 = (bf16[128,768]{1,0:T(8,128)(2,1)}, bf16[128,768]{1,0:T(8,128)(2,1)S(1)}, u32[]{:S(2)}) copy-start(bf16[128,768]{1,0:T(8,128)(2,1)S(1)} %collective-permute-done.10.refs_4_) | copy-start | bytes 589828
  23.1 29.4 %collective-permute-start.8 = (bf16[128,768]{1,0:T(8,128)(2,1)}, bf16[128,768]{1,0:T(8,128)(2,1)S(1)}, u32[]{:S(2)}, u32[]{:S(2)}) collective-permute-start(bf16[128,768]{1,0:T(8,128)(2,1)} %get-tuple-element.20), channel_id=1, source_target_pairs={{0,2},{1,3},{2,4},{3,5},{4,6},{5,7},{6,0},{7,1},{8,10},{9,11},{10,... | collective-permute-start | bytes 589832 | tf_op jit(solution)/shard_map/ppermute | solution.py:25
  40.3 14.9 %copy-start.11 = (bf16[128,768]{1,0:T(8,128)(2,1)}, bf16[128,768]{1,0:T(8,128)(2,1)S(1)}, u32[]{:S(2)}) copy-start(bf16[128,768]{1,0:T(8,128)(2,1)S(1)} %collective-permute-done.11.refs_5_) | copy-start | bytes 589828
  40.3 14.9 %collective-permute-start.9 = (bf16[128,768]{1,0:T(8,128)(2,1)}, bf16[128,768]{1,0:T(8,128)(2,1)S(1)}, u32[]{:S(2)}, u32[]{:S(2)}) collective-permute-start(bf16[128,768]{1,0:T(8,128)(2,1)} %get-tuple-element.21), channel_id=1, source_target_pairs={{0,3},{1,4},{2,5},{3,6},{4,7},{5,0},{6,1},{7,2},{8,11},{9,12},{10,... | collective-permute-start | bytes 589832 | tf_op jit(solution)/shard_map/ppermute | solution.py:25
  48.7 6.6 %copy-start.12 = (bf16[128,768]{1,0:T(8,128)(2,1)}, bf16[128,768]{1,0:T(8,128)(2,1)S(1)}, u32[]{:S(2)}) copy-start(bf16[128,768]{1,0:T(8,128)(2,1)S(1)} %collective-permute-done.12.refs_6_) | copy-start | bytes 589828
  52.5 2.8 %copy-start.13 = (bf16[128,768]{1,0:T(8,128)(2,1)}, bf16[128,768]{1,0:T(8,128)(2,1)S(1)}, u32[]{:S(2)}) copy-start(bf16[128,768]{1,0:T(8,128)(2,1)S(1)} %collective-permute-done.13.refs_7_) | copy-start | bytes 589828
  52.5 2.8 %copy-start.14 = (bf16[128,768]{1,0:T(8,128)(2,1)}, bf16[128,768]{1,0:T(8,128)(2,1)S(1)}, u32[]{:S(2)}) copy-start(bf16[128,768]{1,0:T(8,128)(2,1)S(1)} %collective-permute-done.7.refs_1_) | copy-start | bytes 589828
  52.5 2.8 %copy-start.15 = (bf16[128,768]{1,0:T(8,128)(2,1)}, bf16[128,768]{1,0:T(8,128)(2,1)S(1)}, u32[]{:S(2)}) copy-start(bf16[128,768]{1,0:T(8,128)(2,1)S(1)} %collective-permute-done.8.refs_2_) | copy-start | bytes 589828
  55.2 0.7 copy-start.16
  82.4 14.9 %all-to-all-start.1 = ((bf16[32,4,1024]{2,1,0:T(4,128)(2,1)}), bf16[32,4,1024]{2,1,0:T(4,128)(2,1)S(1)}, u32[]{:S(2)}, u32[]{:S(2)}) async-start(bf16[32,4,1024]{2,1,0:T(4,128)(2,1)} %reshape.158), calls=%async_computation.1 | async-start | bytes 524288 | tf_op jit(solution)/shard_map/all_to_all | solution.py:95
  86.1 15.2 %collective-permute-start.14 = (bf16[256,512]{1,0:T(8,128)(2,1)}, bf16[256,512]{1,0:T(8,128)(2,1)S(1)}, u32[]{:S(2)}, u32[]{:S(2)}) collective-permute-start(bf16[256,512]{1,0:T(8,128)(2,1)} %get-tuple-element.26.refs_0_), channel_id=1, source_target_pairs={{0,1},{1,2},{2,3},{3,4},{4,5},{5,6},{6,7},{7,0},{8,9},{9,10},{10,1... | collective-permute-start | bytes 786440 | tf_op jit(solution)/shard_map/ppermute | solution.py:25
  97.4 42.8 %copy-start.9 = (bf16[32,4,1024]{2,0,1:T(8,128)(2,1)}, bf16[32,4,1024]{2,0,1:T(8,128)(2,1)S(1)}, u32[]{:S(2)}) copy-start(bf16[32,4,1024]{2,0,1:T(8,128)(2,1)S(1)} %copy.18) | copy-start | bytes 786436
  97.4 9.0 %collective-permute-start = (bf16[4,32,1024]{2,1,0:T(8,128)(2,1)S(1)}, bf16[4,32,1024]{2,1,0:T(8,128)(2,1)S(1)}, u32[]{:S(2)}, u32[]{:S(2)}) collective-permute-start(bf16[4,32,1024]{2,1,0:T(8,128)(2,1)S(1)} %bitcast.25), channel_id=1, source_target_pairs={{0,1},{1,2},{2,3},{3,4},{4,5},{5,6},{8,9},{9,10},{10,11},{11,12},{... | collective-permute-start | bytes 786440 | tf_op jit(solution)/shard_map/ppermute | solution.py:25
  100.8 7.7 %collective-permute-start.18 = (bf16[256,512]{1,0:T(8,128)(2,1)}, bf16[256,512]{1,0:T(8,128)(2,1)S(1)}, u32[]{:S(2)}, u32[]{:S(2)}) collective-permute-start(bf16[256,512]{1,0:T(8,128)(2,1)} %get-tuple-element.26.refs_0_), channel_id=1, source_target_pairs={{0,7},{1,0},{2,1},{3,2},{4,3},{5,4},{6,5},{7,6},{8,15},{9,8},{10,9... | collective-permute-start | bytes 786440 | tf_op jit(solution)/shard_map/ppermute | solution.py:25
  101.3 32.9 %copy-start.2 = (bf16[256,512]{1,0:T(8,128)(2,1)}, bf16[256,512]{1,0:T(8,128)(2,1)S(1)}, u32[]{:S(2)}) copy-start(bf16[256,512]{1,0:T(8,128)(2,1)S(1)} %collective-permute-done.14.refs_1_) | copy-start | bytes 786436
  101.3 10.6 %collective-permute-start.15 = (bf16[256,512]{1,0:T(8,128)(2,1)S(1)}, bf16[256,512]{1,0:T(8,128)(2,1)S(1)}, u32[]{:S(2)}, u32[]{:S(2)}) collective-permute-start(bf16[256,512]{1,0:T(8,128)(2,1)S(1)} %collective-permute-done.14.refs_1_), channel_id=1, source_target_pairs={{0,1},{1,2},{2,3},{3,4},{4,5},{5,6},{6,7},{7,0},{8,9},{9,10},{10,1... | collective-permute-start | bytes 786440 | tf_op jit(solution)/shard_map/ppermute | solution.py:25
  102.8 11.8 %collective-permute-start.4 = (bf16[4,32,1024]{2,1,0:T(8,128)(2,1)S(1)}, bf16[4,32,1024]{2,1,0:T(8,128)(2,1)S(1)}, u32[]{:S(2)}, u32[]{:S(2)}) collective-permute-start(bf16[4,32,1024]{2,1,0:T(8,128)(2,1)S(1)} %bitcast.26), channel_id=1, source_target_pairs={{0,7},{1,0},{2,1},{3,2},{4,3},{5,4},{8,15},{9,8},{10,9},{11,10},{1... | collective-permute-start | bytes 786440 | tf_op jit(solution)/shard_map/ppermute | solution.py:25
  106.4 33.8 %copy-start.20 = (bf16[4,32,1024]{2,1,0:T(8,128)(2,1)}, bf16[4,32,1024]{2,1,0:T(8,128)(2,1)S(1)}, u32[]{:S(2)}) copy-start(bf16[4,32,1024]{2,1,0:T(8,128)(2,1)S(1)} %collective-permute-done.refs_1_) | copy-start | bytes 786436
  106.5 11.9 %collective-permute-start.1 = (bf16[4,32,1024]{2,1,0:T(8,128)(2,1)S(1)}, bf16[4,32,1024]{2,1,0:T(8,128)(2,1)S(1)}, u32[]{:S(2)}, u32[]{:S(2)}) collective-permute-start(bf16[4,32,1024]{2,1,0:T(8,128)(2,1)S(1)} %collective-permute-done.refs_1_), channel_id=1, source_target_pairs={{1,2},{2,3},{3,4},{4,5},{5,6},{6,7},{9,10},{10,11},{11,12},{12,13}... | collective-permute-start | bytes 786440 | tf_op jit(solution)/shard_map/ppermute | solution.py:25
  108.5 25.7 %copy-start.3 = (bf16[256,512]{1,0:T(8,128)(2,1)}, bf16[256,512]{1,0:T(8,128)(2,1)S(1)}, u32[]{:S(2)}) copy-start(bf16[256,512]{1,0:T(8,128)(2,1)S(1)} %collective-permute-done.18.refs_7_) | copy-start | bytes 786436
  108.5 11.3 %collective-permute-start.19 = (bf16[256,512]{1,0:T(8,128)(2,1)S(1)}, bf16[256,512]{1,0:T(8,128)(2,1)S(1)}, u32[]{:S(2)}, u32[]{:S(2)}) collective-permute-start(bf16[256,512]{1,0:T(8,128)(2,1)S(1)} %collective-permute-done.18.refs_7_), channel_id=1, source_target_pairs={{0,7},{1,0},{2,1},{3,2},{4,3},{5,4},{6,5},{7,6},{8,15},{9,8},{10,9... | collective-permute-start | bytes 786440 | tf_op jit(solution)/shard_map/ppermute | solution.py:25
  111.9 22.3 %copy-start.4 = (bf16[256,512]{1,0:T(8,128)(2,1)}, bf16[256,512]{1,0:T(8,128)(2,1)S(1)}, u32[]{:S(2)}) copy-start(bf16[256,512]{1,0:T(8,128)(2,1)S(1)} %collective-permute-done.15.refs_2_) | copy-start | bytes 786436
  111.9 11.2 %collective-permute-start.16 = (bf16[256,512]{1,0:T(8,128)(2,1)S(1)}, bf16[256,512]{1,0:T(8,128)(2,1)S(1)}, u32[]{:S(2)}, u32[]{:S(2)}) collective-permute-start(bf16[256,512]{1,0:T(8,128)(2,1)S(1)} %collective-permute-done.15.refs_2_), channel_id=1, source_target_pairs={{0,1},{1,2},{2,3},{3,4},{4,5},{5,6},{6,7},{7,0},{8,9},{9,10},{10,1... | collective-permute-start | bytes 786440 | tf_op jit(solution)/shard_map/ppermute | solution.py:25
  114.6 25.6 %copy-start.21 = (bf16[4,32,1024]{2,1,0:T(8,128)(2,1)}, bf16[4,32,1024]{2,1,0:T(8,128)(2,1)S(1)}, u32[]{:S(2)}) copy-start(bf16[4,32,1024]{2,1,0:T(8,128)(2,1)S(1)} %collective-permute-done.4.refs_7_) | copy-start | bytes 786436
  114.6 10.9 %collective-permute-start.5 = (bf16[4,32,1024]{2,1,0:T(8,128)(2,1)S(1)}, bf16[4,32,1024]{2,1,0:T(8,128)(2,1)}, u32[]{:S(2)}, u32[]{:S(2)}) collective-permute-start(bf16[4,32,1024]{2,1,0:T(8,128)(2,1)S(1)} %collective-permute-done.4.refs_7_), channel_id=1, source_target_pairs={{0,7},{1,0},{2,1},{3,2},{4,3},{7,6},{8,15},{9,8},{10,9},{11,10},{1... | collective-permute-start | bytes 786440 | tf_op jit(solution)/shard_map/ppermute | solution.py:25
  118.3 21.9 %copy-start.22 = (bf16[4,32,1024]{2,1,0:T(8,128)(2,1)}, bf16[4,32,1024]{2,1,0:T(8,128)(2,1)S(1)}, u32[]{:S(2)}) copy-start(bf16[4,32,1024]{2,1,0:T(8,128)(2,1)S(1)} %collective-permute-done.1.refs_2_) | copy-start | bytes 786436
  118.3 10.2 %collective-permute-start.2 = (bf16[4,32,1024]{2,1,0:T(8,128)(2,1)S(1)}, bf16[4,32,1024]{2,1,0:T(8,128)(2,1)}, u32[]{:S(2)}, u32[]{:S(2)}) collective-permute-start(bf16[4,32,1024]{2,1,0:T(8,128)(2,1)S(1)} %collective-permute-done.1.refs_2_), channel_id=1, source_target_pairs={{2,3},{3,4},{4,5},{5,6},{6,7},{7,0},{10,11},{11,12},{12,13},{13,14... | collective-permute-start | bytes 786440 | tf_op jit(solution)/shard_map/ppermute | solution.py:25
  119.9 14.4 %copy-start.5 = (bf16[256,512]{1,0:T(8,128)(2,1)}, bf16[256,512]{1,0:T(8,128)(2,1)S(1)}, u32[]{:S(2)}) copy-start(bf16[256,512]{1,0:T(8,128)(2,1)S(1)} %collective-permute-done.19.refs_6_) | copy-start | bytes 786436
  119.9 14.3 %collective-permute-start.20 = (bf16[256,512]{1,0:T(8,128)(2,1)S(1)}, bf16[256,512]{1,0:T(8,128)(2,1)S(1)}, u32[]{:S(2)}, u32[]{:S(2)}) collective-permute-start(bf16[256,512]{1,0:T(8,128)(2,1)S(1)} %collective-permute-done.19.refs_6_), channel_id=1, source_target_pairs={{0,7},{1,0},{2,1},{3,2},{4,3},{5,4},{6,5},{7,6},{8,15},{9,8},{10,9... | collective-permute-start | bytes 786440 | tf_op jit(solution)/shard_map/ppermute | solution.py:25
  123.1 11.2 %copy-start.6 = (bf16[256,512]{1,0:T(8,128)(2,1)}, bf16[256,512]{1,0:T(8,128)(2,1)S(1)}, u32[]{:S(2)}) copy-start(bf16[256,512]{1,0:T(8,128)(2,1)S(1)} %collective-permute-done.16.refs_3_) | copy-start | bytes 786436
  123.1 11.1 %collective-permute-start.17 = (bf16[256,512]{1,0:T(8,128)(2,1)S(1)}, bf16[256,512]{1,0:T(8,128)(2,1)S(1)}, u32[]{:S(2)}, u32[]{:S(2)}) collective-permute-start(bf16[256,512]{1,0:T(8,128)(2,1)S(1)} %collective-permute-done.16.refs_3_), channel_id=1, source_target_pairs={{0,1},{1,2},{2,3},{3,4},{4,5},{5,6},{6,7},{7,0},{8,9},{9,10},{10,1... | collective-permute-start | bytes 786440 | tf_op jit(solution)/shard_map/ppermute | solution.py:25
  125.5 14.7 %collective-permute-start.6 = (bf16[4,32,1024]{2,1,0:T(8,128)(2,1)}, bf16[4,32,1024]{2,1,0:T(8,128)(2,1)}, u32[]{:S(2)}, u32[]{:S(2)}) collective-permute-start(bf16[4,32,1024]{2,1,0:T(8,128)(2,1)} %collective-permute-done.5.refs_6_), channel_id=1, source_target_pairs={{0,7},{1,0},{2,1},{3,2},{6,5},{7,6},{8,15},{9,8},{10,9},{11,10},{1... | collective-permute-start | bytes 786440 | tf_op jit(solution)/shard_map/ppermute | solution.py:25
  128.5 11.7 %collective-permute-start.3 = (bf16[4,32,1024]{2,1,0:T(8,128)(2,1)}, bf16[4,32,1024]{2,1,0:T(8,128)(2,1)}, u32[]{:S(2)}, u32[]{:S(2)}) collective-permute-start(bf16[4,32,1024]{2,1,0:T(8,128)(2,1)} %collective-permute-done.2.refs_3_), channel_id=1, source_target_pairs={{0,1},{3,4},{4,5},{5,6},{6,7},{7,0},{8,9},{11,12},{12,13},{13,14},... | collective-permute-start | bytes 786440 | tf_op jit(solution)/shard_map/ppermute | solution.py:25
  134.1 0.7 copy-start.7
  134.1 0.8 copy-start.8
  140.2 29.5 %copy-start = (bf16[4,32,4096]{2,1,0:T(8,128)(2,1)S(1)}, bf16[4,32,4096]{2,1,0:T(8,128)(2,1)}, u32[]{:S(2)}) copy-start(bf16[4,32,4096]{2,1,0:T(8,128)(2,1)} %text_ref.1) | copy-start | bytes 3145732
  162.1 24.3 %all-to-all-start.2 = ((bf16[8,128,256]{2,1,0:T(8,128)(2,1)}), bf16[8,128,256]{2,1,0:T(8,128)(2,1)S(1)}, u32[]{:S(2)}, u32[]{:S(2)}) async-start(bf16[8,128,256]{2,1,0:T(8,128)(2,1)} %bitcast.22), calls=%async_computation.2 | async-start | bytes 1048576 | tf_op jit(solution)/shard_map/all_to_all | solution.py:497
  186.4 0.8 copy-start.1
Sparse Core Ops, SparseCore 0:
  9.9 55.2 all-gather.4
  67.7 78.2 all-gather.6

commit v4 on v3

--- a/solution.py
+++ b/solution.py
@@ -186,11 +186,21 @@
 
 
 def text_kernel(place_ref, *refs):
-    parts = len(refs) - 5
+    parts = len(refs) - 7
     chunk_refs = refs[:parts]
-    cos_ref, sin_ref, gain_ref, weight_ref, out_ref = refs[parts:]
+    cos_ref, sin_ref, gain_ref, weight_hbm, out_ref, weight_ref, sems = refs[parts:]
     width = chunk_refs[0].shape[1]
     mine = place_ref[0]
+    copies = []
+    for s in range(parts):
+        begin = pl.multiple_of(lax.rem(mine + (parts - s), parts) * width, width)
+        copies.append(
+            pltpu.make_async_copy(
+                weight_hbm.at[pl.ds(begin, width)], weight_ref.at[s], sems.at[s]
+            )
+        )
+    for copy in copies:
+        copy.start()
     squares = None
     total = None
     for s, chunk_ref in enumerate(chunk_refs):
@@ -199,8 +209,8 @@
         part = jnp.sum(rows * rows, axis=1, keepdims=True)
         squares = part if squares is None else squares + part
         scaled = (rows * gain_ref[pl.ds(at, 1), :]).astype(jnp.bfloat16)
-        block = weight_ref[pl.ds(pl.multiple_of(at * width, width), width), :]
-        term = jnp.dot(scaled, block, preferred_element_type=jnp.float32)
+        copies[s].wait()
+        term = jnp.dot(scaled, weight_ref[s], preferred_element_type=jnp.float32)
         total = term if total is None else total + term
     scale = lax.rsqrt(squares * (1.0 / (parts * width)) + epsilon)
 
@@ -217,9 +227,15 @@
     whole = pl.BlockSpec(memory_space=pltpu.VMEM)
     return pl.pallas_call(
         text_kernel,
-        in_specs=[pl.BlockSpec(memory_space=pltpu.SMEM)] + [whole] * (parts + 4),
+        in_specs=[pl.BlockSpec(memory_space=pltpu.SMEM)]
+        + [whole] * (parts + 3)
+        + [pl.BlockSpec(memory_space=pl.ANY)],
         out_specs=whole,
         out_shape=jax.ShapeDtypeStruct((rows, outs), jnp.bfloat16),
+        scratch_shapes=[
+            pltpu.VMEM((parts, width, outs), jnp.bfloat16),
+            pltpu.SemaphoreType.DMA((parts,)),
+        ],
         cost_estimate=pl.CostEstimate(
             flops=2 * rows * parts * width * outs,
             bytes_accessed=2 * parts * width * (rows + outs),

time: 204 us -> 204 us (level)
  no operation moved by 1% of the time
where the time goes in v4:
time: 204 us; the launch traced here: 203 us
  starting transfers between devices  64.4 us (32%)
  waiting for transfers between devices  48.4 us (24%)
  Pallas kernels  43.3 us (21%)
  blocking collectives  17.2 us (8%)
  between operations  13.8 us (7%)
  other arithmetic  8.57 us (4%)
  local copies, waits for them, and re-layouts  7.32 us (4%)
    ppermute x21, starting transfers between devices, shifted(): return lax.ppermute(value, axis, pairs)  53.2 us
    ppermute x21, waiting for transfers between devices, shifted(): return lax.ppermute(value, axis, pairs)  25.3 us
    all_to_all x1, blocking collectives, exchange_tiles(): got = lax.all_to_all(sent, 'dp', split_axis=0, concat_axis=0, tiled=True)  17.2 us
    pallas_call x1, Pallas kernels, image_qkv_of(): pl.pallas_call(functools.partial(image_kernel, groups=groups, useful=usef...  16 us
    all_to_all x1, waiting for transfers between devices, body(): lax.all_to_all(attended.reshape(parts, each, -1), 'mp', split_axis=0, con...  14.3 us
    pallas_call x1, Pallas kernels, project_out(): pl.pallas_call(out_kernel, in_specs=[whole, pl.BlockSpec(memory_space=pl....  8.73 us
    all_to_all x1, waiting for transfers between devices, exchange_tiles(): lax.all_to_all(ordered.reshape(ranks, image_count, width), 'dp', split_ax...  8.09 us
    all_to_all x1, starting transfers between devices, body(): lax.all_to_all(attended.reshape(parts, each, -1), 'mp', split_axis=0, con...  7.51 us
  transfers between devices with their start and end apart: 25, of which 10 were waited for; matrix products, arithmetic and copies ran while one was open for 7% of the time, Pallas kernels for 17%

profile of v4, /device:TPU:1, one launch (start us, length us, event | category | flops | bytes accessed | tf_op | source)
XLA Modules:
  0.0 203.1 jit_solution(10444716998169962194)
XLA Ops:
  6.5 0.7 all-gather.5.cloned.1.call-update
  7.3 2.4 %shard_map.102 = (bf16[128,768]{1,0:T(8,128)(2,1)}, bf16[128,768]{1,0:T(8,128)(2,1)}, bf16[128,768]{1,0:T(8,128)(2,1)}, bf16[128,768]{1,0:T(8,128)(2,1)}, bf16[1...) custom-call(s32[1]{0:T(128)} %bitcast.13.place_ref, ...), custom_call_target="tpu_custom_call" | custom-call | flops 1048576 | bytes 3145728 | tf_op jit(solution)/shard_map/pallas_call | solution.py:127
  9.7 7.7 %collective-permute-start.10 = (bf16[128,768]{1,0:T(8,128)(2,1)}, bf16[128,768]{1,0:T(8,128)(2,1)S(1)}, u32[]{:S(2)}, u32[]{:S(2)}) collective-permute-start(bf16[128,768]{1,0:T(8,128)(2,1)} %get-tuple-element.22), channel_id=1, source_target_pairs={{0,4},{1,5},{2,6},{3,7},{4,0},{5,1},{6,2},{7,3},{8,12},{9,13},{10,... | collective-permute-start | bytes 589832 | tf_op jit(solution)/shard_map/ppermute | solution.py:25
  17.5 4.0 %collective-permute-start.12 = (bf16[128,768]{1,0:T(8,128)(2,1)}, bf16[128,768]{1,0:T(8,128)(2,1)S(1)}, u32[]{:S(2)}, u32[]{:S(2)}) collective-permute-start(bf16[128,768]{1,0:T(8,128)(2,1)} %get-tuple-element.24), channel_id=1, source_target_pairs={{0,6},{1,7},{2,0},{3,1},{4,2},{5,3},{6,4},{7,5},{8,14},{9,15},{10,... | collective-permute-start | bytes 589832 | tf_op jit(solution)/shard_map/ppermute | solution.py:25
  21.5 0.7 collective-permute-start.13
  22.2 0.7 collective-permute-start.7
  23.0 0.1 pad.12.clone
  23.1 5.0 %collective-permute-start.8 = (bf16[128,768]{1,0:T(8,128)(2,1)}, bf16[128,768]{1,0:T(8,128)(2,1)S(1)}, u32[]{:S(2)}, u32[]{:S(2)}) collective-permute-start(bf16[128,768]{1,0:T(8,128)(2,1)} %get-tuple-element.20), channel_id=1, source_target_pairs={{0,2},{1,3},{2,4},{3,5},{4,6},{5,7},{6,0},{7,1},{8,10},{9,11},{10,... | collective-permute-start | bytes 589832 | tf_op jit(solution)/shard_map/ppermute | solution.py:25
  28.1 12.2 %collective-permute-done.11.refs_5_ = bf16[128,768]{1,0:T(8,128)(2,1)S(1)} collective-permute-done((bf16[128,768]{1,0:T(8,128)(2,1)}, bf16[128,768]{1,0:T(8,128)(2,1)S(1)}, u32[]{:S(2)}, u32[]{:S(2)}) %collective-permute-start.11) | collective-permute-done | bytes 196640 | tf_op jit(solution)/shard_map/ppermute | solution.py:25
  40.3 5.3 %collective-permute-start.9 = (bf16[128,768]{1,0:T(8,128)(2,1)}, bf16[128,768]{1,0:T(8,128)(2,1)S(1)}, u32[]{:S(2)}, u32[]{:S(2)}) collective-permute-start(bf16[128,768]{1,0:T(8,128)(2,1)} %get-tuple-element.21), channel_id=1, source_target_pairs={{0,3},{1,4},{2,5},{3,6},{4,7},{5,0},{6,1},{7,2},{8,11},{9,12},{10,... | collective-permute-start | bytes 589832 | tf_op jit(solution)/shard_map/ppermute | solution.py:25
  45.6 1.3 add_add_fusion.counts_ref
  46.9 1.7 collective-permute-done.12.refs_6_
  48.7 3.8 %collective-permute-done.13.refs_7_ = bf16[128,768]{1,0:T(8,128)(2,1)S(1)} collective-permute-done((bf16[128,768]{1,0:T(8,128)(2,1)}, bf16[128,768]{1,0:T(8,128)(2,1)S(1)}, u32[]{:S(2)}, u32[]{:S(2)}) %collective-permute-start.13) | collective-permute-done | bytes 196640 | tf_op jit(solution)/shard_map/ppermute | solution.py:25
  52.5 2.8 %collective-permute-done.9.refs_3_ = bf16[128,768]{1,0:T(8,128)(2,1)S(1)} collective-permute-done((bf16[128,768]{1,0:T(8,128)(2,1)}, bf16[128,768]{1,0:T(8,128)(2,1)S(1)}, u32[]{:S(2)}, u32[]{:S(2)}) %collective-permute-start.9) | collective-permute-done | bytes 196640 | tf_op jit(solution)/shard_map/ppermute | solution.py:25
  55.3 0.6 copy-done.16
  55.9 2.6 %shard_map.103 = (bf16[256,512]{1,0:T(8,128)(2,1)}, bf16[2048,128]{1,0:T(8,128)(2,1)}) custom-call(s32[3,4]{1,0:T(4,128)} %add_add_fusion.counts_ref, bf16[128,768]{1,0:T(8,128)(2,1)} %get-tuple-element.18.refs_0_, bf16[128,768]{1,0:T(8,128)(2,1)} %copy-done.14, bf16[128,768]{1,0:T(8,128)(2,1)} %copy-done.15, bf16[128,768]{1,0:T(8,128)(2,1)} %copy-done.16, ...), custom_call_target="tpu_custom_call" | custom-call | flops 67108864 | bytes 1572864 | tf_op jit(solution)/shard_map/pallas_call | solution.py:171
  58.5 1.2 copy.19
  59.7 0.7 convert_element_type.26
  60.4 0.1 broadcast_in_dim.16
  60.5 0.1 pad_maximum_fusion
  60.6 17.2 %all_to_all.15 = bf16[32,4,1152]{2,1,0:T(4,128)(2,1)S(1)} all-to-all(bf16[32,4,1152]{2,1,0:T(4,128)(2,1)S(1)} %pad_maximum_fusion), channel_id=1, replica_groups=mesh['dp'=32,'mp'=8] {'dp'}, dimensions={0} | all-to-all | bytes 589824 | tf_op jit(solution)/shard_map/all_to_all | solution.py:86
  77.8 0.8 reshape.157.got_ref
  78.6 2.1 %shard_map.100 = bf16[128,1024]{1,0:T(8,128)(2,1)} custom-call(bf16[128,1152]{1,0:T(8,128)(2,1)} %reshape.157.got_ref), custom_call_target="tpu_custom_call" | custom-call | flops 33554432 | bytes 524288 | tf_op jit(solution)/shard_map/pallas_call | solution.py:88
  80.7 1.8 reshape.158
  82.4 3.7 %all-to-all-start.1 = ((bf16[32,4,1024]{2,1,0:T(4,128)(2,1)}), bf16[32,4,1024]{2,1,0:T(4,128)(2,1)S(1)}, u32[]{:S(2)}, u32[]{:S(2)}) async-start(bf16[32,4,1024]{2,1,0:T(4,128)(2,1)} %reshape.158), calls=%async_computation.1 | async-start | bytes 524288 | tf_op jit(solution)/shard_map/all_to_all | solution.py:95
  86.1 2.4 %collective-permute-start.14 = (bf16[256,512]{1,0:T(8,128)(2,1)}, bf16[256,512]{1,0:T(8,128)(2,1)S(1)}, u32[]{:S(2)}, u32[]{:S(2)}) collective-permute-start(bf16[256,512]{1,0:T(8,128)(2,1)} %get-tuple-element.26.refs_0_), channel_id=1, source_target_pairs={{0,1},{1,2},{2,3},{3,4},{4,5},{5,6},{6,7},{7,0},{8,9},{9,10},{10,1... | collective-permute-start | bytes 786440 | tf_op jit(solution)/shard_map/ppermute | solution.py:25
  88.5 0.7 add_convert_fusion.1
  89.2 8.1 %all-to-all-done.1 = bf16[32,4,1024]{2,1,0:T(4,128)(2,1)S(1)} async-done(((bf16[32,4,1024]{2,1,0:T(4,128)(2,1)}), bf16[32,4,1024]{2,1,0:T(4,128)(2,1)S(1)}, u32[]{:S(2)}, u32[]{:S(2)}) %all-to-all-start.1) | async-done | bytes 262176 | tf_op jit(solution)/shard_map/all_to_all | solution.py:95
  97.3 0.1 copy.18
  97.4 3.3 %collective-permute-start = (bf16[4,32,1024]{2,1,0:T(8,128)(2,1)S(1)}, bf16[4,32,1024]{2,1,0:T(8,128)(2,1)S(1)}, u32[]{:S(2)}, u32[]{:S(2)}) collective-permute-start(bf16[4,32,1024]{2,1,0:T(8,128)(2,1)S(1)} %bitcast.25), channel_id=1, source_target_pairs={{0,1},{1,2},{2,3},{3,4},{4,5},{5,6},{8,9},{9,10},{10,11},{11,12},{... | collective-permute-start | bytes 786440 | tf_op jit(solution)/shard_map/ppermute | solution.py:25
  100.7 0.1 convert_element_type.29
  100.8 0.5 collective-permute-start.18
  101.3 1.0 collective-permute-start.15
  102.3 0.5 fusion
  102.8 3.6 %collective-permute-start.4 = (bf16[4,32,1024]{2,1,0:T(8,128)(2,1)S(1)}, bf16[4,32,1024]{2,1,0:T(8,128)(2,1)S(1)}, u32[]{:S(2)}, u32[]{:S(2)}) collective-permute-start(bf16[4,32,1024]{2,1,0:T(8,128)(2,1)S(1)} %bitcast.26), channel_id=1, source_target_pairs={{0,7},{1,0},{2,1},{3,2},{4,3},{5,4},{8,15},{9,8},{10,9},{11,10},{1... | collective-permute-start | bytes 786440 | tf_op jit(solution)/shard_map/ppermute | solution.py:25
  106.5 0.7 collective-permute-start.1
  107.2 1.4 collective-permute-done.18.refs_7_
  108.5 2.2 %collective-permute-start.19 = (bf16[256,512]{1,0:T(8,128)(2,1)S(1)}, bf16[256,512]{1,0:T(8,128)(2,1)S(1)}, u32[]{:S(2)}, u32[]{:S(2)}) collective-permute-start(bf16[256,512]{1,0:T(8,128)(2,1)S(1)} %collective-permute-done.18.refs_7_), channel_id=1, source_target_pairs={{0,7},{1,0},{2,1},{3,2},{4,3},{5,4},{6,5},{7,6},{8,15},{9,8},{10,9... | collective-permute-start | bytes 786440 | tf_op jit(solution)/shard_map/ppermute | solution.py:25
  110.7 1.2 collective-permute-done.15.refs_2_
  111.9 2.3 %collective-permute-start.16 = (bf16[256,512]{1,0:T(8,128)(2,1)S(1)}, bf16[256,512]{1,0:T(8,128)(2,1)S(1)}, u32[]{:S(2)}, u32[]{:S(2)}) collective-permute-start(bf16[256,512]{1,0:T(8,128)(2,1)S(1)} %collective-permute-done.15.refs_2_), channel_id=1, source_target_pairs={{0,1},{1,2},{2,3},{3,4},{4,5},{5,6},{6,7},{7,0},{8,9},{9,10},{10,1... | collective-permute-start | bytes 786440 | tf_op jit(solution)/shard_map/ppermute | solution.py:25
  114.2 0.4 fusion.1
  114.6 3.7 %collective-permute-start.5 = (bf16[4,32,1024]{2,1,0:T(8,128)(2,1)S(1)}, bf16[4,32,1024]{2,1,0:T(8,128)(2,1)}, u32[]{:S(2)}, u32[]{:S(2)}) collective-permute-start(bf16[4,32,1024]{2,1,0:T(8,128)(2,1)S(1)} %collective-permute-done.4.refs_7_), channel_id=1, source_target_pairs={{0,7},{1,0},{2,1},{3,2},{4,3},{7,6},{8,15},{9,8},{10,9},{11,10},{1... | collective-permute-start | bytes 786440 | tf_op jit(solution)/shard_map/ppermute | solution.py:25
  118.3 1.3 collective-permute-start.2
  119.7 0.2 collective-permute-done.19.refs_6_
  119.9 3.2 %collective-permute-start.20 = (bf16[256,512]{1,0:T(8,128)(2,1)S(1)}, bf16[256,512]{1,0:T(8,128)(2,1)S(1)}, u32[]{:S(2)}, u32[]{:S(2)}) collective-permute-start(bf16[256,512]{1,0:T(8,128)(2,1)S(1)} %collective-permute-done.19.refs_6_), channel_id=1, source_target_pairs={{0,7},{1,0},{2,1},{3,2},{4,3},{5,4},{6,5},{7,6},{8,15},{9,8},{10,9... | collective-permute-start | bytes 786440 | tf_op jit(solution)/shard_map/ppermute | solution.py:25
  123.1 0.3 collective-permute-start.17
  123.5 2.0 collective-permute-done.5.refs_6_
  125.5 3.0 %collective-permute-start.6 = (bf16[4,32,1024]{2,1,0:T(8,128)(2,1)}, bf16[4,32,1024]{2,1,0:T(8,128)(2,1)}, u32[]{:S(2)}, u32[]{:S(2)}) collective-permute-start(bf16[4,32,1024]{2,1,0:T(8,128)(2,1)} %collective-permute-done.5.refs_6_), channel_id=1, source_target_pairs={{0,7},{1,0},{2,1},{3,2},{6,5},{7,6},{8,15},{9,8},{10,9},{11,10},{1... | collective-permute-start | bytes 786440 | tf_op jit(solution)/shard_map/ppermute | solution.py:25
  128.5 2.2 %collective-permute-start.3 = (bf16[4,32,1024]{2,1,0:T(8,128)(2,1)}, bf16[4,32,1024]{2,1,0:T(8,128)(2,1)}, u32[]{:S(2)}, u32[]{:S(2)}) collective-permute-start(bf16[4,32,1024]{2,1,0:T(8,128)(2,1)} %collective-permute-done.2.refs_3_), channel_id=1, source_target_pairs={{0,1},{3,4},{4,5},{5,6},{6,7},{7,0},{8,9},{11,12},{12,13},{13,14},... | collective-permute-start | bytes 786440 | tf_op jit(solution)/shard_map/ppermute | solution.py:25
  130.8 0.8 pad_maximum_fusion.3
  131.6 0.5 broadcast.91
  132.1 0.6 reduce.3
  132.7 0.6 reshape.163.refs_10_
  133.3 0.8 pad_maximum_fusion.1
  134.2 0.6 copy-done.7
  134.8 0.1 copy-done.8
  134.9 5.6 %shard_map.104.text_ref = bf16[256,512]{1,0:T(8,128)(2,1)} custom-call(s32[1]{0:T(128)} %bitcast.13.place_ref, bf16[256,512]{1,0:T(8,128)(2,1)} %get-tuple-element.26.refs_0_, bf16[256,512]{1,0:T(8,128)(2,1)} %copy-done.2, bf16[256,512]{1,0:T(8,128)(2,1)} %copy-done.4, bf16[256,512]{1,0:T(8,128)(2,1)} %copy-done.6, bf16[256,512]{1,0:T(8,128)(2,1)} %copy-done.8, ...), custom_call_target="tpu_custom_call" | custom-call | flops 1073741824 | bytes 6291456 | tf_op jit(solution)/shard_map/pallas_call | solution.py:228
  140.6 16.0 %shard_map.101 = (bf16[6,4,32,512]{3,2,1,0:T(8,128)(2,1)}, bf16[128,4096]{1,0:T(8,128)(2,1)}) custom-call(s32[1]{0:T(128)} %bitcast.13.place_ref, bf16[4,32,1024]{2,1,0:T(8,128)(2,1)} %bitcast.27, bf16[4,32,1024]{2,1,0:T(8,128)(2,1)} %copy-done.20, bf16[4,32,1024]{2,1,0:T(8,128)(2,1)} %copy-done.22, bf16[4,32,1024]{2,1,0:T(8,128)(2,1)} %collective-permute-done.2.refs_3_, ...), custom_call_target="tpu_custom_call" | custom-call | flops 9663676416 | bytes 12582912 | tf_op jit(solution)/shard_map/pallas_call | solution.py:309
  156.6 5.8 %shard_map.105 = bf16[8,4,32,256]{3,2,1,0:T(8,128)(2,1)} custom-call(s32[3,4]{1,0:T(4,128)} %add_add_fusion.counts_ref, bf16[6,4,32,512]{3,2,1,0:T(8,128)(2,1)} %get-tuple-element.17.image_ref, bf16[256,512]{1,0:T(8,128)(2,1)} %shard_map.104.text_ref), custom_call_target="tpu_custom_call" | custom-call | flops 335544320 | bytes 2097152 | tf_op jit(solution)/shard_map/pallas_call | solution.py:389
  162.4 7.5 %all-to-all-start.2 = ((bf16[8,128,256]{2,1,0:T(8,128)(2,1)}), bf16[8,128,256]{2,1,0:T(8,128)(2,1)S(1)}, u32[]{:S(2)}, u32[]{:S(2)}) async-start(bf16[8,128,256]{2,1,0:T(8,128)(2,1)} %bitcast.22), calls=%async_computation.2 | async-start | bytes 1048576 | tf_op jit(solution)/shard_map/all_to_all | solution.py:513
  169.9 2.4 %select_select_fusion = bf16[4,32,4096]{2,1,0:T(8,128)(2,1)} fusion(bf16[4,32,4096]{2,1,0:T(8,128)(2,1)} %bitcast.23, bf16[4,32,4096]{2,1,0:T(8,128)(2,1)S(1)} %copy-done, pred[4,32]{1,0:T(4,128)(4,1)S(1)} %get-tuple-element.36, pred[4,32]{1,0:T(4,128)(4,1)S(1)} %get-tuple-element.35), kind=kLoop, calls=%fused_computation | loop fusion | flops 1048576 | bytes 3145984 | tf_op jit(solution)/shard_map/jit(_where)/select_n | solution.py:504
  172.4 14.3 %all-to-all-done.2.att_ref = bf16[8,128,256]{2,1,0:T(8,128)(2,1)S(1)} async-done(((bf16[8,128,256]{2,1,0:T(8,128)(2,1)}), bf16[8,128,256]{2,1,0:T(8,128)(2,1)S(1)}, u32[]{:S(2)}, u32[]{:S(2)}) %all-to-all-start.2) | async-done | bytes 524320 | tf_op jit(solution)/shard_map/all_to_all | solution.py:513
  186.7 0.8 copy-done.1
  187.5 8.7 %shard_map.106 = bf16[128,4096]{1,0:T(8,128)(2,1)} custom-call(bf16[8,128,256]{2,1,0:T(8,128)(2,1)} %copy-done.1, bf16[32,2048,128]{2,1,0:T(8,128)(2,1)} %bitcast.18, bf16[128,4096]{1,0:T(8,128)(2,1)} %bitcast.19), custom_call_target="tpu_custom_call" | custom-call | flops 2147483648 | bytes 16777216 | tf_op jit(solution)/shard_map/pallas_call | solution.py:439
  (66 shorter events, 0.3 us)
Async XLA Ops:
  6.5 113.1 %copy-start.18 = (s32[4]{0:T(128)S(1)}, s32[4]{0:T(128)}, u32[]{:S(2)}) copy-start(s32[4]{0:T(128)} %param.11) | copy-start | bytes 52
  6.5 113.1 %copy-start.19 = (s32[4]{0:T(128)S(1)}, s32[4]{0:T(128)}, u32[]{:S(2)}) copy-start(s32[4]{0:T(128)} %param.12) | copy-start | bytes 52
  6.5 125.5 %copy-start.17 = (f32[1,4096]{1,0:T(1,128)S(1)}, f32[1,4096]{1,0:T(1,128)}, u32[]{:S(2)}) copy-start(f32[1,4096]{1,0:T(1,128)} %refs_12_.1) | copy-start | bytes 49156
  6.5 127.6 %all-gather.5.cloned.1.call-start = ((), (), s32[]{:S(2)}) async-start(), calls=%async_computation.3 | async-start | bytes 4325376 | tf_op jit(solution)/shard_map/all_gather | solution.py:478
  7.3 179.4 %all-gather.7.cloned.1.call-start = ((), (), s32[]{:S(2)}) async-start(), calls=%async_computation.4 | async-start | bytes 17301504 | tf_op jit(solution)/shard_map/all_gather | solution.py:483
  9.7 13.3 %collective-permute-start.10 = (bf16[128,768]{1,0:T(8,128)(2,1)}, bf16[128,768]{1,0:T(8,128)(2,1)S(1)}, u32[]{:S(2)}, u32[]{:S(2)}) collective-permute-start(bf16[128,768]{1,0:T(8,128)(2,1)} %get-tuple-element.22), channel_id=1, source_target_pairs={{0,4},{1,5},{2,6},{3,7},{4,0},{5,1},{6,2},{7,3},{8,12},{9,13},{10,... | collective-permute-start | bytes 589832 | tf_op jit(solution)/shard_map/ppermute | solution.py:25
  17.5 22.9 %collective-permute-start.11 = (bf16[128,768]{1,0:T(8,128)(2,1)}, bf16[128,768]{1,0:T(8,128)(2,1)S(1)}, u32[]{:S(2)}, u32[]{:S(2)}) collective-permute-start(bf16[128,768]{1,0:T(8,128)(2,1)} %get-tuple-element.23), channel_id=1, source_target_pairs={{0,5},{1,6},{2,7},{3,0},{4,1},{5,2},{6,3},{7,4},{8,13},{9,14},{10,... | collective-permute-start | bytes 589832 | tf_op jit(solution)/shard_map/ppermute | solution.py:25
  17.5 31.2 %collective-permute-start.12 = (bf16[128,768]{1,0:T(8,128)(2,1)}, bf16[128,768]{1,0:T(8,128)(2,1)S(1)}, u32[]{:S(2)}, u32[]{:S(2)}) collective-permute-start(bf16[128,768]{1,0:T(8,128)(2,1)} %get-tuple-element.24), channel_id=1, source_target_pairs={{0,6},{1,7},{2,0},{3,1},{4,2},{5,3},{6,4},{7,5},{8,14},{9,15},{10,... | collective-permute-start | bytes 589832 | tf_op jit(solution)/shard_map/ppermute | solution.py:25
  21.5 30.9 %collective-permute-start.13 = (bf16[128,768]{1,0:T(8,128)(2,1)}, bf16[128,768]{1,0:T(8,128)(2,1)S(1)}, u32[]{:S(2)}, u32[]{:S(2)}) collective-permute-start(bf16[128,768]{1,0:T(8,128)(2,1)} %get-tuple-element.25), channel_id=1, source_target_pairs={{0,7},{1,0},{2,1},{3,2},{4,3},{5,4},{6,5},{7,6},{8,15},{9,8},{10,9... | collective-permute-start | bytes 589832 | tf_op jit(solution)/shard_map/ppermute | solution.py:25
  22.2 30.2 %collective-permute-start.7 = (bf16[128,768]{1,0:T(8,128)(2,1)}, bf16[128,768]{1,0:T(8,128)(2,1)S(1)}, u32[]{:S(2)}, u32[]{:S(2)}) collective-permute-start(bf16[128,768]{1,0:T(8,128)(2,1)} %get-tuple-element.19), channel_id=1, source_target_pairs={{0,1},{1,2},{2,3},{3,4},{4,5},{5,6},{6,7},{7,0},{8,9},{9,10},{10,1... | collective-permute-start | bytes 589832 | tf_op jit(solution)/shard_map/ppermute | solution.py:25
  23.1 32.2 %copy-start.10 = (bf16[128,768]{1,0:T(8,128)(2,1)}, bf16[128,768]{1,0:T(8,128)(2,1)S(1)}, u32[]{:S(2)}) copy-start(bf16[128,768]{1,0:T(8,128)(2,1)S(1)} %collective-permute-done.10.refs_4_) | copy-start | bytes 589828
  23.1 29.4 %collective-permute-start.8 = (bf16[128,768]{1,0:T(8,128)(2,1)}, bf16[128,768]{1,0:T(8,128)(2,1)S(1)}, u32[]{:S(2)}, u32[]{:S(2)}) collective-permute-start(bf16[128,768]{1,0:T(8,128)(2,1)} %get-tuple-element.20), channel_id=1, source_target_pairs={{0,2},{1,3},{2,4},{3,5},{4,6},{5,7},{6,0},{7,1},{8,10},{9,11},{10,... | collective-permute-start | bytes 589832 | tf_op jit(solution)/shard_map/ppermute | solution.py:25
  40.3 14.9 %copy-start.11 = (bf16[128,768]{1,0:T(8,128)(2,1)}, bf16[128,768]{1,0:T(8,128)(2,1)S(1)}, u32[]{:S(2)}) copy-start(bf16[128,768]{1,0:T(8,128)(2,1)S(1)} %collective-permute-done.11.refs_5_) | copy-start | bytes 589828
  40.3 14.9 %collective-permute-start.9 = (bf16[128,768]{1,0:T(8,128)(2,1)}, bf16[128,768]{1,0:T(8,128)(2,1)S(1)}, u32[]{:S(2)}, u32[]{:S(2)}) collective-permute-start(bf16[128,768]{1,0:T(8,128)(2,1)} %get-tuple-element.21), channel_id=1, source_target_pairs={{0,3},{1,4},{2,5},{3,6},{4,7},{5,0},{6,1},{7,2},{8,11},{9,12},{10,... | collective-permute-start | bytes 589832 | tf_op jit(solution)/shard_map/ppermute | solution.py:25
  48.7 6.6 %copy-start.12 = (bf16[128,768]{1,0:T(8,128)(2,1)}, bf16[128,768]{1,0:T(8,128)(2,1)S(1)}, u32[]{:S(2)}) copy-start(bf16[128,768]{1,0:T(8,128)(2,1)S(1)} %collective-permute-done.12.refs_6_) | copy-start | bytes 589828
  52.5 2.8 %copy-start.13 = (bf16[128,768]{1,0:T(8,128)(2,1)}, bf16[128,768]{1,0:T(8,128)(2,1)S(1)}, u32[]{:S(2)}) copy-start(bf16[128,768]{1,0:T(8,128)(2,1)S(1)} %collective-permute-done.13.refs_7_) | copy-start | bytes 589828
  52.5 2.8 %copy-start.14 = (bf16[128,768]{1,0:T(8,128)(2,1)}, bf16[128,768]{1,0:T(8,128)(2,1)S(1)}, u32[]{:S(2)}) copy-start(bf16[128,768]{1,0:T(8,128)(2,1)S(1)} %collective-permute-done.7.refs_1_) | copy-start | bytes 589828
  52.5 2.8 %copy-start.15 = (bf16[128,768]{1,0:T(8,128)(2,1)}, bf16[128,768]{1,0:T(8,128)(2,1)S(1)}, u32[]{:S(2)}) copy-start(bf16[128,768]{1,0:T(8,128)(2,1)S(1)} %collective-permute-done.8.refs_2_) | copy-start | bytes 589828
  55.2 0.7 copy-start.16
  82.4 14.9 %all-to-all-start.1 = ((bf16[32,4,1024]{2,1,0:T(4,128)(2,1)}), bf16[32,4,1024]{2,1,0:T(4,128)(2,1)S(1)}, u32[]{:S(2)}, u32[]{:S(2)}) async-start(bf16[32,4,1024]{2,1,0:T(4,128)(2,1)} %reshape.158), calls=%async_computation.1 | async-start | bytes 524288 | tf_op jit(solution)/shard_map/all_to_all | solution.py:95
  86.1 15.2 %collective-permute-start.14 = (bf16[256,512]{1,0:T(8,128)(2,1)}, bf16[256,512]{1,0:T(8,128)(2,1)S(1)}, u32[]{:S(2)}, u32[]{:S(2)}) collective-permute-start(bf16[256,512]{1,0:T(8,128)(2,1)} %get-tuple-element.26.refs_0_), channel_id=1, source_target_pairs={{0,1},{1,2},{2,3},{3,4},{4,5},{5,6},{6,7},{7,0},{8,9},{9,10},{10,1... | collective-permute-start | bytes 786440 | tf_op jit(solution)/shard_map/ppermute | solution.py:25
  97.4 43.1 %copy-start.9 = (bf16[32,4,1024]{2,0,1:T(8,128)(2,1)}, bf16[32,4,1024]{2,0,1:T(8,128)(2,1)S(1)}, u32[]{:S(2)}) copy-start(bf16[32,4,1024]{2,0,1:T(8,128)(2,1)S(1)} %copy.18) | copy-start | bytes 786436
  97.4 9.0 %collective-permute-start = (bf16[4,32,1024]{2,1,0:T(8,128)(2,1)S(1)}, bf16[4,32,1024]{2,1,0:T(8,128)(2,1)S(1)}, u32[]{:S(2)}, u32[]{:S(2)}) collective-permute-start(bf16[4,32,1024]{2,1,0:T(8,128)(2,1)S(1)} %bitcast.25), channel_id=1, source_target_pairs={{0,1},{1,2},{2,3},{3,4},{4,5},{5,6},{8,9},{9,10},{10,11},{11,12},{... | collective-permute-start | bytes 786440 | tf_op jit(solution)/shard_map/ppermute | solution.py:25
  100.8 7.7 %collective-permute-start.18 = (bf16[256,512]{1,0:T(8,128)(2,1)}, bf16[256,512]{1,0:T(8,128)(2,1)S(1)}, u32[]{:S(2)}, u32[]{:S(2)}) collective-permute-start(bf16[256,512]{1,0:T(8,128)(2,1)} %get-tuple-element.26.refs_0_), channel_id=1, source_target_pairs={{0,7},{1,0},{2,1},{3,2},{4,3},{5,4},{6,5},{7,6},{8,15},{9,8},{10,9... | collective-permute-start | bytes 786440 | tf_op jit(solution)/shard_map/ppermute | solution.py:25
  101.3 32.9 %copy-start.2 = (bf16[256,512]{1,0:T(8,128)(2,1)}, bf16[256,512]{1,0:T(8,128)(2,1)S(1)}, u32[]{:S(2)}) copy-start(bf16[256,512]{1,0:T(8,128)(2,1)S(1)} %collective-permute-done.14.refs_1_) | copy-start | bytes 786436
  101.3 10.6 %collective-permute-start.15 = (bf16[256,512]{1,0:T(8,128)(2,1)S(1)}, bf16[256,512]{1,0:T(8,128)(2,1)S(1)}, u32[]{:S(2)}, u32[]{:S(2)}) collective-permute-start(bf16[256,512]{1,0:T(8,128)(2,1)S(1)} %collective-permute-done.14.refs_1_), channel_id=1, source_target_pairs={{0,1},{1,2},{2,3},{3,4},{4,5},{5,6},{6,7},{7,0},{8,9},{9,10},{10,1... | collective-permute-start | bytes 786440 | tf_op jit(solution)/shard_map/ppermute | solution.py:25
  102.8 11.8 %collective-permute-start.4 = (bf16[4,32,1024]{2,1,0:T(8,128)(2,1)S(1)}, bf16[4,32,1024]{2,1,0:T(8,128)(2,1)S(1)}, u32[]{:S(2)}, u32[]{:S(2)}) collective-permute-start(bf16[4,32,1024]{2,1,0:T(8,128)(2,1)S(1)} %bitcast.26), channel_id=1, source_target_pairs={{0,7},{1,0},{2,1},{3,2},{4,3},{5,4},{8,15},{9,8},{10,9},{11,10},{1... | collective-permute-start | bytes 786440 | tf_op jit(solution)/shard_map/ppermute | solution.py:25
  106.4 34.1 %copy-start.20 = (bf16[4,32,1024]{2,1,0:T(8,128)(2,1)}, bf16[4,32,1024]{2,1,0:T(8,128)(2,1)S(1)}, u32[]{:S(2)}) copy-start(bf16[4,32,1024]{2,1,0:T(8,128)(2,1)S(1)} %collective-permute-done.refs_1_) | copy-start | bytes 786436
  106.5 11.9 %collective-permute-start.1 = (bf16[4,32,1024]{2,1,0:T(8,128)(2,1)S(1)}, bf16[4,32,1024]{2,1,0:T(8,128)(2,1)S(1)}, u32[]{:S(2)}, u32[]{:S(2)}) collective-permute-start(bf16[4,32,1024]{2,1,0:T(8,128)(2,1)S(1)} %collective-permute-done.refs_1_), channel_id=1, source_target_pairs={{1,2},{2,3},{3,4},{4,5},{5,6},{6,7},{9,10},{10,11},{11,12},{12,13}... | collective-permute-start | bytes 786440 | tf_op jit(solution)/shard_map/ppermute | solution.py:25
  108.5 25.7 %copy-start.3 = (bf16[256,512]{1,0:T(8,128)(2,1)}, bf16[256,512]{1,0:T(8,128)(2,1)S(1)}, u32[]{:S(2)}) copy-start(bf16[256,512]{1,0:T(8,128)(2,1)S(1)} %collective-permute-done.18.refs_7_) | copy-start | bytes 786436
  108.5 11.3 %collective-permute-start.19 = (bf16[256,512]{1,0:T(8,128)(2,1)S(1)}, bf16[256,512]{1,0:T(8,128)(2,1)S(1)}, u32[]{:S(2)}, u32[]{:S(2)}) collective-permute-start(bf16[256,512]{1,0:T(8,128)(2,1)S(1)} %collective-permute-done.18.refs_7_), channel_id=1, source_target_pairs={{0,7},{1,0},{2,1},{3,2},{4,3},{5,4},{6,5},{7,6},{8,15},{9,8},{10,9... | collective-permute-start | bytes 786440 | tf_op jit(solution)/shard_map/ppermute | solution.py:25
  111.9 22.3 %copy-start.4 = (bf16[256,512]{1,0:T(8,128)(2,1)}, bf16[256,512]{1,0:T(8,128)(2,1)S(1)}, u32[]{:S(2)}) copy-start(bf16[256,512]{1,0:T(8,128)(2,1)S(1)} %collective-permute-done.15.refs_2_) | copy-start | bytes 786436
  111.9 11.2 %collective-permute-start.16 = (bf16[256,512]{1,0:T(8,128)(2,1)S(1)}, bf16[256,512]{1,0:T(8,128)(2,1)S(1)}, u32[]{:S(2)}, u32[]{:S(2)}) collective-permute-start(bf16[256,512]{1,0:T(8,128)(2,1)S(1)} %collective-permute-done.15.refs_2_), channel_id=1, source_target_pairs={{0,1},{1,2},{2,3},{3,4},{4,5},{5,6},{6,7},{7,0},{8,9},{9,10},{10,1... | collective-permute-start | bytes 786440 | tf_op jit(solution)/shard_map/ppermute | solution.py:25
  114.6 25.9 %copy-start.21 = (bf16[4,32,1024]{2,1,0:T(8,128)(2,1)}, bf16[4,32,1024]{2,1,0:T(8,128)(2,1)S(1)}, u32[]{:S(2)}) copy-start(bf16[4,32,1024]{2,1,0:T(8,128)(2,1)S(1)} %collective-permute-done.4.refs_7_) | copy-start | bytes 786436
  114.6 10.9 %collective-permute-start.5 = (bf16[4,32,1024]{2,1,0:T(8,128)(2,1)S(1)}, bf16[4,32,1024]{2,1,0:T(8,128)(2,1)}, u32[]{:S(2)}, u32[]{:S(2)}) collective-permute-start(bf16[4,32,1024]{2,1,0:T(8,128)(2,1)S(1)} %collective-permute-done.4.refs_7_), channel_id=1, source_target_pairs={{0,7},{1,0},{2,1},{3,2},{4,3},{7,6},{8,15},{9,8},{10,9},{11,10},{1... | collective-permute-start | bytes 786440 | tf_op jit(solution)/shard_map/ppermute | solution.py:25
  118.3 22.2 %copy-start.22 = (bf16[4,32,1024]{2,1,0:T(8,128)(2,1)}, bf16[4,32,1024]{2,1,0:T(8,128)(2,1)S(1)}, u32[]{:S(2)}) copy-start(bf16[4,32,1024]{2,1,0:T(8,128)(2,1)S(1)} %collective-permute-done.1.refs_2_) | copy-start | bytes 786436
  118.3 10.2 %collective-permute-start.2 = (bf16[4,32,1024]{2,1,0:T(8,128)(2,1)S(1)}, bf16[4,32,1024]{2,1,0:T(8,128)(2,1)}, u32[]{:S(2)}, u32[]{:S(2)}) collective-permute-start(bf16[4,32,1024]{2,1,0:T(8,128)(2,1)S(1)} %collective-permute-done.1.refs_2_), channel_id=1, source_target_pairs={{2,3},{3,4},{4,5},{5,6},{6,7},{7,0},{10,11},{11,12},{12,13},{13,14... | collective-permute-start | bytes 786440 | tf_op jit(solution)/shard_map/ppermute | solution.py:25
  119.9 14.4 %copy-start.5 = (bf16[256,512]{1,0:T(8,128)(2,1)}, bf16[256,512]{1,0:T(8,128)(2,1)S(1)}, u32[]{:S(2)}) copy-start(bf16[256,512]{1,0:T(8,128)(2,1)S(1)} %collective-permute-done.19.refs_6_) | copy-start | bytes 786436
  119.9 14.3 %collective-permute-start.20 = (bf16[256,512]{1,0:T(8,128)(2,1)S(1)}, bf16[256,512]{1,0:T(8,128)(2,1)S(1)}, u32[]{:S(2)}, u32[]{:S(2)}) collective-permute-start(bf16[256,512]{1,0:T(8,128)(2,1)S(1)} %collective-permute-done.19.refs_6_), channel_id=1, source_target_pairs={{0,7},{1,0},{2,1},{3,2},{4,3},{5,4},{6,5},{7,6},{8,15},{9,8},{10,9... | collective-permute-start | bytes 786440 | tf_op jit(solution)/shard_map/ppermute | solution.py:25
  123.1 11.2 %copy-start.6 = (bf16[256,512]{1,0:T(8,128)(2,1)}, bf16[256,512]{1,0:T(8,128)(2,1)S(1)}, u32[]{:S(2)}) copy-start(bf16[256,512]{1,0:T(8,128)(2,1)S(1)} %collective-permute-done.16.refs_3_) | copy-start | bytes 786436
  123.1 11.1 %collective-permute-start.17 = (bf16[256,512]{1,0:T(8,128)(2,1)S(1)}, bf16[256,512]{1,0:T(8,128)(2,1)S(1)}, u32[]{:S(2)}, u32[]{:S(2)}) collective-permute-start(bf16[256,512]{1,0:T(8,128)(2,1)S(1)} %collective-permute-done.16.refs_3_), channel_id=1, source_target_pairs={{0,1},{1,2},{2,3},{3,4},{4,5},{5,6},{6,7},{7,0},{8,9},{9,10},{10,1... | collective-permute-start | bytes 786440 | tf_op jit(solution)/shard_map/ppermute | solution.py:25
  125.5 15.0 %collective-permute-start.6 = (bf16[4,32,1024]{2,1,0:T(8,128)(2,1)}, bf16[4,32,1024]{2,1,0:T(8,128)(2,1)}, u32[]{:S(2)}, u32[]{:S(2)}) collective-permute-start(bf16[4,32,1024]{2,1,0:T(8,128)(2,1)} %collective-permute-done.5.refs_6_), channel_id=1, source_target_pairs={{0,7},{1,0},{2,1},{3,2},{6,5},{7,6},{8,15},{9,8},{10,9},{11,10},{1... | collective-permute-start | bytes 786440 | tf_op jit(solution)/shard_map/ppermute | solution.py:25
  128.5 12.0 %collective-permute-start.3 = (bf16[4,32,1024]{2,1,0:T(8,128)(2,1)}, bf16[4,32,1024]{2,1,0:T(8,128)(2,1)}, u32[]{:S(2)}, u32[]{:S(2)}) collective-permute-start(bf16[4,32,1024]{2,1,0:T(8,128)(2,1)} %collective-permute-done.2.refs_3_), channel_id=1, source_target_pairs={{0,1},{3,4},{4,5},{5,6},{6,7},{7,0},{8,9},{11,12},{12,13},{13,14},... | collective-permute-start | bytes 786440 | tf_op jit(solution)/shard_map/ppermute | solution.py:25
  134.1 0.7 copy-start.7
  134.1 0.8 copy-start.8
  140.6 29.4 %copy-start = (bf16[4,32,4096]{2,1,0:T(8,128)(2,1)S(1)}, bf16[4,32,4096]{2,1,0:T(8,128)(2,1)}, u32[]{:S(2)}) copy-start(bf16[4,32,4096]{2,1,0:T(8,128)(2,1)} %text_ref.1) | copy-start | bytes 3145732
  162.4 24.3 %all-to-all-start.2 = ((bf16[8,128,256]{2,1,0:T(8,128)(2,1)}), bf16[8,128,256]{2,1,0:T(8,128)(2,1)S(1)}, u32[]{:S(2)}, u32[]{:S(2)}) async-start(bf16[8,128,256]{2,1,0:T(8,128)(2,1)} %bitcast.22), calls=%async_computation.2 | async-start | bytes 1048576 | tf_op jit(solution)/shard_map/all_to_all | solution.py:513
  186.7 0.8 copy-start.1
Sparse Core Ops, SparseCore 0:
  9.9 55.2 all-gather.4
  67.7 78.2 all-gather.6

commit v5 on v4

--- a/solution.py
+++ b/solution.py
@@ -375,8 +375,9 @@
         ) * (1.0 / math.sqrt(HS))
         scores = jnp.where(allowed, scores, -1e30)
         row_max = jnp.max(scores, axis=1, keepdims=True)
-        weights = jnp.where(allowed, jnp.exp(scores - row_max), 0.0)
-        probabilities = (weights / jnp.sum(weights, axis=1, keepdims=True)).astype(jnp.bfloat16)
+        weights = jnp.exp(scores - row_max)
+        share = 1.0 / jnp.sum(weights, axis=1, keepdims=True)
+        probabilities = (weights * share).astype(jnp.bfloat16)
         attended = jnp.dot(probabilities, values, preferred_element_type=jnp.float32)
         out_ref[:, :, :, g * HS : (g + 1) * HS] = attended.astype(jnp.bfloat16).reshape(
             parts, 1, local_rows, HS

time: 204 us -> 204 us (level)
  no operation moved by 1% of the time
where the time goes in v5:
time: 204 us; the launch traced here: 203 us
  starting transfers between devices  64.4 us (32%)
  waiting for transfers between devices  48.4 us (24%)
  Pallas kernels  43.3 us (21%)
  blocking collectives  17.2 us (8%)
  between operations  13.8 us (7%)
  other arithmetic  8.57 us (4%)
  local copies, waits for them, and re-layouts  7.32 us (4%)
    ppermute x21, starting transfers between devices, shifted(): return lax.ppermute(value, axis, pairs)  53.2 us
    ppermute x21, waiting for transfers between devices, shifted(): return lax.ppermute(value, axis, pairs)  25.3 us
    all_to_all x1, blocking collectives, exchange_tiles(): got = lax.all_to_all(sent, 'dp', split_axis=0, concat_axis=0, tiled=True)  17.2 us
    pallas_call x1, Pallas kernels, image_qkv_of(): pl.pallas_call(functools.partial(image_kernel, groups=groups, useful=usef...  16 us
    all_to_all x1, waiting for transfers between devices, body(): lax.all_to_all(attended.reshape(parts, each, -1), 'mp', split_axis=0, con...  14.3 us
    pallas_call x1, Pallas kernels, project_out(): pl.pallas_call(out_kernel, in_specs=[whole, pl.BlockSpec(memory_space=pl....  8.73 us
    all_to_all x1, waiting for transfers between devices, exchange_tiles(): lax.all_to_all(ordered.reshape(ranks, image_count, width), 'dp', split_ax...  8.09 us
    all_to_all x1, starting transfers between devices, body(): lax.all_to_all(attended.reshape(parts, each, -1), 'mp', split_axis=0, con...  7.51 us
  transfers between devices with their start and end apart: 25, of which 10 were waited for; matrix products, arithmetic and copies ran while one was open for 7% of the time, Pallas kernels for 17%

profile of v5, /device:TPU:1, one launch (start us, length us, event | category | flops | bytes accessed | tf_op | source)
XLA Modules:
  0.0 203.1 jit_solution(16836165357096582724)
XLA Ops:
  6.5 0.7 all-gather.5.cloned.1.call-update
  7.3 2.4 %shard_map.102 = (bf16[128,768]{1,0:T(8,128)(2,1)}, bf16[128,768]{1,0:T(8,128)(2,1)}, bf16[128,768]{1,0:T(8,128)(2,1)}, bf16[128,768]{1,0:T(8,128)(2,1)}, bf16[1...) custom-call(s32[1]{0:T(128)} %bitcast.13.place_ref, ...), custom_call_target="tpu_custom_call" | custom-call | flops 1048576 | bytes 3145728 | tf_op jit(solution)/shard_map/pallas_call | solution.py:127
  9.7 7.7 %collective-permute-start.10 = (bf16[128,768]{1,0:T(8,128)(2,1)}, bf16[128,768]{1,0:T(8,128)(2,1)S(1)}, u32[]{:S(2)}, u32[]{:S(2)}) collective-permute-start(bf16[128,768]{1,0:T(8,128)(2,1)} %get-tuple-element.22), channel_id=1, source_target_pairs={{0,4},{1,5},{2,6},{3,7},{4,0},{5,1},{6,2},{7,3},{8,12},{9,13},{10,... | collective-permute-start | bytes 589832 | tf_op jit(solution)/shard_map/ppermute | solution.py:25
  17.5 4.0 %collective-permute-start.12 = (bf16[128,768]{1,0:T(8,128)(2,1)}, bf16[128,768]{1,0:T(8,128)(2,1)S(1)}, u32[]{:S(2)}, u32[]{:S(2)}) collective-permute-start(bf16[128,768]{1,0:T(8,128)(2,1)} %get-tuple-element.24), channel_id=1, source_target_pairs={{0,6},{1,7},{2,0},{3,1},{4,2},{5,3},{6,4},{7,5},{8,14},{9,15},{10,... | collective-permute-start | bytes 589832 | tf_op jit(solution)/shard_map/ppermute | solution.py:25
  21.5 0.7 collective-permute-start.13
  22.2 0.7 collective-permute-start.7
  23.0 0.1 pad.12.clone
  23.1 5.0 %collective-permute-start.8 = (bf16[128,768]{1,0:T(8,128)(2,1)}, bf16[128,768]{1,0:T(8,128)(2,1)S(1)}, u32[]{:S(2)}, u32[]{:S(2)}) collective-permute-start(bf16[128,768]{1,0:T(8,128)(2,1)} %get-tuple-element.20), channel_id=1, source_target_pairs={{0,2},{1,3},{2,4},{3,5},{4,6},{5,7},{6,0},{7,1},{8,10},{9,11},{10,... | collective-permute-start | bytes 589832 | tf_op jit(solution)/shard_map/ppermute | solution.py:25
  28.1 12.2 %collective-permute-done.11.refs_5_ = bf16[128,768]{1,0:T(8,128)(2,1)S(1)} collective-permute-done((bf16[128,768]{1,0:T(8,128)(2,1)}, bf16[128,768]{1,0:T(8,128)(2,1)S(1)}, u32[]{:S(2)}, u32[]{:S(2)}) %collective-permute-start.11) | collective-permute-done | bytes 196640 | tf_op jit(solution)/shard_map/ppermute | solution.py:25
  40.3 5.3 %collective-permute-start.9 = (bf16[128,768]{1,0:T(8,128)(2,1)}, bf16[128,768]{1,0:T(8,128)(2,1)S(1)}, u32[]{:S(2)}, u32[]{:S(2)}) collective-permute-start(bf16[128,768]{1,0:T(8,128)(2,1)} %get-tuple-element.21), channel_id=1, source_target_pairs={{0,3},{1,4},{2,5},{3,6},{4,7},{5,0},{6,1},{7,2},{8,11},{9,12},{10,... | collective-permute-start | bytes 589832 | tf_op jit(solution)/shard_map/ppermute | solution.py:25
  45.6 1.3 add_add_fusion.counts_ref
  46.9 1.7 collective-permute-done.12.refs_6_
  48.7 3.8 %collective-permute-done.13.refs_7_ = bf16[128,768]{1,0:T(8,128)(2,1)S(1)} collective-permute-done((bf16[128,768]{1,0:T(8,128)(2,1)}, bf16[128,768]{1,0:T(8,128)(2,1)S(1)}, u32[]{:S(2)}, u32[]{:S(2)}) %collective-permute-start.13) | collective-permute-done | bytes 196640 | tf_op jit(solution)/shard_map/ppermute | solution.py:25
  52.5 2.8 %collective-permute-done.9.refs_3_ = bf16[128,768]{1,0:T(8,128)(2,1)S(1)} collective-permute-done((bf16[128,768]{1,0:T(8,128)(2,1)}, bf16[128,768]{1,0:T(8,128)(2,1)S(1)}, u32[]{:S(2)}, u32[]{:S(2)}) %collective-permute-start.9) | collective-permute-done | bytes 196640 | tf_op jit(solution)/shard_map/ppermute | solution.py:25
  55.3 0.6 copy-done.16
  55.9 2.6 %shard_map.103 = (bf16[256,512]{1,0:T(8,128)(2,1)}, bf16[2048,128]{1,0:T(8,128)(2,1)}) custom-call(s32[3,4]{1,0:T(4,128)} %add_add_fusion.counts_ref, bf16[128,768]{1,0:T(8,128)(2,1)} %get-tuple-element.18.refs_0_, bf16[128,768]{1,0:T(8,128)(2,1)} %copy-done.14, bf16[128,768]{1,0:T(8,128)(2,1)} %copy-done.15, bf16[128,768]{1,0:T(8,128)(2,1)} %copy-done.16, ...), custom_call_target="tpu_custom_call" | custom-call | flops 67108864 | bytes 1572864 | tf_op jit(solution)/shard_map/pallas_call | solution.py:171
  58.5 1.2 copy.19
  59.7 0.7 convert_element_type.26
  60.4 0.1 broadcast_in_dim.16
  60.5 0.1 pad_maximum_fusion
  60.6 17.2 %all_to_all.15 = bf16[32,4,1152]{2,1,0:T(4,128)(2,1)S(1)} all-to-all(bf16[32,4,1152]{2,1,0:T(4,128)(2,1)S(1)} %pad_maximum_fusion), channel_id=1, replica_groups=mesh['dp'=32,'mp'=8] {'dp'}, dimensions={0} | all-to-all | bytes 589824 | tf_op jit(solution)/shard_map/all_to_all | solution.py:86
  77.8 0.8 reshape.157.got_ref
  78.6 2.1 %shard_map.100 = bf16[128,1024]{1,0:T(8,128)(2,1)} custom-call(bf16[128,1152]{1,0:T(8,128)(2,1)} %reshape.157.got_ref), custom_call_target="tpu_custom_call" | custom-call | flops 33554432 | bytes 524288 | tf_op jit(solution)/shard_map/pallas_call | solution.py:88
  80.7 1.8 reshape.158
  82.4 3.7 %all-to-all-start.1 = ((bf16[32,4,1024]{2,1,0:T(4,128)(2,1)}), bf16[32,4,1024]{2,1,0:T(4,128)(2,1)S(1)}, u32[]{:S(2)}, u32[]{:S(2)}) async-start(bf16[32,4,1024]{2,1,0:T(4,128)(2,1)} %reshape.158), calls=%async_computation.1 | async-start | bytes 524288 | tf_op jit(solution)/shard_map/all_to_all | solution.py:95
  86.1 2.4 %collective-permute-start.14 = (bf16[256,512]{1,0:T(8,128)(2,1)}, bf16[256,512]{1,0:T(8,128)(2,1)S(1)}, u32[]{:S(2)}, u32[]{:S(2)}) collective-permute-start(bf16[256,512]{1,0:T(8,128)(2,1)} %get-tuple-element.26.refs_0_), channel_id=1, source_target_pairs={{0,1},{1,2},{2,3},{3,4},{4,5},{5,6},{6,7},{7,0},{8,9},{9,10},{10,1... | collective-permute-start | bytes 786440 | tf_op jit(solution)/shard_map/ppermute | solution.py:25
  88.5 0.7 add_convert_fusion.1
  89.2 8.1 %all-to-all-done.1 = bf16[32,4,1024]{2,1,0:T(4,128)(2,1)S(1)} async-done(((bf16[32,4,1024]{2,1,0:T(4,128)(2,1)}), bf16[32,4,1024]{2,1,0:T(4,128)(2,1)S(1)}, u32[]{:S(2)}, u32[]{:S(2)}) %all-to-all-start.1) | async-done | bytes 262176 | tf_op jit(solution)/shard_map/all_to_all | solution.py:95
  97.3 0.1 copy.18
  97.4 3.3 %collective-permute-start = (bf16[4,32,1024]{2,1,0:T(8,128)(2,1)S(1)}, bf16[4,32,1024]{2,1,0:T(8,128)(2,1)S(1)}, u32[]{:S(2)}, u32[]{:S(2)}) collective-permute-start(bf16[4,32,1024]{2,1,0:T(8,128)(2,1)S(1)} %bitcast.25), channel_id=1, source_target_pairs={{0,1},{1,2},{2,3},{3,4},{4,5},{5,6},{8,9},{9,10},{10,11},{11,12},{... | collective-permute-start | bytes 786440 | tf_op jit(solution)/shard_map/ppermute | solution.py:25
  100.7 0.1 convert_element_type.29
  100.8 0.5 collective-permute-start.18
  101.3 1.0 collective-permute-start.15
  102.3 0.5 fusion
  102.8 3.6 %collective-permute-start.4 = (bf16[4,32,1024]{2,1,0:T(8,128)(2,1)S(1)}, bf16[4,32,1024]{2,1,0:T(8,128)(2,1)S(1)}, u32[]{:S(2)}, u32[]{:S(2)}) collective-permute-start(bf16[4,32,1024]{2,1,0:T(8,128)(2,1)S(1)} %bitcast.26), channel_id=1, source_target_pairs={{0,7},{1,0},{2,1},{3,2},{4,3},{5,4},{8,15},{9,8},{10,9},{11,10},{1... | collective-permute-start | bytes 786440 | tf_op jit(solution)/shard_map/ppermute | solution.py:25
  106.5 0.7 collective-permute-start.1
  107.2 1.4 collective-permute-done.18.refs_7_
  108.5 2.2 %collective-permute-start.19 = (bf16[256,512]{1,0:T(8,128)(2,1)S(1)}, bf16[256,512]{1,0:T(8,128)(2,1)S(1)}, u32[]{:S(2)}, u32[]{:S(2)}) collective-permute-start(bf16[256,512]{1,0:T(8,128)(2,1)S(1)} %collective-permute-done.18.refs_7_), channel_id=1, source_target_pairs={{0,7},{1,0},{2,1},{3,2},{4,3},{5,4},{6,5},{7,6},{8,15},{9,8},{10,9... | collective-permute-start | bytes 786440 | tf_op jit(solution)/shard_map/ppermute | solution.py:25
  110.7 1.2 collective-permute-done.15.refs_2_
  111.9 2.3 %collective-permute-start.16 = (bf16[256,512]{1,0:T(8,128)(2,1)S(1)}, bf16[256,512]{1,0:T(8,128)(2,1)S(1)}, u32[]{:S(2)}, u32[]{:S(2)}) collective-permute-start(bf16[256,512]{1,0:T(8,128)(2,1)S(1)} %collective-permute-done.15.refs_2_), channel_id=1, source_target_pairs={{0,1},{1,2},{2,3},{3,4},{4,5},{5,6},{6,7},{7,0},{8,9},{9,10},{10,1... | collective-permute-start | bytes 786440 | tf_op jit(solution)/shard_map/ppermute | solution.py:25
  114.2 0.4 fusion.1
  114.6 3.7 %collective-permute-start.5 = (bf16[4,32,1024]{2,1,0:T(8,128)(2,1)S(1)}, bf16[4,32,1024]{2,1,0:T(8,128)(2,1)}, u32[]{:S(2)}, u32[]{:S(2)}) collective-permute-start(bf16[4,32,1024]{2,1,0:T(8,128)(2,1)S(1)} %collective-permute-done.4.refs_7_), channel_id=1, source_target_pairs={{0,7},{1,0},{2,1},{3,2},{4,3},{7,6},{8,15},{9,8},{10,9},{11,10},{1... | collective-permute-start | bytes 786440 | tf_op jit(solution)/shard_map/ppermute | solution.py:25
  118.3 1.3 collective-permute-start.2
  119.7 0.2 collective-permute-done.19.refs_6_
  119.9 3.2 %collective-permute-start.20 = (bf16[256,512]{1,0:T(8,128)(2,1)S(1)}, bf16[256,512]{1,0:T(8,128)(2,1)S(1)}, u32[]{:S(2)}, u32[]{:S(2)}) collective-permute-start(bf16[256,512]{1,0:T(8,128)(2,1)S(1)} %collective-permute-done.19.refs_6_), channel_id=1, source_target_pairs={{0,7},{1,0},{2,1},{3,2},{4,3},{5,4},{6,5},{7,6},{8,15},{9,8},{10,9... | collective-permute-start | bytes 786440 | tf_op jit(solution)/shard_map/ppermute | solution.py:25
  123.1 0.3 collective-permute-start.17
  123.5 2.0 collective-permute-done.5.refs_6_
  125.5 3.0 %collective-permute-start.6 = (bf16[4,32,1024]{2,1,0:T(8,128)(2,1)}, bf16[4,32,1024]{2,1,0:T(8,128)(2,1)}, u32[]{:S(2)}, u32[]{:S(2)}) collective-permute-start(bf16[4,32,1024]{2,1,0:T(8,128)(2,1)} %collective-permute-done.5.refs_6_), channel_id=1, source_target_pairs={{0,7},{1,0},{2,1},{3,2},{6,5},{7,6},{8,15},{9,8},{10,9},{11,10},{1... | collective-permute-start | bytes 786440 | tf_op jit(solution)/shard_map/ppermute | solution.py:25
  128.5 2.2 %collective-permute-start.3 = (bf16[4,32,1024]{2,1,0:T(8,128)(2,1)}, bf16[4,32,1024]{2,1,0:T(8,128)(2,1)}, u32[]{:S(2)}, u32[]{:S(2)}) collective-permute-start(bf16[4,32,1024]{2,1,0:T(8,128)(2,1)} %collective-permute-done.2.refs_3_), channel_id=1, source_target_pairs={{0,1},{3,4},{4,5},{5,6},{6,7},{7,0},{8,9},{11,12},{12,13},{13,14},... | collective-permute-start | bytes 786440 | tf_op jit(solution)/shard_map/ppermute | solution.py:25
  130.8 0.8 pad_maximum_fusion.3
  131.6 0.5 broadcast.91
  132.1 0.6 reduce.3
  132.7 0.6 reshape.163.refs_10_
  133.3 0.8 pad_maximum_fusion.1
  134.2 0.6 copy-done.7
  134.8 0.1 copy-done.8
  134.9 5.6 %shard_map.104.text_ref = bf16[256,512]{1,0:T(8,128)(2,1)} custom-call(s32[1]{0:T(128)} %bitcast.13.place_ref, bf16[256,512]{1,0:T(8,128)(2,1)} %get-tuple-element.26.refs_0_, bf16[256,512]{1,0:T(8,128)(2,1)} %copy-done.2, bf16[256,512]{1,0:T(8,128)(2,1)} %copy-done.4, bf16[256,512]{1,0:T(8,128)(2,1)} %copy-done.6, bf16[256,512]{1,0:T(8,128)(2,1)} %copy-done.8, ...), custom_call_target="tpu_custom_call" | custom-call | flops 1073741824 | bytes 6291456 | tf_op jit(solution)/shard_map/pallas_call | solution.py:228
  140.6 16.0 %shard_map.101 = (bf16[6,4,32,512]{3,2,1,0:T(8,128)(2,1)}, bf16[128,4096]{1,0:T(8,128)(2,1)}) custom-call(s32[1]{0:T(128)} %bitcast.13.place_ref, bf16[4,32,1024]{2,1,0:T(8,128)(2,1)} %bitcast.27, bf16[4,32,1024]{2,1,0:T(8,128)(2,1)} %copy-done.20, bf16[4,32,1024]{2,1,0:T(8,128)(2,1)} %copy-done.22, bf16[4,32,1024]{2,1,0:T(8,128)(2,1)} %collective-permute-done.2.refs_3_, ...), custom_call_target="tpu_custom_call" | custom-call | flops 9663676416 | bytes 12582912 | tf_op jit(solution)/shard_map/pallas_call | solution.py:309
  156.6 5.8 %shard_map.105 = bf16[8,4,32,256]{3,2,1,0:T(8,128)(2,1)} custom-call(s32[3,4]{1,0:T(4,128)} %add_add_fusion.counts_ref, bf16[6,4,32,512]{3,2,1,0:T(8,128)(2,1)} %get-tuple-element.17.image_ref, bf16[256,512]{1,0:T(8,128)(2,1)} %shard_map.104.text_ref), custom_call_target="tpu_custom_call" | custom-call | flops 335544320 | bytes 2097152 | tf_op jit(solution)/shard_map/pallas_call | solution.py:390
  162.4 7.5 %all-to-all-start.2 = ((bf16[8,128,256]{2,1,0:T(8,128)(2,1)}), bf16[8,128,256]{2,1,0:T(8,128)(2,1)S(1)}, u32[]{:S(2)}, u32[]{:S(2)}) async-start(bf16[8,128,256]{2,1,0:T(8,128)(2,1)} %bitcast.22), calls=%async_computation.2 | async-start | bytes 1048576 | tf_op jit(solution)/shard_map/all_to_all | solution.py:514
  170.0 2.4 %select_select_fusion = bf16[4,32,4096]{2,1,0:T(8,128)(2,1)} fusion(bf16[4,32,4096]{2,1,0:T(8,128)(2,1)} %bitcast.23, bf16[4,32,4096]{2,1,0:T(8,128)(2,1)S(1)} %copy-done, pred[4,32]{1,0:T(4,128)(4,1)S(1)} %get-tuple-element.36, pred[4,32]{1,0:T(4,128)(4,1)S(1)} %get-tuple-element.35), kind=kLoop, calls=%fused_computation | loop fusion | flops 1048576 | bytes 3145984 | tf_op jit(solution)/shard_map/jit(_where)/select_n | solution.py:505
  172.4 14.3 %all-to-all-done.2.att_ref = bf16[8,128,256]{2,1,0:T(8,128)(2,1)S(1)} async-done(((bf16[8,128,256]{2,1,0:T(8,128)(2,1)}), bf16[8,128,256]{2,1,0:T(8,128)(2,1)S(1)}, u32[]{:S(2)}, u32[]{:S(2)}) %all-to-all-start.2) | async-done | bytes 524320 | tf_op jit(solution)/shard_map/all_to_all | solution.py:514
  186.7 0.8 copy-done.1
  187.5 8.7 %shard_map.106 = bf16[128,4096]{1,0:T(8,128)(2,1)} custom-call(bf16[8,128,256]{2,1,0:T(8,128)(2,1)} %copy-done.1, bf16[32,2048,128]{2,1,0:T(8,128)(2,1)} %bitcast.18, bf16[128,4096]{1,0:T(8,128)(2,1)} %bitcast.19), custom_call_target="tpu_custom_call" | custom-call | flops 2147483648 | bytes 16777216 | tf_op jit(solution)/shard_map/pallas_call | solution.py:440
  (66 shorter events, 0.3 us)
Async XLA Ops:
  6.5 113.1 %copy-start.18 = (s32[4]{0:T(128)S(1)}, s32[4]{0:T(128)}, u32[]{:S(2)}) copy-start(s32[4]{0:T(128)} %param.11) | copy-start | bytes 52
  6.5 113.1 %copy-start.19 = (s32[4]{0:T(128)S(1)}, s32[4]{0:T(128)}, u32[]{:S(2)}) copy-start(s32[4]{0:T(128)} %param.12) | copy-start | bytes 52
  6.5 125.5 %copy-start.17 = (f32[1,4096]{1,0:T(1,128)S(1)}, f32[1,4096]{1,0:T(1,128)}, u32[]{:S(2)}) copy-start(f32[1,4096]{1,0:T(1,128)} %refs_12_.1) | copy-start | bytes 49156
  6.5 127.6 %all-gather.5.cloned.1.call-start = ((), (), s32[]{:S(2)}) async-start(), calls=%async_computation.3 | async-start | bytes 4325376 | tf_op jit(solution)/shard_map/all_gather | solution.py:479
  7.3 179.4 %all-gather.7.cloned.1.call-start = ((), (), s32[]{:S(2)}) async-start(), calls=%async_computation.4 | async-start | bytes 17301504 | tf_op jit(solution)/shard_map/all_gather | solution.py:484
  9.7 13.3 %collective-permute-start.10 = (bf16[128,768]{1,0:T(8,128)(2,1)}, bf16[128,768]{1,0:T(8,128)(2,1)S(1)}, u32[]{:S(2)}, u32[]{:S(2)}) collective-permute-start(bf16[128,768]{1,0:T(8,128)(2,1)} %get-tuple-element.22), channel_id=1, source_target_pairs={{0,4},{1,5},{2,6},{3,7},{4,0},{5,1},{6,2},{7,3},{8,12},{9,13},{10,... | collective-permute-start | bytes 589832 | tf_op jit(solution)/shard_map/ppermute | solution.py:25
  17.5 22.9 %collective-permute-start.11 = (bf16[128,768]{1,0:T(8,128)(2,1)}, bf16[128,768]{1,0:T(8,128)(2,1)S(1)}, u32[]{:S(2)}, u32[]{:S(2)}) collective-permute-start(bf16[128,768]{1,0:T(8,128)(2,1)} %get-tuple-element.23), channel_id=1, source_target_pairs={{0,5},{1,6},{2,7},{3,0},{4,1},{5,2},{6,3},{7,4},{8,13},{9,14},{10,... | collective-permute-start | bytes 589832 | tf_op jit(solution)/shard_map/ppermute | solution.py:25
  17.5 31.2 %collective-permute-start.12 = (bf16[128,768]{1,0:T(8,128)(2,1)}, bf16[128,768]{1,0:T(8,128)(2,1)S(1)}, u32[]{:S(2)}, u32[]{:S(2)}) collective-permute-start(bf16[128,768]{1,0:T(8,128)(2,1)} %get-tuple-element.24), channel_id=1, source_target_pairs={{0,6},{1,7},{2,0},{3,1},{4,2},{5,3},{6,4},{7,5},{8,14},{9,15},{10,... | collective-permute-start | bytes 589832 | tf_op jit(solution)/shard_map/ppermute | solution.py:25
  21.5 30.9 %collective-permute-start.13 = (bf16[128,768]{1,0:T(8,128)(2,1)}, bf16[128,768]{1,0:T(8,128)(2,1)S(1)}, u32[]{:S(2)}, u32[]{:S(2)}) collective-permute-start(bf16[128,768]{1,0:T(8,128)(2,1)} %get-tuple-element.25), channel_id=1, source_target_pairs={{0,7},{1,0},{2,1},{3,2},{4,3},{5,4},{6,5},{7,6},{8,15},{9,8},{10,9... | collective-permute-start | bytes 589832 | tf_op jit(solution)/shard_map/ppermute | solution.py:25
  22.2 30.2 %collective-permute-start.7 = (bf16[128,768]{1,0:T(8,128)(2,1)}, bf16[128,768]{1,0:T(8,128)(2,1)S(1)}, u32[]{:S(2)}, u32[]{:S(2)}) collective-permute-start(bf16[128,768]{1,0:T(8,128)(2,1)} %get-tuple-element.19), channel_id=1, source_target_pairs={{0,1},{1,2},{2,3},{3,4},{4,5},{5,6},{6,7},{7,0},{8,9},{9,10},{10,1... | collective-permute-start | bytes 589832 | tf_op jit(solution)/shard_map/ppermute | solution.py:25
  23.1 32.2 %copy-start.10 = (bf16[128,768]{1,0:T(8,128)(2,1)}, bf16[128,768]{1,0:T(8,128)(2,1)S(1)}, u32[]{:S(2)}) copy-start(bf16[128,768]{1,0:T(8,128)(2,1)S(1)} %collective-permute-done.10.refs_4_) | copy-start | bytes 589828
  23.1 29.4 %collective-permute-start.8 = (bf16[128,768]{1,0:T(8,128)(2,1)}, bf16[128,768]{1,0:T(8,128)(2,1)S(1)}, u32[]{:S(2)}, u32[]{:S(2)}) collective-permute-start(bf16[128,768]{1,0:T(8,128)(2,1)} %get-tuple-element.20), channel_id=1, source_target_pairs={{0,2},{1,3},{2,4},{3,5},{4,6},{5,7},{6,0},{7,1},{8,10},{9,11},{10,... | collective-permute-start | bytes 589832 | tf_op jit(solution)/shard_map/ppermute | solution.py:25
  40.3 14.9 %copy-start.11 = (bf16[128,768]{1,0:T(8,128)(2,1)}, bf16[128,768]{1,0:T(8,128)(2,1)S(1)}, u32[]{:S(2)}) copy-start(bf16[128,768]{1,0:T(8,128)(2,1)S(1)} %collective-permute-done.11.refs_5_) | copy-start | bytes 589828
  40.3 14.9 %collective-permute-start.9 = (bf16[128,768]{1,0:T(8,128)(2,1)}, bf16[128,768]{1,0:T(8,128)(2,1)S(1)}, u32[]{:S(2)}, u32[]{:S(2)}) collective-permute-start(bf16[128,768]{1,0:T(8,128)(2,1)} %get-tuple-element.21), channel_id=1, source_target_pairs={{0,3},{1,4},{2,5},{3,6},{4,7},{5,0},{6,1},{7,2},{8,11},{9,12},{10,... | collective-permute-start | bytes 589832 | tf_op jit(solution)/shard_map/ppermute | solution.py:25
  48.7 6.6 %copy-start.12 = (bf16[128,768]{1,0:T(8,128)(2,1)}, bf16[128,768]{1,0:T(8,128)(2,1)S(1)}, u32[]{:S(2)}) copy-start(bf16[128,768]{1,0:T(8,128)(2,1)S(1)} %collective-permute-done.12.refs_6_) | copy-start | bytes 589828
  52.5 2.8 %copy-start.13 = (bf16[128,768]{1,0:T(8,128)(2,1)}, bf16[128,768]{1,0:T(8,128)(2,1)S(1)}, u32[]{:S(2)}) copy-start(bf16[128,768]{1,0:T(8,128)(2,1)S(1)} %collective-permute-done.13.refs_7_) | copy-start | bytes 589828
  52.5 2.8 %copy-start.14 = (bf16[128,768]{1,0:T(8,128)(2,1)}, bf16[128,768]{1,0:T(8,128)(2,1)S(1)}, u32[]{:S(2)}) copy-start(bf16[128,768]{1,0:T(8,128)(2,1)S(1)} %collective-permute-done.7.refs_1_) | copy-start | bytes 589828
  52.5 2.8 %copy-start.15 = (bf16[128,768]{1,0:T(8,128)(2,1)}, bf16[128,768]{1,0:T(8,128)(2,1)S(1)}, u32[]{:S(2)}) copy-start(bf16[128,768]{1,0:T(8,128)(2,1)S(1)} %collective-permute-done.8.refs_2_) | copy-start | bytes 589828
  55.2 0.7 copy-start.16
  82.4 14.9 %all-to-all-start.1 = ((bf16[32,4,1024]{2,1,0:T(4,128)(2,1)}), bf16[32,4,1024]{2,1,0:T(4,128)(2,1)S(1)}, u32[]{:S(2)}, u32[]{:S(2)}) async-start(bf16[32,4,1024]{2,1,0:T(4,128)(2,1)} %reshape.158), calls=%async_computation.1 | async-start | bytes 524288 | tf_op jit(solution)/shard_map/all_to_all | solution.py:95
  86.1 15.2 %collective-permute-start.14 = (bf16[256,512]{1,0:T(8,128)(2,1)}, bf16[256,512]{1,0:T(8,128)(2,1)S(1)}, u32[]{:S(2)}, u32[]{:S(2)}) collective-permute-start(bf16[256,512]{1,0:T(8,128)(2,1)} %get-tuple-element.26.refs_0_), channel_id=1, source_target_pairs={{0,1},{1,2},{2,3},{3,4},{4,5},{5,6},{6,7},{7,0},{8,9},{9,10},{10,1... | collective-permute-start | bytes 786440 | tf_op jit(solution)/shard_map/ppermute | solution.py:25
  97.4 43.1 %copy-start.9 = (bf16[32,4,1024]{2,0,1:T(8,128)(2,1)}, bf16[32,4,1024]{2,0,1:T(8,128)(2,1)S(1)}, u32[]{:S(2)}) copy-start(bf16[32,4,1024]{2,0,1:T(8,128)(2,1)S(1)} %copy.18) | copy-start | bytes 786436
  97.4 9.0 %collective-permute-start = (bf16[4,32,1024]{2,1,0:T(8,128)(2,1)S(1)}, bf16[4,32,1024]{2,1,0:T(8,128)(2,1)S(1)}, u32[]{:S(2)}, u32[]{:S(2)}) collective-permute-start(bf16[4,32,1024]{2,1,0:T(8,128)(2,1)S(1)} %bitcast.25), channel_id=1, source_target_pairs={{0,1},{1,2},{2,3},{3,4},{4,5},{5,6},{8,9},{9,10},{10,11},{11,12},{... | collective-permute-start | bytes 786440 | tf_op jit(solution)/shard_map/ppermute | solution.py:25
  100.8 7.7 %collective-permute-start.18 = (bf16[256,512]{1,0:T(8,128)(2,1)}, bf16[256,512]{1,0:T(8,128)(2,1)S(1)}, u32[]{:S(2)}, u32[]{:S(2)}) collective-permute-start(bf16[256,512]{1,0:T(8,128)(2,1)} %get-tuple-element.26.refs_0_), channel_id=1, source_target_pairs={{0,7},{1,0},{2,1},{3,2},{4,3},{5,4},{6,5},{7,6},{8,15},{9,8},{10,9... | collective-permute-start | bytes 786440 | tf_op jit(solution)/shard_map/ppermute | solution.py:25
  101.3 32.9 %copy-start.2 = (bf16[256,512]{1,0:T(8,128)(2,1)}, bf16[256,512]{1,0:T(8,128)(2,1)S(1)}, u32[]{:S(2)}) copy-start(bf16[256,512]{1,0:T(8,128)(2,1)S(1)} %collective-permute-done.14.refs_1_) | copy-start | bytes 786436
  101.3 10.6 %collective-permute-start.15 = (bf16[256,512]{1,0:T(8,128)(2,1)S(1)}, bf16[256,512]{1,0:T(8,128)(2,1)S(1)}, u32[]{:S(2)}, u32[]{:S(2)}) collective-permute-start(bf16[256,512]{1,0:T(8,128)(2,1)S(1)} %collective-permute-done.14.refs_1_), channel_id=1, source_target_pairs={{0,1},{1,2},{2,3},{3,4},{4,5},{5,6},{6,7},{7,0},{8,9},{9,10},{10,1... | collective-permute-start | bytes 786440 | tf_op jit(solution)/shard_map/ppermute | solution.py:25
  102.8 11.8 %collective-permute-start.4 = (bf16[4,32,1024]{2,1,0:T(8,128)(2,1)S(1)}, bf16[4,32,1024]{2,1,0:T(8,128)(2,1)S(1)}, u32[]{:S(2)}, u32[]{:S(2)}) collective-permute-start(bf16[4,32,1024]{2,1,0:T(8,128)(2,1)S(1)} %bitcast.26), channel_id=1, source_target_pairs={{0,7},{1,0},{2,1},{3,2},{4,3},{5,4},{8,15},{9,8},{10,9},{11,10},{1... | collective-permute-start | bytes 786440 | tf_op jit(solution)/shard_map/ppermute | solution.py:25
  106.4 34.1 %copy-start.20 = (bf16[4,32,1024]{2,1,0:T(8,128)(2,1)}, bf16[4,32,1024]{2,1,0:T(8,128)(2,1)S(1)}, u32[]{:S(2)}) copy-start(bf16[4,32,1024]{2,1,0:T(8,128)(2,1)S(1)} %collective-permute-done.refs_1_) | copy-start | bytes 786436
  106.5 11.9 %collective-permute-start.1 = (bf16[4,32,1024]{2,1,0:T(8,128)(2,1)S(1)}, bf16[4,32,1024]{2,1,0:T(8,128)(2,1)S(1)}, u32[]{:S(2)}, u32[]{:S(2)}) collective-permute-start(bf16[4,32,1024]{2,1,0:T(8,128)(2,1)S(1)} %collective-permute-done.refs_1_), channel_id=1, source_target_pairs={{1,2},{2,3},{3,4},{4,5},{5,6},{6,7},{9,10},{10,11},{11,12},{12,13}... | collective-permute-start | bytes 786440 | tf_op jit(solution)/shard_map/ppermute | solution.py:25
  108.5 25.7 %copy-start.3 = (bf16[256,512]{1,0:T(8,128)(2,1)}, bf16[256,512]{1,0:T(8,128)(2,1)S(1)}, u32[]{:S(2)}) copy-start(bf16[256,512]{1,0:T(8,128)(2,1)S(1)} %collective-permute-done.18.refs_7_) | copy-start | bytes 786436
  108.5 11.3 %collective-permute-start.19 = (bf16[256,512]{1,0:T(8,128)(2,1)S(1)}, bf16[256,512]{1,0:T(8,128)(2,1)S(1)}, u32[]{:S(2)}, u32[]{:S(2)}) collective-permute-start(bf16[256,512]{1,0:T(8,128)(2,1)S(1)} %collective-permute-done.18.refs_7_), channel_id=1, source_target_pairs={{0,7},{1,0},{2,1},{3,2},{4,3},{5,4},{6,5},{7,6},{8,15},{9,8},{10,9... | collective-permute-start | bytes 786440 | tf_op jit(solution)/shard_map/ppermute | solution.py:25
  111.9 22.3 %copy-start.4 = (bf16[256,512]{1,0:T(8,128)(2,1)}, bf16[256,512]{1,0:T(8,128)(2,1)S(1)}, u32[]{:S(2)}) copy-start(bf16[256,512]{1,0:T(8,128)(2,1)S(1)} %collective-permute-done.15.refs_2_) | copy-start | bytes 786436
  111.9 11.2 %collective-permute-start.16 = (bf16[256,512]{1,0:T(8,128)(2,1)S(1)}, bf16[256,512]{1,0:T(8,128)(2,1)S(1)}, u32[]{:S(2)}, u32[]{:S(2)}) collective-permute-start(bf16[256,512]{1,0:T(8,128)(2,1)S(1)} %collective-permute-done.15.refs_2_), channel_id=1, source_target_pairs={{0,1},{1,2},{2,3},{3,4},{4,5},{5,6},{6,7},{7,0},{8,9},{9,10},{10,1... | collective-permute-start | bytes 786440 | tf_op jit(solution)/shard_map/ppermute | solution.py:25
  114.6 25.9 %copy-start.21 = (bf16[4,32,1024]{2,1,0:T(8,128)(2,1)}, bf16[4,32,1024]{2,1,0:T(8,128)(2,1)S(1)}, u32[]{:S(2)}) copy-start(bf16[4,32,1024]{2,1,0:T(8,128)(2,1)S(1)} %collective-permute-done.4.refs_7_) | copy-start | bytes 786436
  114.6 10.9 %collective-permute-start.5 = (bf16[4,32,1024]{2,1,0:T(8,128)(2,1)S(1)}, bf16[4,32,1024]{2,1,0:T(8,128)(2,1)}, u32[]{:S(2)}, u32[]{:S(2)}) collective-permute-start(bf16[4,32,1024]{2,1,0:T(8,128)(2,1)S(1)} %collective-permute-done.4.refs_7_), channel_id=1, source_target_pairs={{0,7},{1,0},{2,1},{3,2},{4,3},{7,6},{8,15},{9,8},{10,9},{11,10},{1... | collective-permute-start | bytes 786440 | tf_op jit(solution)/shard_map/ppermute | solution.py:25
  118.3 22.2 %copy-start.22 = (bf16[4,32,1024]{2,1,0:T(8,128)(2,1)}, bf16[4,32,1024]{2,1,0:T(8,128)(2,1)S(1)}, u32[]{:S(2)}) copy-start(bf16[4,32,1024]{2,1,0:T(8,128)(2,1)S(1)} %collective-permute-done.1.refs_2_) | copy-start | bytes 786436
  118.3 10.2 %collective-permute-start.2 = (bf16[4,32,1024]{2,1,0:T(8,128)(2,1)S(1)}, bf16[4,32,1024]{2,1,0:T(8,128)(2,1)}, u32[]{:S(2)}, u32[]{:S(2)}) collective-permute-start(bf16[4,32,1024]{2,1,0:T(8,128)(2,1)S(1)} %collective-permute-done.1.refs_2_), channel_id=1, source_target_pairs={{2,3},{3,4},{4,5},{5,6},{6,7},{7,0},{10,11},{11,12},{12,13},{13,14... | collective-permute-start | bytes 786440 | tf_op jit(solution)/shard_map/ppermute | solution.py:25
  119.9 14.4 %copy-start.5 = (bf16[256,512]{1,0:T(8,128)(2,1)}, bf16[256,512]{1,0:T(8,128)(2,1)S(1)}, u32[]{:S(2)}) copy-start(bf16[256,512]{1,0:T(8,128)(2,1)S(1)} %collective-permute-done.19.refs_6_) | copy-start | bytes 786436
  119.9 14.3 %collective-permute-start.20 = (bf16[256,512]{1,0:T(8,128)(2,1)S(1)}, bf16[256,512]{1,0:T(8,128)(2,1)S(1)}, u32[]{:S(2)}, u32[]{:S(2)}) collective-permute-start(bf16[256,512]{1,0:T(8,128)(2,1)S(1)} %collective-permute-done.19.refs_6_), channel_id=1, source_target_pairs={{0,7},{1,0},{2,1},{3,2},{4,3},{5,4},{6,5},{7,6},{8,15},{9,8},{10,9... | collective-permute-start | bytes 786440 | tf_op jit(solution)/shard_map/ppermute | solution.py:25
  123.1 11.2 %copy-start.6 = (bf16[256,512]{1,0:T(8,128)(2,1)}, bf16[256,512]{1,0:T(8,128)(2,1)S(1)}, u32[]{:S(2)}) copy-start(bf16[256,512]{1,0:T(8,128)(2,1)S(1)} %collective-permute-done.16.refs_3_) | copy-start | bytes 786436
  123.1 11.1 %collective-permute-start.17 = (bf16[256,512]{1,0:T(8,128)(2,1)S(1)}, bf16[256,512]{1,0:T(8,128)(2,1)S(1)}, u32[]{:S(2)}, u32[]{:S(2)}) collective-permute-start(bf16[256,512]{1,0:T(8,128)(2,1)S(1)} %collective-permute-done.16.refs_3_), channel_id=1, source_target_pairs={{0,1},{1,2},{2,3},{3,4},{4,5},{5,6},{6,7},{7,0},{8,9},{9,10},{10,1... | collective-permute-start | bytes 786440 | tf_op jit(solution)/shard_map/ppermute | solution.py:25
  125.5 15.0 %collective-permute-start.6 = (bf16[4,32,1024]{2,1,0:T(8,128)(2,1)}, bf16[4,32,1024]{2,1,0:T(8,128)(2,1)}, u32[]{:S(2)}, u32[]{:S(2)}) collective-permute-start(bf16[4,32,1024]{2,1,0:T(8,128)(2,1)} %collective-permute-done.5.refs_6_), channel_id=1, source_target_pairs={{0,7},{1,0},{2,1},{3,2},{6,5},{7,6},{8,15},{9,8},{10,9},{11,10},{1... | collective-permute-start | bytes 786440 | tf_op jit(solution)/shard_map/ppermute | solution.py:25
  128.5 12.0 %collective-permute-start.3 = (bf16[4,32,1024]{2,1,0:T(8,128)(2,1)}, bf16[4,32,1024]{2,1,0:T(8,128)(2,1)}, u32[]{:S(2)}, u32[]{:S(2)}) collective-permute-start(bf16[4,32,1024]{2,1,0:T(8,128)(2,1)} %collective-permute-done.2.refs_3_), channel_id=1, source_target_pairs={{0,1},{3,4},{4,5},{5,6},{6,7},{7,0},{8,9},{11,12},{12,13},{13,14},... | collective-permute-start | bytes 786440 | tf_op jit(solution)/shard_map/ppermute | solution.py:25
  134.1 0.7 copy-start.7
  134.1 0.8 copy-start.8
  140.6 29.4 %copy-start = (bf16[4,32,4096]{2,1,0:T(8,128)(2,1)S(1)}, bf16[4,32,4096]{2,1,0:T(8,128)(2,1)}, u32[]{:S(2)}) copy-start(bf16[4,32,4096]{2,1,0:T(8,128)(2,1)} %text_ref.1) | copy-start | bytes 3145732
  162.4 24.3 %all-to-all-start.2 = ((bf16[8,128,256]{2,1,0:T(8,128)(2,1)}), bf16[8,128,256]{2,1,0:T(8,128)(2,1)S(1)}, u32[]{:S(2)}, u32[]{:S(2)}) async-start(bf16[8,128,256]{2,1,0:T(8,128)(2,1)} %bitcast.22), calls=%async_computation.2 | async-start | bytes 1048576 | tf_op jit(solution)/shard_map/all_to_all | solution.py:514
  186.7 0.8 copy-start.1
Sparse Core Ops, SparseCore 0:
  9.9 55.2 all-gather.4
  67.7 78.2 all-gather.6
